TPU v7x, 512 devices: a whole 4x4x16 slice. The times are simulated.
512 devices in a mesh: dp: 64 (over z, y), tensor: 8 (over x, core).
Axes of the slice: x: 4, y: 4, z: 16, core: 2. Of those that a mesh axis runs over, the one named last changes fastest.
Arguments:
- normed_input: bfloat16 [8192, 8192], P('dp', 'tensor'), may hold values from -6 to 6
- key_cotangent: bfloat16 [8192, 1024], P('dp', 'tensor'), may hold values from -6 to 6
- frozen_key_weight: bfloat16 [8192, 1024], P(None, 'tensor'), may hold values from -0.1875 to 0.1875
- adapter_down_maps: bfloat16 [32, 8192, 16], P(None, 'tensor'), may hold values from -0.0625 to 0.0625
- adapter_up_maps: bfloat16 [32, 16, 1024], P(None, None, 'tensor'), may hold values from -0.1875 to 0.1875
- document_of_token: int32 [8192], P('dp'), may hold values from 0 to 127, never falling along the last dimension, each value on 1 to 512 neighbouring positions
- tenant_of_document: int32 [128], replicated, may hold values from 0 to 31
- tenant_slot_index: int32 [32], replicated, may hold values from 0 to 31, each once
Outputs:
- input_gradient: bfloat16 [8192, 8192], P('dp', 'tensor')
- down_gradient: bfloat16 [32, 8192, 16], P(None, 'tensor')
- up_gradient: bfloat16 [32, 16, 1024], P(None, None, 'tensor')
Inputs may be any that keep to these rules, and one draw needn't show every extreme that they name: `document_of_token`: never falling along the tokens; each document 1 to (512) tokens. `tenant_slot_index`: each slot once.
All inputs are finite; a program needn't handle non-finite values.
Results may differ from a plain program's by a relative error of at most 0.008.
Values may be sent and summed in bfloat16 or wider, within the bound.
No kernel may reach another device: no remote copies, remote signals or barrier semaphores. Data moves between devices by JAX's collectives and lax.ppermute only.
A program may use at most 64 MiB of HBM per device.

v0:
```python
import jax
import jax.numpy as jnp
from jax import lax
from jax.sharding import PartitionSpec as P

adapter_scale = 2.0


def from_everyone(value, axis):
    length = lax.axis_size(axis)
    return lax.all_to_all(
        jnp.broadcast_to(value[None], (length, *value.shape)), axis, 0, 0, tiled=True
    )


def of_everyone(value, axis):
    everything = from_everyone(value, axis)
    return jnp.sum(everything, axis=0)


def packed_total(arrays, axis):
    ends = [0]
    for a in arrays:
        ends.append(ends[-1] + a.size)
    total = of_everyone(jnp.concatenate([a.ravel() for a in arrays]), axis)
    return tuple((total[b:e].reshape(a.shape) for a, b, e in zip(arrays, ends, ends[1:])))


def cut_along(value, dim, length):
    before, after = (value.shape[:dim], value.shape[dim + 1 :])
    return jnp.moveaxis(value.reshape(*before, length, -1, *after), dim, 0)


def sum_at_owner(value, axis, dim):
    length = lax.axis_size(axis)
    blocks = lax.all_to_all(cut_along(value, dim, length), axis, 0, 0, tiled=True)
    return jnp.sum(blocks, axis=0)


def per_device(
    normed_input,
    key_cotangent,
    frozen_key_weight,
    adapter_down_maps,
    adapter_up_maps,
    document_of_token,
    tenant_of_document,
    tenant_slot_index,
):
    tenant_count, token_rows, adapter_rank = adapter_down_maps.shape
    key_heads_width = adapter_up_maps.shape[2]
    slot = jnp.take(tenant_slot_index, jnp.take(tenant_of_document, document_of_token))
    member = (slot[:, None] == jnp.arange(tenant_count, dtype=jnp.int32)[None, :]).astype(
        jnp.float32
    )
    down_flattened = jnp.transpose(adapter_down_maps, (1, 0, 2)).reshape(
        token_rows, tenant_count * adapter_rank
    )
    up_flattened = jnp.transpose(adapter_up_maps, (2, 0, 1)).reshape(
        key_heads_width, tenant_count * adapter_rank
    )
    h_all = jnp.dot(normed_input, down_flattened, preferred_element_type=jnp.float32).reshape(
        -1, tenant_count, adapter_rank
    )
    g_all = jnp.dot(key_cotangent, up_flattened, preferred_element_type=jnp.float32).reshape(
        -1, tenant_count, adapter_rank
    )
    h_part = jnp.sum(h_all * member[:, :, None], axis=1)
    g_part = jnp.sum(g_all * member[:, :, None], axis=1)
    h_total, g_total = packed_total((h_part, g_part), "tensor")
    low_h = h_total.astype(jnp.bfloat16)
    low_g = g_total.astype(jnp.bfloat16)
    spread_hidden = (
        (member[:, :, None] * low_h.astype(jnp.float32)[:, None, :])
        .astype(jnp.bfloat16)
        .reshape(-1, tenant_count * adapter_rank)
    )
    spread_cotangent = (
        (member[:, :, None] * low_g.astype(jnp.float32)[:, None, :])
        .astype(jnp.bfloat16)
        .reshape(-1, tenant_count * adapter_rank)
    )
    down_gradient_piece = adapter_scale * jnp.dot(
        normed_input.T, spread_cotangent, preferred_element_type=jnp.float32
    )
    up_gradient_piece = adapter_scale * jnp.dot(
        spread_hidden.T, key_cotangent, preferred_element_type=jnp.float32
    )
    grad_a_sum, grad_b_sum = lax.psum((down_gradient_piece, up_gradient_piece), "dp")
    frozen_output = sum_at_owner(
        jnp.dot(frozen_key_weight, key_cotangent.T, preferred_element_type=jnp.float32), "tensor", 0
    ).T
    adapter_output = jnp.dot(spread_cotangent, down_flattened.T, preferred_element_type=jnp.float32)
    input_gradient = (frozen_output + adapter_scale * adapter_output).astype(jnp.bfloat16)
    down_gradient = jnp.transpose(
        grad_a_sum.reshape(token_rows, tenant_count, adapter_rank), (1, 0, 2)
    ).astype(jnp.bfloat16)
    up_gradient = grad_b_sum.reshape(tenant_count, adapter_rank, key_heads_width).astype(
        jnp.bfloat16
    )
    return (input_gradient, down_gradient, up_gradient)


def solution(mesh):
    in_specs = (
        P("dp", "tensor"),
        P("dp", "tensor"),
        P(None, "tensor"),
        P(None, "tensor", None),
        P(None, None, "tensor"),
        P("dp"),
        P(),
        P(),
    )
    out_specs = (P("dp", "tensor"), P(None, "tensor", None), P(None, None, "tensor"))
    return jax.shard_map(
        per_device, mesh=mesh, in_specs=in_specs, out_specs=out_specs, check_vma=False
    )
```

profile of v0, /device:TPU:4, one launch (start us, length us, event | category | flops | bytes accessed | tf_op | source)
XLA Modules:
  0.0 345.8 jit_solution(14891194659746946430)
XLA Ops:
  0.6 0.0 copy-start
  0.6 0.0 copy-start.2
  0.7 0.8 compare_select_fusion.1
  1.5 1.6 gather_fusion
  3.1 0.7 compare_select_fusion
  3.7 1.6 gather_fusion.1
  5.3 1.1 fusion.4
  6.5 0.1 copy.43
  6.6 0.1 reshape.111
  6.7 2.1 fusion.3
  8.8 0.1 copy.41
  8.9 0.1 reshape.109
  9.0 0.7 broadcast_in_dim.16
  9.7 9.1 %all-to-all-start.1 = ((f32[8,1,4096]{2,1,0:T(1,128)}), f32[8,1,4096]{2,1,0:T(1,128)S(1)}, u32[]{:S(2)}, u32[]{:S(2)}) async-start(f32[8,1,4096]{2,1,0:T(1,128)} %broadcast_in_dim.16), calls=%async_computation.1 | async-start | bytes 262144 | tf_op jit(solution)/shard_map/all_to_all | solution.py:11
  18.9 0.0 copy-done
  18.9 0.0 copy-done.2
  18.9 2.7 fusion.11
  21.6 0.7 all-to-all-done.1
  22.3 0.0 copy-start.1
  22.3 7.3 %all-to-all-start = ((f32[8,1024,128]{2,1,0:T(8,128)}), f32[8,1024,128]{2,1,0:T(8,128)}, u32[]{:S(2)}, u32[]{:S(2)}) async-start(f32[8,1024,128]{2,1,0:T(8,128)} %bitcast.45), calls=%async_computation | async-start | bytes 8388608 | tf_op jit(solution)/shard_map/all_to_all | solution.py:36
  29.6 0.1 reduce_sum.39
  29.7 0.1 reshape.112
  29.8 0.1 copy.45
  29.8 0.1 reshape.113
  29.9 0.1 copy.48
  30.0 0.1 multiply_convert_fusion
  30.0 0.1 copy.47
  30.1 0.0 copy-done.1
  30.1 1.8 multiply_bitcast_fusion
  31.9 0.1 copy.49
  32.0 0.2 convolution_multiply_fusion
  32.2 308.3 %all-reduce.2 = (bf16[1024,512]{0,1:T(8,128)(2,1)}, bf16[512,128]{1,0:T(8,128)(2,1)}) all-reduce(f32[1024,512]{0,1:T(8,128)} %multiply_bitcast_fusion, f32[512,128]{1,0:T(8,128)S(1)} %convolution_multiply_fusion), channel_id=1, replica_groups=mesh['dp'=64,'tensor'=8] {'dp'}, use_global_device_ids=true, to_apply=%region_4.5 | all-reduce | flops 589824 | bytes 3538944 | tf_op jit(solution)/shard_map/psum | solution.py:89
  340.5 0.0 all-to-all-done
  340.5 2.4 reduce_sum.36
  342.9 0.2 copy.39
  343.1 2.7 fusion.2
  (6 shorter events, 0.0 us)
Async XLA Ops:
  0.6 18.2 %copy-start = (bf16[8192,128]{1,0:T(8,128)(2,1)S(1)}, bf16[8192,128]{1,0:T(8,128)(2,1)}, u32[]{:S(2)}) copy-start(bf16[8192,128]{1,0:T(8,128)(2,1)} %param.10) | copy-start | bytes 6291460
  0.6 18.2 %copy-start.2 = (bf16[128,128]{1,0:T(8,128)(2,1)S(1)}, bf16[128,128]{1,0:T(8,128)(2,1)}, u32[]{:S(2)}) copy-start(bf16[128,128]{1,0:T(8,128)(2,1)} %param.9) | copy-start | bytes 98308
  9.7 12.6 %all-to-all-start.1 = ((f32[8,1,4096]{2,1,0:T(1,128)}), f32[8,1,4096]{2,1,0:T(1,128)S(1)}, u32[]{:S(2)}, u32[]{:S(2)}) async-start(f32[8,1,4096]{2,1,0:T(1,128)} %broadcast_in_dim.16), calls=%async_computation.1 | async-start | bytes 262144 | tf_op jit(solution)/shard_map/all_to_all | solution.py:11
  22.3 7.8 %copy-start.1 = (bf16[128,1024]{1,0:T(8,128)(2,1)S(1)}, bf16[128,1024]{1,0:T(8,128)(2,1)}, u32[]{:S(2)}) copy-start(bf16[128,1024]{1,0:T(8,128)(2,1)} %param.8) | copy-start | bytes 786436
  22.3 318.2 %all-to-all-start = ((f32[8,1024,128]{2,1,0:T(8,128)}), f32[8,1024,128]{2,1,0:T(8,128)}, u32[]{:S(2)}, u32[]{:S(2)}) async-start(f32[8,1024,128]{2,1,0:T(8,128)} %bitcast.45), calls=%async_computation | async-start | bytes 8388608 | tf_op jit(solution)/shard_map/all_to_all | solution.py:36
where the time goes:
time: 346 us
  blocking collectives  308 us (89%)
  starting transfers between devices  16.4 us (5%)
  matrix products  10.6 us (3%)
  local copies, waits for them, and re-layouts  4.87 us (1%)
  other arithmetic  4.14 us (1%)
    psum x1, blocking collectives, per_device(): lax.psum((down_gradient_piece, up_gradient_piece), 'dp')  308 us
    all_to_all x1, starting transfers between devices, from_everyone(): lax.all_to_all(jnp.broadcast_to(value[None], (length, *value.shape)), axi...  9.15 us
    all_to_all x1, starting transfers between devices, sum_at_owner(): lax.all_to_all(cut_along(value, dim, length), axis, 0, 0, tiled=True)  7.27 us
  transfers between devices with their start and end apart: 2, of which 1 were waited for; matrix products, arithmetic and copies ran while one was open for 2% of the time, Pallas kernels for 0%

commit v1 on v0

v1 whole, which is shorter than its diff:
```python
import jax
import jax.numpy as jnp
from jax import lax
from jax.experimental import pallas as pl
from jax.experimental.pallas import tpu as pltpu
from jax.sharding import Mesh, PartitionSpec as P

adapter_scale = 2.0

Z, Y, T = 16, 4, 8
SLOTS, RANK = 32, 16
ROWS = SLOTS * RANK
bf16, f32 = jnp.bfloat16, jnp.float32
NT = (((1,), (1,)), ((), ()))


def call(body, outs, flops=0, **kw):
    return pl.pallas_call(
        body,
        out_shape=[jax.ShapeDtypeStruct(s, d) for s, d in outs],
        cost_estimate=pl.CostEstimate(flops=flops, bytes_accessed=0, transcendentals=0),
        **kw,
    )


def members(slot):
    return lax.broadcasted_iota(jnp.int32, (ROWS, slot.shape[1]), 0) // RANK == slot


def spread(low, member):
    return jnp.where(member, jnp.concatenate([low] * SLOTS, axis=0), 0.0)


def partial_kernel(x, c, down, up, doc, tenant, index, pack, part, slot_out):
    n = x.shape[0]
    tenant_of = (lax.broadcasted_iota(jnp.int32, (SLOTS, tenant.shape[1]), 0) == tenant[...]).astype(bf16)
    table = jnp.broadcast_to(index[...].astype(f32), (8, SLOTS)).astype(bf16)
    slot_of_doc = jnp.dot(table, tenant_of, preferred_element_type=f32).astype(bf16)
    doc_of = (lax.broadcasted_iota(jnp.int32, (tenant.shape[1], n), 0) == doc[...]).astype(bf16)
    slot = jnp.dot(slot_of_doc, doc_of, preferred_element_type=f32)
    slot_out[...] = slot
    member = members(slot[:1].astype(jnp.int32))
    xt = x[...].astype(f32).T
    ct = c[...].astype(f32).T
    h_all = jnp.dot(down[...], xt.astype(bf16), preferred_element_type=f32)
    g_all = jnp.dot(up[...], ct.astype(bf16), preferred_element_type=f32)
    g = jnp.sum(jnp.where(member, g_all, 0.0).reshape(SLOTS, RANK, n), axis=0)
    h = jnp.sum(jnp.where(member, h_all, 0.0).reshape(SLOTS, RANK, n), axis=0)
    both = jnp.concatenate([g, h], axis=0)
    for i in range(T):
        part[i] = both
    fx, fc = xt.shape[0] // Z, ct.shape[0] // Z
    for z in range(Z):
        pack[z] = jnp.concatenate(
            [xt[z * fx : (z + 1) * fx], ct[z * fc : (z + 1) * fc], slot], axis=0
        ).astype(bf16)


def low_kernel(parts, low, mine):
    total = jnp.sum(parts[...], axis=0).astype(bf16)
    mine[...] = total
    for z in range(Z):
        low[z] = total


def gradient_kernel(pack, low, out):
    fx, fc = 64, 8
    xs, cs, gs, hs = [], [], [], []
    for z in range(Z):
        block = pack[z].astype(f32)
        member = members(block[fx + fc : fx + fc + 1].astype(jnp.int32))
        both = low[z].astype(f32)
        xs.append(block[:fx].astype(bf16))
        cs.append(block[fx : fx + fc].astype(bf16))
        gs.append(spread(both[:RANK], member).astype(bf16))
        hs.append(spread(both[RANK:], member).astype(bf16))
    cat = lambda v: jnp.concatenate(v, axis=1)
    down = lax.dot_general(cat(xs), cat(gs), NT, preferred_element_type=f32)
    up = lax.dot_general(cat(cs), cat(hs), NT, preferred_element_type=f32)
    both = jnp.concatenate([down, up], axis=0)
    rows = ROWS // Y
    for y in range(Y):
        out[y] = both[:, y * rows : (y + 1) * rows]


def finish_kernel(parts, out):
    total = (adapter_scale * jnp.sum(parts[...], axis=0)).astype(bf16)
    for z in range(Z):
        out[z] = total


def layout_kernel(parts, out):
    fx = 64
    v = parts[...].astype(f32)
    down = v[:, :fx].reshape(-1, v.shape[2]).T
    up = v[:, fx:].reshape(-1, v.shape[2]).T
    both = jnp.concatenate([down, up], axis=1).astype(bf16)
    for y in range(Y):
        out[y] = both


def frozen_kernel(c, w, out):
    out[0] = lax.dot_general(c[...], w[...], NT, preferred_element_type=f32).astype(bf16)


def input_kernel(parts, low, slot, down, out):
    g = low[...].astype(f32)[:RANK]
    s = spread(g, members(slot[:1].astype(jnp.int32))).T.astype(bf16)
    adapter = jnp.dot(s, down[...], preferred_element_type=f32)
    frozen = jnp.sum(parts[...].astype(f32), axis=0)
    out[...] = (frozen + adapter_scale * adapter).astype(bf16)


def swap(value, axis):
    return lax.all_to_all(value, axis, 0, 0, tiled=True)


def per_device(x, c, w, down, up, doc, tenant, index):
    n, fx = x.shape
    fc = c.shape[1]
    down_rows = jnp.transpose(down, (0, 2, 1)).reshape(ROWS, fx)
    up_rows = up.reshape(ROWS, fc)
    pack, part, slot = call(
        partial_kernel, [((Z, 80, n), bf16), ((T, 32, n), f32), ((8, n), f32)], flops=10**9
    )(x, c, down_rows, up_rows, doc[None], tenant[None], index[None])
    parts = swap(part, "tensor")
    packs = swap(pack, "z")
    low, mine = call(low_kernel, [((Z, 32, n), bf16), ((32, n), bf16)])(parts)
    lows = swap(low, "z")
    (frozen,) = call(
        frozen_kernel,
        [((T, n, fx), bf16)],
        flops=2 * n * fc * fx * T,
        grid=(T,),
        in_specs=[pl.BlockSpec((n, fc), lambda i: (0, 0)), pl.BlockSpec((fx, fc), lambda i: (i, 0))],
        out_specs=[pl.BlockSpec((1, n, fx), lambda i: (i, 0, 0))],
    )(c, w)
    frozens = swap(frozen, "tensor")
    (piece,) = call(gradient_kernel, [((Y, 72, ROWS // Y), f32)], flops=2 * 2048 * 512 * 512)(packs, lows)
    (mine_out,) = call(finish_kernel, [((Z, 72, ROWS // Y), bf16)])(swap(piece, "y"))
    (block,) = call(layout_kernel, [((Y, ROWS // Y, fx + fc), bf16)])(swap(mine_out, "z"))
    (input_gradient,) = call(input_kernel, [((n, fx), bf16)], flops=10**9)(frozens, mine, slot, down_rows)
    whole = swap(block, "y").reshape(ROWS, fx + fc)
    down_gradient = jnp.transpose(whole[:, :fx].reshape(SLOTS, RANK, fx), (0, 2, 1))
    up_gradient = whole[:, fx:].reshape(SLOTS, RANK, fc)
    return input_gradient, down_gradient, up_gradient


def solution(mesh):
    grid = Mesh(mesh.devices.reshape(Z, Y, T), ("z", "y", "tensor"))
    dp = ("z", "y")
    in_specs = (
        P(dp, "tensor"),
        P(dp, "tensor"),
        P(None, "tensor"),
        P(None, "tensor", None),
        P(None, None, "tensor"),
        P(dp),
        P(),
        P(),
    )
    out_specs = (P(dp, "tensor"), P(None, "tensor", None), P(None, None, "tensor"))
    return jax.shard_map(
        per_device, mesh=grid, in_specs=in_specs, out_specs=out_specs, check_vma=False
    )
```

time: 346 us -> 161 us (0.47)
  the two profiles are of different devices: /device:TPU:4 before, /device:TPU:1 now
where the time goes in v1:
time: 161 us; the launch traced here: 160 us
  blocking collectives  66.9 us (42%)
  waiting for transfers between devices  43.2 us (27%)
  starting transfers between devices  27.5 us (17%)
  Pallas kernels  20.5 us (13%)
  local copies, waits for them, and re-layouts  1.79 us (1%)
    all_to_all x4, blocking collectives, swap(): return lax.all_to_all(value, axis, 0, 0, tiled=True)  66.9 us
    all_to_all x3, waiting for transfers between devices, swap(): return lax.all_to_all(value, axis, 0, 0, tiled=True)  43.2 us
    all_to_all x3, starting transfers between devices, swap(): return lax.all_to_all(value, axis, 0, 0, tiled=True)  27.5 us
    pallas_call x1, Pallas kernels, per_device(): call(frozen_kernel, [((T, n, fx), bf16)], flops=2 * n * fc * fx * T, grid...  6.41 us
  transfers between devices with their start and end apart: 3, of which 3 were waited for; matrix products, arithmetic and copies ran while one was open for 0% of the time, Pallas kernels for 7%

profile of v1, /device:TPU:1, one launch (start us, length us, event | category | flops | bytes accessed | tf_op | source)
XLA Modules:
  0.0 160.5 jit_solution(9414593015767681578)
XLA Ops:
  0.6 2.7 %shard_map.104 = (bf16[16,80,128]{2,1,0:T(8,128)(2,1)}, f32[8,32,128]{2,1,0:T(8,128)}, f32[8,128]{1,0:T(8,128)}) custom-call(bf16[128,1024]{1,0:T(8,128)(2,1)} %x.1, bf16[128,128]{1,0:T(8,128)(2,1)} %c.3, bf16[512,1024]{1,0:T(8,128)(2,1)} %bitcast.16, bf16[512,128]{1,0:T(8,128)(2,1)} %bitcast.18, s32[1,128]{1,0:T(1,128)} %bitcast.19, s32[1,128]{1,0:T(1,128)} %bitcast.20, ...), custom_call_target="tpu_custom_call" | custom-call | flops 1000000000 | tf_op jit(solution)/shard_map/pallas_call | solution.py:123
  3.3 16.0 %all_to_all.35.parts = f32[8,32,128]{2,1,0:T(8,128)} all-to-all(f32[8,32,128]{2,1,0:T(8,128)} %get-tuple-element.8), channel_id=1, replica_groups=mesh['z'=16,'y'=4,'tensor'=8] {'tensor'}, dimensions={0} | all-to-all | bytes 262144 | tf_op jit(solution)/shard_map/all_to_all | solution.py:115
  19.3 1.6 shard_map.105
  20.9 22.1 %all_to_all.36.low = bf16[16,32,128]{2,1,0:T(8,128)(2,1)} all-to-all(bf16[16,32,128]{2,1,0:T(8,128)(2,1)} %get-tuple-element.12), channel_id=1, replica_groups=mesh['z'=16,'y'=4,'tensor'=8] {'z'}, dimensions={0} | all-to-all | bytes 262144 | tf_op jit(solution)/shard_map/all_to_all | solution.py:115
  43.0 19.5 %all_to_all.37.pack = bf16[16,80,128]{2,1,0:T(8,128)(2,1)} all-to-all(bf16[16,80,128]{2,1,0:T(8,128)(2,1)} %get-tuple-element.11), channel_id=1, replica_groups=mesh['z'=16,'y'=4,'tensor'=8] {'z'}, dimensions={0} | all-to-all | bytes 655360 | tf_op jit(solution)/shard_map/all_to_all | solution.py:115
  62.5 3.0 %shard_map.107 = f32[4,72,128]{2,1,0:T(8,128)} custom-call(bf16[16,80,128]{2,1,0:T(8,128)(2,1)} %all_to_all.37.pack, bf16[16,32,128]{2,1,0:T(8,128)(2,1)} %all_to_all.36.low), custom_call_target="tpu_custom_call" | custom-call | flops 1073741824 | tf_op jit(solution)/shard_map/pallas_call | solution.py:139
  65.5 9.2 %all_to_all.38.parts = f32[4,72,128]{2,1,0:T(8,128)} all-to-all(f32[4,72,128]{2,1,0:T(8,128)} %shard_map.107), channel_id=1, replica_groups=mesh['z'=16,'y'=4,'tensor'=8] {'y'}, dimensions={0} | all-to-all | bytes 294912 | tf_op jit(solution)/shard_map/all_to_all | solution.py:115
  74.7 1.6 %shard_map.108 = bf16[16,72,128]{2,1,0:T(8,128)(2,1)} custom-call(f32[4,72,128]{2,1,0:T(8,128)} %all_to_all.38.parts), custom_call_target="tpu_custom_call" | custom-call | tf_op jit(solution)/shard_map/pallas_call | solution.py:140
  76.3 12.6 %all-to-all-start.5 = ((bf16[16,72,128]{2,1,0:T(8,128)(2,1)}), bf16[16,72,128]{2,1,0:T(8,128)(2,1)S(1)}, u32[]{:S(2)}, u32[]{:S(2)}) async-start(bf16[16,72,128]{2,1,0:T(8,128)(2,1)} %shard_map.108), calls=%async_computation.5 | async-start | bytes 589824 | tf_op jit(solution)/shard_map/all_to_all | solution.py:115
  88.9 6.4 %shard_map.103 = bf16[8,128,1024]{2,1,0:T(8,128)(2,1)} custom-call(bf16[128,128]{1,0:T(8,128)(2,1)} %c.3, bf16[8192,128]{1,0:T(8,128)(2,1)} %w.1), custom_call_target="tpu_custom_call" | custom-call | flops 268435456 | tf_op jit(solution)/shard_map/pallas_call | solution.py:130
  95.3 6.6 %all-to-all-done.5.parts = bf16[16,72,128]{2,1,0:T(8,128)(2,1)S(1)} async-done(((bf16[16,72,128]{2,1,0:T(8,128)(2,1)}), bf16[16,72,128]{2,1,0:T(8,128)(2,1)S(1)}, u32[]{:S(2)}, u32[]{:S(2)}) %all-to-all-start.5) | async-done | bytes 294944 | tf_op jit(solution)/shard_map/all_to_all | solution.py:115
  101.9 0.0 copy-start.1
  101.9 11.4 %all-to-all-start = ((bf16[8,128,1024]{2,1,0:T(8,128)(2,1)}), bf16[8,128,1024]{2,1,0:T(8,128)(2,1)S(1)}, u32[]{:S(2)}, u32[]{:S(2)}) async-start(bf16[8,128,1024]{2,1,0:T(8,128)(2,1)} %shard_map.103), calls=%async_computation | async-start | bytes 4194304 | tf_op jit(solution)/shard_map/all_to_all | solution.py:115
  113.3 0.0 copy-done.1
  113.3 2.2 %shard_map.109 = bf16[4,128,1152]{2,1,0:T(8,128)(2,1)} custom-call(bf16[16,72,128]{2,1,0:T(8,128)(2,1)} %copy-done.1), custom_call_target="tpu_custom_call" | custom-call | tf_op jit(solution)/shard_map/pallas_call | solution.py:141
  115.5 24.1 %all-to-all-done.parts = bf16[8,128,1024]{2,1,0:T(8,128)(2,1)S(1)} async-done(((bf16[8,128,1024]{2,1,0:T(8,128)(2,1)}), bf16[8,128,1024]{2,1,0:T(8,128)(2,1)S(1)}, u32[]{:S(2)}, u32[]{:S(2)}) %all-to-all-start) | async-done | bytes 2097184 | tf_op jit(solution)/shard_map/all_to_all | solution.py:115
  139.6 0.0 copy-start
  139.6 3.5 %all-to-all-start.6 = ((bf16[4,128,1152]{2,1,0:T(8,128)(2,1)}), bf16[4,128,1152]{2,1,0:T(8,128)(2,1)S(1)}, u32[]{:S(2)}, u32[]{:S(2)}) async-start(bf16[4,128,1152]{2,1,0:T(8,128)(2,1)} %shard_map.109), calls=%async_computation.6 | async-start | bytes 2359296 | tf_op jit(solution)/shard_map/all_to_all | solution.py:115
  143.1 0.0 copy-done
  143.1 3.1 %shard_map.106 = bf16[128,1024]{1,0:T(8,128)(2,1)} custom-call(bf16[8,128,1024]{2,1,0:T(8,128)(2,1)} %copy-done, bf16[32,128]{1,0:T(8,128)(2,1)} %get-tuple-element.9.low, f32[8,128]{1,0:T(8,128)} %get-tuple-element.10.slot, bf16[512,1024]{1,0:T(8,128)(2,1)} %bitcast.17), custom_call_target="tpu_custom_call" | custom-call | flops 1000000000 | tf_op jit(solution)/shard_map/pallas_call | solution.py:142
  146.2 12.5 %all-to-all-done.6 = bf16[4,128,1152]{2,1,0:T(8,128)(2,1)S(1)} async-done(((bf16[4,128,1152]{2,1,0:T(8,128)(2,1)}), bf16[4,128,1152]{2,1,0:T(8,128)(2,1)S(1)}, u32[]{:S(2)}, u32[]{:S(2)}) %all-to-all-start.6) | async-done | bytes 1179680 | tf_op jit(solution)/shard_map/all_to_all | solution.py:115
  158.7 1.1 slice.8
  159.8 0.7 slice.9
Async XLA Ops:
  76.3 25.6 %all-to-all-start.5 = ((bf16[16,72,128]{2,1,0:T(8,128)(2,1)}), bf16[16,72,128]{2,1,0:T(8,128)(2,1)S(1)}, u32[]{:S(2)}, u32[]{:S(2)}) async-start(bf16[16,72,128]{2,1,0:T(8,128)(2,1)} %shard_map.108), calls=%async_computation.5 | async-start | bytes 589824 | tf_op jit(solution)/shard_map/all_to_all | solution.py:115
  101.9 11.4 %copy-start.1 = (bf16[16,72,128]{2,1,0:T(8,128)(2,1)}, bf16[16,72,128]{2,1,0:T(8,128)(2,1)S(1)}, u32[]{:S(2)}) copy-start(bf16[16,72,128]{2,1,0:T(8,128)(2,1)S(1)} %all-to-all-done.5.parts) | copy-start | bytes 884740
  101.9 37.6 %all-to-all-start = ((bf16[8,128,1024]{2,1,0:T(8,128)(2,1)}), bf16[8,128,1024]{2,1,0:T(8,128)(2,1)S(1)}, u32[]{:S(2)}, u32[]{:S(2)}) async-start(bf16[8,128,1024]{2,1,0:T(8,128)(2,1)} %shard_map.103), calls=%async_computation | async-start | bytes 4194304 | tf_op jit(solution)/shard_map/all_to_all | solution.py:115
  139.6 3.5 %copy-start = (bf16[8,128,1024]{2,1,0:T(8,128)(2,1)}, bf16[8,128,1024]{2,1,0:T(8,128)(2,1)S(1)}, u32[]{:S(2)}) copy-start(bf16[8,128,1024]{2,1,0:T(8,128)(2,1)S(1)} %all-to-all-done.parts) | copy-start | bytes 6291460
  139.6 19.1 %all-to-all-start.6 = ((bf16[4,128,1152]{2,1,0:T(8,128)(2,1)}), bf16[4,128,1152]{2,1,0:T(8,128)(2,1)S(1)}, u32[]{:S(2)}, u32[]{:S(2)}) async-start(bf16[4,128,1152]{2,1,0:T(8,128)(2,1)} %shard_map.109), calls=%async_computation.6 | async-start | bytes 2359296 | tf_op jit(solution)/shard_map/all_to_all | solution.py:115

commit v2 on v1

v2 whole, which is shorter than its diff:
```python
import jax
import jax.numpy as jnp
from jax import lax
from jax.experimental import pallas as pl
from jax.experimental.pallas import tpu as pltpu
from jax.sharding import Mesh, PartitionSpec as P

adapter_scale = 2.0

Z, Y, T = 16, 4, 8
SLOTS, RANK = 32, 16
ROWS = SLOTS * RANK
bf16, f32 = jnp.bfloat16, jnp.float32
NT = (((1,), (1,)), ((), ()))


def call(body, outs, flops=0, **kw):
    return pl.pallas_call(
        body,
        out_shape=[jax.ShapeDtypeStruct(s, d) for s, d in outs],
        cost_estimate=pl.CostEstimate(flops=flops, bytes_accessed=0, transcendentals=0),
        **kw,
    )


def spread(low, slot, first=0, slots=SLOTS):
    at = lax.broadcasted_iota(jnp.int32, (slots * RANK, low.shape[1]), 0) // RANK + first
    return jnp.where(at == slot, jnp.concatenate([low] * slots, axis=0), 0.0)


def partial_kernel(x, c, down, up, doc, tenant, index, me, pack, part, slot_out):
    n = x.shape[0]
    tenant_of = (lax.broadcasted_iota(jnp.int32, (SLOTS, tenant.shape[1]), 0) == tenant[...]).astype(bf16)
    table = jnp.broadcast_to(index[...].astype(f32), (8, SLOTS)).astype(bf16)
    slot_of_doc = jnp.dot(table, tenant_of, preferred_element_type=f32).astype(bf16)
    doc_of = (lax.broadcasted_iota(jnp.int32, (tenant.shape[1], n), 0) == doc[...]).astype(bf16)
    slot = jnp.dot(slot_of_doc, doc_of, preferred_element_type=f32)
    slot_out[...] = slot
    member = lax.broadcasted_iota(jnp.int32, (ROWS, n), 0) // RANK == slot[:1].astype(jnp.int32)
    h_all = lax.dot_general(down[...], x[...], NT, preferred_element_type=f32)
    g_all = lax.dot_general(up[...], c[...], NT, preferred_element_type=f32)
    g = jnp.sum(jnp.where(member, g_all, 0.0).reshape(SLOTS, RANK, n), axis=0)
    h = jnp.sum(jnp.where(member, h_all, 0.0).reshape(SLOTS, RANK, n), axis=0)
    both = jnp.concatenate([g, h], axis=0)
    for i in range(Y * T):
        part[i] = both
    fx = x.shape[1] // Y
    slots = jnp.concatenate([slot, jnp.zeros((8, pack.shape[2] - n), f32)], axis=1)
    for y in range(Y):
        mine = jnp.concatenate([x[:, y * fx : (y + 1) * fx], c[...]], axis=1)
        pack[(y - me[0]) & (Y - 1)] = jnp.concatenate([mine.astype(f32), slots], axis=0).astype(bf16)


def gradient_kernel(me, parts, p0, p1, p2, p3, out, low_out):
    fx = p0.shape[1] - 128
    gs, hs = [], []
    for k, pack in enumerate((p0, p1, p2, p3)):
        at = (me[0] - k) & (Y - 1)
        both = parts[at * T]
        for j in range(1, T):
            both = both + parts[at * T + j]
        both = both.astype(bf16)
        if k == 0:
            low_out[...] = both
        both = both.astype(f32)
        slot = pack[128:, :128].astype(f32)[:1].astype(jnp.int32)
        gs.append(spread(both[:RANK], slot).astype(bf16))
        hs.append(spread(both[RANK:], slot, me[0] * (SLOTS // Y), SLOTS // Y).astype(bf16))
    xs = jnp.concatenate([p[:128, :fx] for p in (p0, p1, p2, p3)], axis=0)
    cs = jnp.concatenate([p[:128, fx:] for p in (p0, p1, p2, p3)], axis=0)
    down = jnp.dot(jnp.concatenate(gs, axis=1), xs, preferred_element_type=f32)
    up = jnp.dot(jnp.concatenate(hs, axis=1), cs, preferred_element_type=f32)
    rd, ru = ROWS // Z, ROWS // Y // Z
    for z in range(Z):
        one = down[z * rd : (z + 1) * rd]
        out[z] = jnp.concatenate([one[:, :128], one[:, 128:], up[z * ru : (z + 1) * ru]], axis=0).astype(bf16)


def finish_kernel(parts, out):
    total = (adapter_scale * jnp.sum(parts[...].astype(f32), axis=0)).astype(bf16)
    for z in range(Z):
        out[z] = total


def layout_kernel(me, g0, g1, g2, g3, down, up):
    rd = ROWS // Z
    for k, g in enumerate((g0, g1, g2, g3)):
        at = (me[0] - k) & (Y - 1)
        v = g[...].astype(f32)
        down[:, pl.ds(pl.multiple_of(at * 256, 256), 128)] = v[:, :rd].reshape(ROWS, 128).astype(bf16)
        down[:, pl.ds(pl.multiple_of(at * 256 + 128, 128), 128)] = v[:, rd : 2 * rd].reshape(ROWS, 128).astype(bf16)
        up[pl.ds(pl.multiple_of(at * 128, 128), 128)] = v[:, 2 * rd :].reshape(128, 128).astype(bf16)


def frozen_kernel(where, c, w, out):
    out[0] = lax.dot_general(c[...], w[...], NT, preferred_element_type=f32).astype(bf16)


def pair_kernel(kept, came, o0, o1, o2, o3):
    for k, out in enumerate((o0, o1, o2, o3)):
        out[...] = (kept[k].astype(f32) + came[k].astype(f32)).astype(bf16)


def input_kernel(f0, f1, f2, f3, low, slot, down, out):
    g = low[...].astype(f32)[:RANK]
    s = spread(g, slot[:1].astype(jnp.int32)).T.astype(bf16)
    adapter = jnp.dot(s, down[...], preferred_element_type=f32)
    frozen = (f0[...].astype(f32) + f1[...].astype(f32)) + (f2[...].astype(f32) + f3[...].astype(f32))
    out[...] = (frozen + adapter_scale * adapter).astype(bf16)


def swap(value, axis):
    return lax.all_to_all(value, axis, 0, 0, tiled=True)


def shift(value, axis, by):
    size = lax.axis_size(axis)
    return lax.ppermute(value, axis, [(i, (i + by) % size) for i in range(size)])


def specs(count):
    return [pl.BlockSpec(memory_space=pltpu.SMEM)] + [pl.BlockSpec(memory_space=pltpu.VMEM)] * count


def frozen_blocks(c, w, place):
    n, fc = c.shape
    fx = w.shape[0] // T
    return pl.pallas_call(
        frozen_kernel,
        grid_spec=pltpu.PrefetchScalarGridSpec(
            num_scalar_prefetch=1,
            grid=(4,),
            in_specs=[
                pl.BlockSpec((n, fc), lambda i, p: (0, 0)),
                pl.BlockSpec((fx, fc), lambda i, p: (((p[0] + i) & 3) * 2 + p[1], 0)),
            ],
            out_specs=pl.BlockSpec((1, n, fx), lambda i, p: (i, 0, 0)),
        ),
        out_shape=jax.ShapeDtypeStruct((4, n, fx), bf16),
        cost_estimate=pl.CostEstimate(flops=10**9, bytes_accessed=0, transcendentals=0),
    )(place, c, w)


def per_device(x, c, w, down, up, doc, tenant, index):
    n, fx = x.shape
    fc = c.shape[1]
    me = lax.axis_index("y")[None]
    at = lax.axis_index("tensor")
    down_rows = jnp.transpose(down, (0, 2, 1)).reshape(ROWS, fx)
    up_rows = up.reshape(ROWS, fc)
    block = (ROWS // Z * 2 + ROWS // Y // Z, 128)
    pack, part, slot = call(
        partial_kernel,
        [((Y, n + 8, fx // Y + fc), bf16), ((Y * T, 2 * RANK, n), f32), ((8, n), f32)],
        flops=10**9,
        in_specs=[pl.BlockSpec(memory_space=pltpu.VMEM)] * 7 + [pl.BlockSpec(memory_space=pltpu.SMEM)],
    )(x, c, down_rows, up_rows, doc[None], tenant[None], index[None], me)
    parts = swap(part, ("y", "tensor"))
    packs = [pack[0]]
    for k in (1, 2, 3):
        packs.append(shift(pack[k], "y", k))
    piece, low = call(
        gradient_kernel,
        [((Z, *block), bf16), ((2 * RANK, n), bf16)],
        flops=10**9,
        in_specs=specs(5),
    )(me, parts, *packs)
    sums = swap(piece, "z")
    send = frozen_blocks(c, w, jnp.stack([at // 2, 1 - at % 2]))
    came = lax.ppermute(send, "tensor", [(j, j ^ 1) for j in range(T)])
    kept = frozen_blocks(c, w, jnp.stack([at // 2, at % 2]))
    pairs = call(pair_kernel, [((n, fx), bf16)] * 4, flops=10**8)(kept, came)
    frozens = [pairs[0]]
    for k in (1, 2, 3):
        frozens.append(shift(pairs[k], "tensor", 2 * k))
    (done,) = call(finish_kernel, [((Z, *block), bf16)], flops=10**8)(sums)
    rows = swap(done, "z")
    (input_gradient,) = call(input_kernel, [((n, fx), bf16)], flops=10**9)(*frozens, low, slot, down_rows)
    outs = [rows]
    for k in (1, 2, 3):
        outs.append(shift(rows, "y", k))
    whole, up_whole = call(layout_kernel, [((ROWS, fx), bf16), ((ROWS, fc), bf16)], in_specs=specs(4))(me, *outs)
    down_gradient = jnp.transpose(whole.reshape(SLOTS, RANK, fx), (0, 2, 1))
    up_gradient = up_whole.reshape(SLOTS, RANK, fc)
    return input_gradient, down_gradient, up_gradient


def solution(mesh):
    grid = Mesh(mesh.devices.reshape(Z, Y, T), ("z", "y", "tensor"))
    dp = ("z", "y")
    in_specs = (
        P(dp, "tensor"),
        P(dp, "tensor"),
        P(None, "tensor"),
        P(None, "tensor", None),
        P(None, None, "tensor"),
        P(dp),
        P(),
        P(),
    )
    out_specs = (P(dp, "tensor"), P(None, "tensor", None), P(None, None, "tensor"))

    return jax.shard_map(per_device, mesh=grid, in_specs=in_specs, out_specs=out_specs, check_vma=False)
```

time: 161 us -> 116 us (0.72)
  the two profiles are of different devices: /device:TPU:1 before, /device:TPU:8 now
where the time goes in v2:
time: 116 us; the launch traced here: 115 us
  starting transfers between devices  62.2 us (54%)
  Pallas kernels  23.6 us (20%)
  waiting for transfers between devices  21.4 us (18%)
  local copies, waits for them, and re-layouts  5.72 us (5%)
  other arithmetic  1.31 us (1%)
    ppermute x9, starting transfers between devices, shift(): lax.ppermute(value, axis, [(i, (i + by) % size) for i in range(size)])  31.5 us
    all_to_all x3, starting transfers between devices, swap(): return lax.all_to_all(value, axis, 0, 0, tiled=True)  28.8 us
    all_to_all x3, waiting for transfers between devices, swap(): return lax.all_to_all(value, axis, 0, 0, tiled=True)  12.4 us
    ppermute x9, waiting for transfers between devices, shift(): lax.ppermute(value, axis, [(i, (i + by) % size) for i in range(size)])  8.98 us
    pallas_call x2, Pallas kernels, frozen_blocks(): pl.pallas_call(frozen_kernel, grid_spec=pltpu.PrefetchScalarGridSpec(num_...  8.93 us
    unnamed x26, local copies, waits for them, and re-layouts  3.98 us
    pallas_call x1, Pallas kernels, per_device(): call(partial_kernel, [((Y, n + 8, fx // Y + fc), bf16), ((Y * T, 2 * RANK...  2.92 us
    pallas_call x1, Pallas kernels, per_device(): call(input_kernel, [((n, fx), bf16)], flops=10 ** 9)  2.64 us
  transfers between devices with their start and end apart: 13, of which 5 were waited for; matrix products, arithmetic and copies ran while one was open for 3% of the time, Pallas kernels for 14%

profile of v2, /device:TPU:8, one launch (start us, length us, event | category | flops | bytes accessed | tf_op | source)
XLA Modules:
  0.0 115.2 jit_solution(4922235281402061908)
XLA Ops:
  0.6 2.9 %shard_map.106 = (bf16[4,136,384]{2,1,0:T(8,128)(2,1)}, f32[32,32,128]{2,1,0:T(8,128)}, f32[8,128]{1,0:T(8,128)}) custom-call(bf16[128,1024]{1,0:T(8,128)(2,1)} %x.1, bf16[128,128]{1,0:T(8,128)(2,1)} %c.5, bf16[512,1024]{1,0:T(8,128)(2,1)} %bitcast.23, bf16[512,128]{1,0:T(8,128)(2,1)} %bitcast.26, s32[1,128]{1,0:T(1,128)} %bitcast.28, s32[1,128]{1,0:T(1,128)} %bitcast.29, ...), custom_call_target="tpu_custom_call" | custom-call | flops 1000000000 | tf_op jit(solution)/shard_map/pallas_call | solution.py:152
  3.6 9.4 %all-to-all-start = ((f32[32,32,128]{2,1,0:T(8,128)}), f32[32,32,128]{2,1,0:T(8,128)S(1)}, u32[]{:S(2)}, u32[]{:S(2)}) async-start(f32[32,32,128]{2,1,0:T(8,128)} %get-tuple-element.18), calls=%async_computation | async-start | bytes 1048576 | tf_op jit(solution)/shard_map/all_to_all | solution.py:113
  12.9 1.7 %slice_bitcast_fusion = (bf16[136,384]{1,0:T(8,128)(2,1)S(1)}, bf16[136,384]{1,0:T(8,128)(2,1)S(1)}, bf16[136,384]{1,0:T(8,128)(2,1)S(1)}, bf16[136,384]{1,0:T(8,128)(2,1)}) fusion(bf16[4,136,384]{2,1,0:T(8,128)(2,1)} %get-tuple-element.19), kind=kLoop, calls=%fused_computation | loop fusion | bytes 835584 | tf_op jit(solution)/shard_map/squeeze | solution.py:161
  14.7 3.4 %collective-permute-start.4 = (bf16[136,384]{1,0:T(8,128)(2,1)S(1)}, bf16[136,384]{1,0:T(8,128)(2,1)S(1)}, u32[]{:S(2)}, u32[]{:S(2)}) collective-permute-start(bf16[136,384]{1,0:T(8,128)(2,1)S(1)} %get-tuple-element.27), channel_id=1, source_target_pairs={{0,8},{8,16},{16,24},{24,0},{1,9},{9,17},{17,25},{25,1},{2,10},{10... | collective-permute-start | bytes 313352 | tf_op jit(solution)/shard_map/ppermute | solution.py:118
  18.1 2.8 %collective-permute-start.5 = (bf16[136,384]{1,0:T(8,128)(2,1)S(1)}, bf16[136,384]{1,0:T(8,128)(2,1)S(1)}, u32[]{:S(2)}, u32[]{:S(2)}) collective-permute-start(bf16[136,384]{1,0:T(8,128)(2,1)S(1)} %get-tuple-element.26), channel_id=1, source_target_pairs={{0,16},{8,24},{16,0},{24,8},{1,17},{9,25},{17,1},{25,9},{2,18},{10... | collective-permute-start | bytes 313352 | tf_op jit(solution)/shard_map/ppermute | solution.py:118
  20.9 4.3 %collective-permute-start.6 = (bf16[136,384]{1,0:T(8,128)(2,1)S(1)}, bf16[136,384]{1,0:T(8,128)(2,1)S(1)}, u32[]{:S(2)}, u32[]{:S(2)}) collective-permute-start(bf16[136,384]{1,0:T(8,128)(2,1)S(1)} %get-tuple-element.25), channel_id=1, source_target_pairs={{0,24},{8,0},{16,8},{24,16},{1,25},{9,1},{17,9},{25,17},{2,26},{10... | collective-permute-start | bytes 313352 | tf_op jit(solution)/shard_map/ppermute | solution.py:118
  25.2 0.0 collective-permute-done.4.p1
  25.2 0.0 copy-start.10
  25.2 1.5 %collective-permute-done.5.p2 = bf16[136,384]{1,0:T(8,128)(2,1)S(1)} collective-permute-done((bf16[136,384]{1,0:T(8,128)(2,1)S(1)}, bf16[136,384]{1,0:T(8,128)(2,1)S(1)}, u32[]{:S(2)}, u32[]{:S(2)}) %collective-permute-start.5) | collective-permute-done | bytes 104480 | tf_op jit(solution)/shard_map/ppermute | solution.py:118
  26.7 0.0 copy-start.11
  26.7 1.8 %collective-permute-done.6.p3 = bf16[136,384]{1,0:T(8,128)(2,1)S(1)} collective-permute-done((bf16[136,384]{1,0:T(8,128)(2,1)S(1)}, bf16[136,384]{1,0:T(8,128)(2,1)S(1)}, u32[]{:S(2)}, u32[]{:S(2)}) %collective-permute-start.6) | collective-permute-done | bytes 104480 | tf_op jit(solution)/shard_map/ppermute | solution.py:118
  28.5 0.0 copy-start.12
  28.5 0.0 all-to-all-done.parts
  28.5 0.0 copy-start.3
  28.5 0.0 copy-done.10
  28.6 0.0 copy-done.11
  28.6 0.6 copy-done.12
  29.2 0.2 copy-done.3
  29.4 2.3 %shard_map.107 = (bf16[16,72,128]{2,1,0:T(8,128)(2,1)}, bf16[32,128]{1,0:T(8,128)(2,1)}) custom-call(s32[1]{0:T(128)} %bitcast.3.me, f32[32,32,128]{2,1,0:T(8,128)} %copy-done.3, bf16[136,384]{1,0:T(8,128)(2,1)} %get-tuple-element.28.p0, bf16[136,384]{1,0:T(8,128)(2,1)} %copy-done.10, bf16[136,384]{1,0:T(8,128)(2,1)} %copy-done.11, bf16[136,384]{1,0:T(8,128)(2,1)} %copy-done.12), custom_call_target="tpu_custom_call" | custom-call | flops 1000000000 | tf_op jit(solution)/shard_map/pallas_call | solution.py:162
  31.6 13.3 %all-to-all-start.1 = ((bf16[16,72,128]{2,1,0:T(8,128)(2,1)}), bf16[16,72,128]{2,1,0:T(8,128)(2,1)S(1)}, u32[]{:S(2)}, u32[]{:S(2)}) async-start(bf16[16,72,128]{2,1,0:T(8,128)(2,1)} %get-tuple-element.22), calls=%async_computation.1 | async-start | bytes 589824 | tf_op jit(solution)/shard_map/all_to_all | solution.py:113
  44.9 0.7 pad_add_fusion.1.where
  45.6 4.5 %shard_map.104 = bf16[4,128,1024]{2,1,0:T(8,128)(2,1)} custom-call(s32[2]{0:T(128)} %pad_add_fusion.1.where, bf16[128,128]{1,0:T(8,128)(2,1)} %c.5, bf16[8192,128]{1,0:T(8,128)(2,1)} %w.3), custom_call_target="tpu_custom_call" | custom-call | flops 1000000000 | tf_op jit(solution)/shard_map/pallas_call | solution.py:128
  50.0 1.9 %collective-permute-start = (bf16[4,128,1024]{2,1,0:T(8,128)(2,1)}, bf16[4,128,1024]{2,1,0:T(8,128)(2,1)S(1)}, u32[]{:S(2)}, u32[]{:S(2)}) collective-permute-start(bf16[4,128,1024]{2,1,0:T(8,128)(2,1)} %shard_map.104), channel_id=1, source_target_pairs={{0,1},{1,0},{2,3},{3,2},{4,5},{5,4},{6,7},{7,6},{8,9},{9,8},{10,11... | collective-permute-start | bytes 3145736 | tf_op jit(solution)/shard_map/ppermute | solution.py:170
  52.0 12.4 %all-to-all-done.1.parts = bf16[16,72,128]{2,1,0:T(8,128)(2,1)S(1)} async-done(((bf16[16,72,128]{2,1,0:T(8,128)(2,1)}), bf16[16,72,128]{2,1,0:T(8,128)(2,1)S(1)}, u32[]{:S(2)}, u32[]{:S(2)}) %all-to-all-start.1) | async-done | bytes 294944 | tf_op jit(solution)/shard_map/all_to_all | solution.py:113
  64.4 0.0 copy-start
  64.4 0.7 copy-done
  65.1 1.7 %shard_map.109 = bf16[16,72,128]{2,1,0:T(8,128)(2,1)} custom-call(bf16[16,72,128]{2,1,0:T(8,128)(2,1)} %copy-done), custom_call_target="tpu_custom_call" | custom-call | flops 100000000 | tf_op jit(solution)/shard_map/pallas_call | solution.py:176
  66.8 6.1 %all-to-all-start.2 = ((bf16[16,72,128]{2,1,0:T(8,128)(2,1)}), bf16[16,72,128]{2,1,0:T(8,128)(2,1)S(1)}, u32[]{:S(2)}, u32[]{:S(2)}) async-start(bf16[16,72,128]{2,1,0:T(8,128)(2,1)} %shard_map.109), calls=%async_computation.2 | async-start | bytes 589824 | tf_op jit(solution)/shard_map/all_to_all | solution.py:113
  73.0 0.7 pad_add_fusion.where
  73.6 4.5 %shard_map.103.kept = bf16[4,128,1024]{2,1,0:T(8,128)(2,1)} custom-call(s32[2]{0:T(128)} %pad_add_fusion.where, bf16[128,128]{1,0:T(8,128)(2,1)} %c.5, bf16[8192,128]{1,0:T(8,128)(2,1)} %w.3), custom_call_target="tpu_custom_call" | custom-call | flops 1000000000 | tf_op jit(solution)/shard_map/pallas_call | solution.py:128
  78.1 0.0 collective-permute-done.came
  78.1 0.0 copy-start.2
  78.1 1.0 copy-done.2
  79.1 2.6 %shard_map.105 = (bf16[128,1024]{1,0:T(8,128)(2,1)}, bf16[128,1024]{1,0:T(8,128)(2,1)}, bf16[128,1024]{1,0:T(8,128)(2,1)}, bf16[128,1024]{1,0:T(8,128)(2,1)}) custom-call(bf16[4,128,1024]{2,1,0:T(8,128)(2,1)} %shard_map.103.kept, bf16[4,128,1024]{2,1,0:T(8,128)(2,1)} %copy-done.2), custom_call_target="tpu_custom_call" | custom-call | flops 100000000 | tf_op jit(solution)/shard_map/pallas_call | solution.py:172
  81.6 3.0 %collective-permute-start.1 = (bf16[128,1024]{1,0:T(8,128)(2,1)}, bf16[128,1024]{1,0:T(8,128)(2,1)S(1)}, u32[]{:S(2)}, u32[]{:S(2)}) collective-permute-start(bf16[128,1024]{1,0:T(8,128)(2,1)} %get-tuple-element.15), channel_id=1, source_target_pairs={{0,2},{1,3},{2,4},{3,5},{4,6},{5,7},{6,0},{7,1},{8,10},{9,11},{10,... | collective-permute-start | bytes 786440 | tf_op jit(solution)/shard_map/ppermute | solution.py:118
  84.7 4.6 %collective-permute-start.2 = (bf16[128,1024]{1,0:T(8,128)(2,1)}, bf16[128,1024]{1,0:T(8,128)(2,1)S(1)}, u32[]{:S(2)}, u32[]{:S(2)}) collective-permute-start(bf16[128,1024]{1,0:T(8,128)(2,1)} %get-tuple-element.16), channel_id=1, source_target_pairs={{0,4},{1,5},{2,6},{3,7},{4,0},{5,1},{6,2},{7,3},{8,12},{9,13},{10,... | collective-permute-start | bytes 786440 | tf_op jit(solution)/shard_map/ppermute | solution.py:118
  89.3 3.3 %collective-permute-start.3 = (bf16[128,1024]{1,0:T(8,128)(2,1)}, bf16[128,1024]{1,0:T(8,128)(2,1)S(1)}, u32[]{:S(2)}, u32[]{:S(2)}) collective-permute-start(bf16[128,1024]{1,0:T(8,128)(2,1)} %get-tuple-element.17), channel_id=1, source_target_pairs={{0,6},{1,7},{2,0},{3,1},{4,2},{5,3},{6,4},{7,5},{8,14},{9,15},{10,... | collective-permute-start | bytes 786440 | tf_op jit(solution)/shard_map/ppermute | solution.py:118
  92.7 0.0 all-to-all-done.2.g0
  92.7 0.0 copy-start.1
  92.7 2.1 %collective-permute-start.7 = (bf16[16,72,128]{2,1,0:T(8,128)(2,1)S(1)}, bf16[16,72,128]{2,1,0:T(8,128)(2,1)S(1)}, u32[]{:S(2)}, u32[]{:S(2)}) collective-permute-start(bf16[16,72,128]{2,1,0:T(8,128)(2,1)S(1)} %all-to-all-done.2.g0), channel_id=1, source_target_pairs={{0,8},{8,16},{16,24},{24,0},{1,9},{9,17},{17,25},{25,1},{2,10},{10... | collective-permute-start | bytes 884744 | tf_op jit(solution)/shard_map/ppermute | solution.py:118
  94.8 4.0 %collective-permute-start.8 = (bf16[16,72,128]{2,1,0:T(8,128)(2,1)S(1)}, bf16[16,72,128]{2,1,0:T(8,128)(2,1)S(1)}, u32[]{:S(2)}, u32[]{:S(2)}) collective-permute-start(bf16[16,72,128]{2,1,0:T(8,128)(2,1)S(1)} %all-to-all-done.2.g0), channel_id=1, source_target_pairs={{0,16},{8,24},{16,0},{24,8},{1,17},{9,25},{17,1},{25,9},{2,18},{10... | collective-permute-start | bytes 884744 | tf_op jit(solution)/shard_map/ppermute | solution.py:118
  98.8 0.0 collective-permute-done.1.f1
  98.8 0.0 copy-start.7
  98.8 3.9 %collective-permute-start.9 = (bf16[16,72,128]{2,1,0:T(8,128)(2,1)S(1)}, bf16[16,72,128]{2,1,0:T(8,128)(2,1)S(1)}, u32[]{:S(2)}, u32[]{:S(2)}) collective-permute-start(bf16[16,72,128]{2,1,0:T(8,128)(2,1)S(1)} %all-to-all-done.2.g0), channel_id=1, source_target_pairs={{0,24},{8,0},{16,8},{24,16},{1,25},{9,1},{17,9},{25,17},{2,26},{10... | collective-permute-start | bytes 884744 | tf_op jit(solution)/shard_map/ppermute | solution.py:118
  102.7 0.0 collective-permute-done.2.f2
  102.7 0.0 copy-start.8
  102.8 0.0 collective-permute-done.3.f3
  102.8 0.0 copy-start.9
  102.8 0.0 copy-done.7
  102.8 0.7 copy-done.8
  103.4 0.1 copy-done.9
  103.5 2.6 %shard_map.108 = bf16[128,1024]{1,0:T(8,128)(2,1)} custom-call(bf16[128,1024]{1,0:T(8,128)(2,1)} %get-tuple-element.14.f0, bf16[128,1024]{1,0:T(8,128)(2,1)} %copy-done.7, bf16[128,1024]{1,0:T(8,128)(2,1)} %copy-done.8, bf16[128,1024]{1,0:T(8,128)(2,1)} %copy-done.9, bf16[32,128]{1,0:T(8,128)(2,1)} %get-tuple-element.20.low, ...), custom_call_target="tpu_custom_call" | custom-call | flops 1000000000 | tf_op jit(solution)/shard_map/pallas_call | solution.py:178
  106.2 0.0 collective-permute-done.7.g1
  106.2 0.0 copy-start.4
  106.2 1.9 %collective-permute-done.8.g2 = bf16[16,72,128]{2,1,0:T(8,128)(2,1)S(1)} collective-permute-done((bf16[16,72,128]{2,1,0:T(8,128)(2,1)S(1)}, bf16[16,72,128]{2,1,0:T(8,128)(2,1)S(1)}, u32[]{:S(2)}, u32[]{:S(2)}) %collective-permute-start.8) | collective-permute-done | bytes 294944 | tf_op jit(solution)/shard_map/ppermute | solution.py:118
  108.1 0.0 copy-start.5
  108.1 3.8 %collective-permute-done.9.g3 = bf16[16,72,128]{2,1,0:T(8,128)(2,1)S(1)} collective-permute-done((bf16[16,72,128]{2,1,0:T(8,128)(2,1)S(1)}, bf16[16,72,128]{2,1,0:T(8,128)(2,1)S(1)}, u32[]{:S(2)}, u32[]{:S(2)}) %collective-permute-start.9) | collective-permute-done | bytes 294944 | tf_op jit(solution)/shard_map/ppermute | solution.py:118
  111.9 0.0 copy-done.1
  111.9 0.0 copy-done.4
  111.9 0.0 copy-done.5
  111.9 0.0 copy-start.6
  111.9 0.7 copy-done.6
  112.6 2.6 %shard_map.110 = (bf16[512,1024]{1,0:T(8,128)(2,1)}, bf16[512,128]{1,0:T(8,128)(2,1)}) custom-call(s32[1]{0:T(128)} %bitcast.3.me, bf16[16,72,128]{2,1,0:T(8,128)(2,1)} %copy-done.1, bf16[16,72,128]{2,1,0:T(8,128)(2,1)} %copy-done.4, bf16[16,72,128]{2,1,0:T(8,128)(2,1)} %copy-done.5, bf16[16,72,128]{2,1,0:T(8,128)(2,1)} %copy-done.6), custom_call_target="tpu_custom_call" | custom-call | tf_op jit(solution)/shard_map/pallas_call | solution.py:182
Async XLA Ops:
  3.6 25.0 %all-to-all-start = ((f32[32,32,128]{2,1,0:T(8,128)}), f32[32,32,128]{2,1,0:T(8,128)S(1)}, u32[]{:S(2)}, u32[]{:S(2)}) async-start(f32[32,32,128]{2,1,0:T(8,128)} %get-tuple-element.18), calls=%async_computation | async-start | bytes 1048576 | tf_op jit(solution)/shard_map/all_to_all | solution.py:113
  14.7 10.5 %collective-permute-start.4 = (bf16[136,384]{1,0:T(8,128)(2,1)S(1)}, bf16[136,384]{1,0:T(8,128)(2,1)S(1)}, u32[]{:S(2)}, u32[]{:S(2)}) collective-permute-start(bf16[136,384]{1,0:T(8,128)(2,1)S(1)} %get-tuple-element.27), channel_id=1, source_target_pairs={{0,8},{8,16},{16,24},{24,0},{1,9},{9,17},{17,25},{25,1},{2,10},{10... | collective-permute-start | bytes 313352 | tf_op jit(solution)/shard_map/ppermute | solution.py:118
  18.1 8.6 %collective-permute-start.5 = (bf16[136,384]{1,0:T(8,128)(2,1)S(1)}, bf16[136,384]{1,0:T(8,128)(2,1)S(1)}, u32[]{:S(2)}, u32[]{:S(2)}) collective-permute-start(bf16[136,384]{1,0:T(8,128)(2,1)S(1)} %get-tuple-element.26), channel_id=1, source_target_pairs={{0,16},{8,24},{16,0},{24,8},{1,17},{9,25},{17,1},{25,9},{2,18},{10... | collective-permute-start | bytes 313352 | tf_op jit(solution)/shard_map/ppermute | solution.py:118
  20.9 7.7 %collective-permute-start.6 = (bf16[136,384]{1,0:T(8,128)(2,1)S(1)}, bf16[136,384]{1,0:T(8,128)(2,1)S(1)}, u32[]{:S(2)}, u32[]{:S(2)}) collective-permute-start(bf16[136,384]{1,0:T(8,128)(2,1)S(1)} %get-tuple-element.25), channel_id=1, source_target_pairs={{0,24},{8,0},{16,8},{24,16},{1,25},{9,1},{17,9},{25,17},{2,26},{10... | collective-permute-start | bytes 313352 | tf_op jit(solution)/shard_map/ppermute | solution.py:118
  25.2 3.3 %copy-start.10 = (bf16[136,384]{1,0:T(8,128)(2,1)}, bf16[136,384]{1,0:T(8,128)(2,1)S(1)}, u32[]{:S(2)}) copy-start(bf16[136,384]{1,0:T(8,128)(2,1)S(1)} %collective-permute-done.4.p1) | copy-start | bytes 313348
  26.7 1.8 %copy-start.11 = (bf16[136,384]{1,0:T(8,128)(2,1)}, bf16[136,384]{1,0:T(8,128)(2,1)S(1)}, u32[]{:S(2)}) copy-start(bf16[136,384]{1,0:T(8,128)(2,1)S(1)} %collective-permute-done.5.p2) | copy-start | bytes 313348
  28.5 0.6 copy-start.12
  28.5 0.8 copy-start.3
  31.6 32.8 %all-to-all-start.1 = ((bf16[16,72,128]{2,1,0:T(8,128)(2,1)}), bf16[16,72,128]{2,1,0:T(8,128)(2,1)S(1)}, u32[]{:S(2)}, u32[]{:S(2)}) async-start(bf16[16,72,128]{2,1,0:T(8,128)(2,1)} %get-tuple-element.22), calls=%async_computation.1 | async-start | bytes 589824 | tf_op jit(solution)/shard_map/all_to_all | solution.py:113
  50.0 28.0 %collective-permute-start = (bf16[4,128,1024]{2,1,0:T(8,128)(2,1)}, bf16[4,128,1024]{2,1,0:T(8,128)(2,1)S(1)}, u32[]{:S(2)}, u32[]{:S(2)}) collective-permute-start(bf16[4,128,1024]{2,1,0:T(8,128)(2,1)} %shard_map.104), channel_id=1, source_target_pairs={{0,1},{1,0},{2,3},{3,2},{4,5},{5,4},{6,7},{7,6},{8,9},{9,8},{10,11... | collective-permute-start | bytes 3145736 | tf_op jit(solution)/shard_map/ppermute | solution.py:170
  64.4 0.7 copy-start
  66.8 25.8 %all-to-all-start.2 = ((bf16[16,72,128]{2,1,0:T(8,128)(2,1)}), bf16[16,72,128]{2,1,0:T(8,128)(2,1)S(1)}, u32[]{:S(2)}, u32[]{:S(2)}) async-start(bf16[16,72,128]{2,1,0:T(8,128)(2,1)} %shard_map.109), calls=%async_computation.2 | async-start | bytes 589824 | tf_op jit(solution)/shard_map/all_to_all | solution.py:113
  78.1 1.0 copy-start.2
  81.6 17.2 %collective-permute-start.1 = (bf16[128,1024]{1,0:T(8,128)(2,1)}, bf16[128,1024]{1,0:T(8,128)(2,1)S(1)}, u32[]{:S(2)}, u32[]{:S(2)}) collective-permute-start(bf16[128,1024]{1,0:T(8,128)(2,1)} %get-tuple-element.15), channel_id=1, source_target_pairs={{0,2},{1,3},{2,4},{3,5},{4,6},{5,7},{6,0},{7,1},{8,10},{9,11},{10,... | collective-permute-start | bytes 786440 | tf_op jit(solution)/shard_map/ppermute | solution.py:118
  84.7 18.1 %collective-permute-start.2 = (bf16[128,1024]{1,0:T(8,128)(2,1)}, bf16[128,1024]{1,0:T(8,128)(2,1)S(1)}, u32[]{:S(2)}, u32[]{:S(2)}) collective-permute-start(bf16[128,1024]{1,0:T(8,128)(2,1)} %get-tuple-element.16), channel_id=1, source_target_pairs={{0,4},{1,5},{2,6},{3,7},{4,0},{5,1},{6,2},{7,3},{8,12},{9,13},{10,... | collective-permute-start | bytes 786440 | tf_op jit(solution)/shard_map/ppermute | solution.py:118
  89.3 13.5 %collective-permute-start.3 = (bf16[128,1024]{1,0:T(8,128)(2,1)}, bf16[128,1024]{1,0:T(8,128)(2,1)S(1)}, u32[]{:S(2)}, u32[]{:S(2)}) collective-permute-start(bf16[128,1024]{1,0:T(8,128)(2,1)} %get-tuple-element.17), channel_id=1, source_target_pairs={{0,6},{1,7},{2,0},{3,1},{4,2},{5,3},{6,4},{7,5},{8,14},{9,15},{10,... | collective-permute-start | bytes 786440 | tf_op jit(solution)/shard_map/ppermute | solution.py:118
  92.7 19.2 %copy-start.1 = (bf16[16,72,128]{2,1,0:T(8,128)(2,1)}, bf16[16,72,128]{2,1,0:T(8,128)(2,1)S(1)}, u32[]{:S(2)}) copy-start(bf16[16,72,128]{2,1,0:T(8,128)(2,1)S(1)} %all-to-all-done.2.g0) | copy-start | bytes 884740
  92.7 13.5 %collective-permute-start.7 = (bf16[16,72,128]{2,1,0:T(8,128)(2,1)S(1)}, bf16[16,72,128]{2,1,0:T(8,128)(2,1)S(1)}, u32[]{:S(2)}, u32[]{:S(2)}) collective-permute-start(bf16[16,72,128]{2,1,0:T(8,128)(2,1)S(1)} %all-to-all-done.2.g0), channel_id=1, source_target_pairs={{0,8},{8,16},{16,24},{24,0},{1,9},{9,17},{17,25},{25,1},{2,10},{10... | collective-permute-start | bytes 884744 | tf_op jit(solution)/shard_map/ppermute | solution.py:118
  94.8 13.3 %collective-permute-start.8 = (bf16[16,72,128]{2,1,0:T(8,128)(2,1)S(1)}, bf16[16,72,128]{2,1,0:T(8,128)(2,1)S(1)}, u32[]{:S(2)}, u32[]{:S(2)}) collective-permute-start(bf16[16,72,128]{2,1,0:T(8,128)(2,1)S(1)} %all-to-all-done.2.g0), channel_id=1, source_target_pairs={{0,16},{8,24},{16,0},{24,8},{1,17},{9,25},{17,1},{25,9},{2,18},{10... | collective-permute-start | bytes 884744 | tf_op jit(solution)/shard_map/ppermute | solution.py:118
  98.8 3.9 %copy-start.7 = (bf16[128,1024]{1,0:T(8,128)(2,1)}, bf16[128,1024]{1,0:T(8,128)(2,1)S(1)}, u32[]{:S(2)}) copy-start(bf16[128,1024]{1,0:T(8,128)(2,1)S(1)} %collective-permute-done.1.f1) | copy-start | bytes 786436
  98.8 13.0 %collective-permute-start.9 = (bf16[16,72,128]{2,1,0:T(8,128)(2,1)S(1)}, bf16[16,72,128]{2,1,0:T(8,128)(2,1)S(1)}, u32[]{:S(2)}, u32[]{:S(2)}) collective-permute-start(bf16[16,72,128]{2,1,0:T(8,128)(2,1)S(1)} %all-to-all-done.2.g0), channel_id=1, source_target_pairs={{0,24},{8,0},{16,8},{24,16},{1,25},{9,1},{17,9},{25,17},{2,26},{10... | collective-permute-start | bytes 884744 | tf_op jit(solution)/shard_map/ppermute | solution.py:118
  102.7 0.7 copy-start.8
  102.8 0.8 copy-start.9
  106.2 5.7 %copy-start.4 = (bf16[16,72,128]{2,1,0:T(8,128)(2,1)}, bf16[16,72,128]{2,1,0:T(8,128)(2,1)S(1)}, u32[]{:S(2)}) copy-start(bf16[16,72,128]{2,1,0:T(8,128)(2,1)S(1)} %collective-permute-done.7.g1) | copy-start | bytes 884740
  108.1 3.8 %copy-start.5 = (bf16[16,72,128]{2,1,0:T(8,128)(2,1)}, bf16[16,72,128]{2,1,0:T(8,128)(2,1)S(1)}, u32[]{:S(2)}) copy-start(bf16[16,72,128]{2,1,0:T(8,128)(2,1)S(1)} %collective-permute-done.8.g2) | copy-start | bytes 884740
  111.9 0.7 copy-start.6

commit v3 on v2

--- a/solution.py
+++ b/solution.py
@@ -14,9 +14,13 @@
 NT = (((1,), (1,)), ((), ()))
 
 
+GRANT = pltpu.CompilerParams(vmem_limit_bytes=12 << 20)
+
+
 def call(body, outs, flops=0, **kw):
     return pl.pallas_call(
         body,
+        compiler_params=GRANT,
         out_shape=[jax.ShapeDtypeStruct(s, d) for s, d in outs],
         cost_estimate=pl.CostEstimate(flops=flops, bytes_accessed=0, transcendentals=0),
         **kw,
@@ -28,7 +32,7 @@
     return jnp.where(at == slot, jnp.concatenate([low] * slots, axis=0), 0.0)
 
 
-def partial_kernel(x, c, down, up, doc, tenant, index, me, pack, part, slot_out):
+def partial_kernel(x, c, down, up, doc, tenant, index, me, part, slot_out, *packs):
     n = x.shape[0]
     tenant_of = (lax.broadcasted_iota(jnp.int32, (SLOTS, tenant.shape[1]), 0) == tenant[...]).astype(bf16)
     table = jnp.broadcast_to(index[...].astype(f32), (8, SLOTS)).astype(bf16)
@@ -45,17 +49,18 @@
     for i in range(Y * T):
         part[i] = both
     fx = x.shape[1] // Y
-    slots = jnp.concatenate([slot, jnp.zeros((8, pack.shape[2] - n), f32)], axis=1)
-    for y in range(Y):
-        mine = jnp.concatenate([x[:, y * fx : (y + 1) * fx], c[...]], axis=1)
-        pack[(y - me[0]) & (Y - 1)] = jnp.concatenate([mine.astype(f32), slots], axis=0).astype(bf16)
+    slots = jnp.concatenate([slot, jnp.zeros((8, fx + c.shape[1] - n), f32)], axis=1)
+    for k, pack in enumerate(packs):
+        at = pl.multiple_of((me[0] ^ k) * fx, fx)
+        mine = jnp.concatenate([x[:, pl.ds(at, fx)], c[...]], axis=1)
+        pack[...] = jnp.concatenate([mine.astype(f32), slots], axis=0).astype(bf16)
 
 
 def gradient_kernel(me, parts, p0, p1, p2, p3, out, low_out):
     fx = p0.shape[1] - 128
     gs, hs = [], []
     for k, pack in enumerate((p0, p1, p2, p3)):
-        at = (me[0] - k) & (Y - 1)
+        at = me[0] ^ k
         both = parts[at * T]
         for j in range(1, T):
             both = both + parts[at * T + j]
@@ -85,7 +90,7 @@
 def layout_kernel(me, g0, g1, g2, g3, down, up):
     rd = ROWS // Z
     for k, g in enumerate((g0, g1, g2, g3)):
-        at = (me[0] - k) & (Y - 1)
+        at = me[0] ^ k
         v = g[...].astype(f32)
         down[:, pl.ds(pl.multiple_of(at * 256, 256), 128)] = v[:, :rd].reshape(ROWS, 128).astype(bf16)
         down[:, pl.ds(pl.multiple_of(at * 256 + 128, 128), 128)] = v[:, rd : 2 * rd].reshape(ROWS, 128).astype(bf16)
@@ -113,9 +118,8 @@
     return lax.all_to_all(value, axis, 0, 0, tiled=True)
 
 
-def shift(value, axis, by):
-    size = lax.axis_size(axis)
-    return lax.ppermute(value, axis, [(i, (i + by) % size) for i in range(size)])
+def trade(value, axis, k):
+    return lax.ppermute(value, axis, [(i, i ^ k) for i in range(lax.axis_size(axis))])
 
 
 def specs(count):
@@ -127,12 +131,13 @@
     fx = w.shape[0] // T
     return pl.pallas_call(
         frozen_kernel,
+        compiler_params=GRANT,
         grid_spec=pltpu.PrefetchScalarGridSpec(
             num_scalar_prefetch=1,
             grid=(4,),
             in_specs=[
                 pl.BlockSpec((n, fc), lambda i, p: (0, 0)),
-                pl.BlockSpec((fx, fc), lambda i, p: (((p[0] + i) & 3) * 2 + p[1], 0)),
+                pl.BlockSpec((fx, fc), lambda i, p: ((p[0] ^ i) * 2 + p[1], 0)),
             ],
             out_specs=pl.BlockSpec((1, n, fx), lambda i, p: (i, 0, 0)),
         ),
@@ -149,16 +154,15 @@
     down_rows = jnp.transpose(down, (0, 2, 1)).reshape(ROWS, fx)
     up_rows = up.reshape(ROWS, fc)
     block = (ROWS // Z * 2 + ROWS // Y // Z, 128)
-    pack, part, slot = call(
+    part, slot, *packs = call(
         partial_kernel,
-        [((Y, n + 8, fx // Y + fc), bf16), ((Y * T, 2 * RANK, n), f32), ((8, n), f32)],
+        [((Y * T, 2 * RANK, n), f32), ((8, n), f32)] + [((n + 8, fx // Y + fc), bf16)] * Y,
         flops=10**9,
         in_specs=[pl.BlockSpec(memory_space=pltpu.VMEM)] * 7 + [pl.BlockSpec(memory_space=pltpu.SMEM)],
     )(x, c, down_rows, up_rows, doc[None], tenant[None], index[None], me)
     parts = swap(part, ("y", "tensor"))
-    packs = [pack[0]]
     for k in (1, 2, 3):
-        packs.append(shift(pack[k], "y", k))
+        packs[k] = trade(packs[k], "y", k)
     piece, low = call(
         gradient_kernel,
         [((Z, *block), bf16), ((2 * RANK, n), bf16)],
@@ -166,19 +170,19 @@
         in_specs=specs(5),
     )(me, parts, *packs)
     sums = swap(piece, "z")
-    send = frozen_blocks(c, w, jnp.stack([at // 2, 1 - at % 2]))
-    came = lax.ppermute(send, "tensor", [(j, j ^ 1) for j in range(T)])
-    kept = frozen_blocks(c, w, jnp.stack([at // 2, at % 2]))
+    send = frozen_blocks(c, w, jnp.stack([at >> 1, (at & 1) ^ 1]))
+    came = trade(send, "tensor", 1)
+    kept = frozen_blocks(c, w, jnp.stack([at >> 1, at & 1]))
     pairs = call(pair_kernel, [((n, fx), bf16)] * 4, flops=10**8)(kept, came)
     frozens = [pairs[0]]
     for k in (1, 2, 3):
-        frozens.append(shift(pairs[k], "tensor", 2 * k))
+        frozens.append(trade(pairs[k], "tensor", 2 * k))
     (done,) = call(finish_kernel, [((Z, *block), bf16)], flops=10**8)(sums)
     rows = swap(done, "z")
     (input_gradient,) = call(input_kernel, [((n, fx), bf16)], flops=10**9)(*frozens, low, slot, down_rows)
     outs = [rows]
     for k in (1, 2, 3):
-        outs.append(shift(rows, "y", k))
+        outs.append(trade(rows, "y", k))
     whole, up_whole = call(layout_kernel, [((ROWS, fx), bf16), ((ROWS, fc), bf16)], in_specs=specs(4))(me, *outs)
     down_gradient = jnp.transpose(whole.reshape(SLOTS, RANK, fx), (0, 2, 1))
     up_gradient = up_whole.reshape(SLOTS, RANK, fc)

time: 116 us -> 118 us (1.017)
  the two profiles are of different devices: /device:TPU:8 before, /device:TPU:34 now
where the time goes in v3:
time: 118 us; the launch traced here: 117 us
  starting transfers between devices  61.5 us (52%)
  waiting for transfers between devices  38.6 us (33%)
  Pallas kernels  10.1 us (9%)
  local copies, waits for them, and re-layouts  5.81 us (5%)
    ppermute x10, starting transfers between devices, trade(): lax.ppermute(value, axis, [(i, i ^ k) for i in range(lax.axis_size(axis))])  32.1 us
    all_to_all x3, starting transfers between devices, swap(): return lax.all_to_all(value, axis, 0, 0, tiled=True)  29.5 us
    all_to_all x3, waiting for transfers between devices, swap(): return lax.all_to_all(value, axis, 0, 0, tiled=True)  21.4 us
    ppermute x10, waiting for transfers between devices, trade(): lax.ppermute(value, axis, [(i, i ^ k) for i in range(lax.axis_size(axis))])  17.2 us
    unnamed x20, local copies, waits for them, and re-layouts  5.81 us
    pallas_call x2, Pallas kernels, frozen_blocks(): pl.pallas_call(frozen_kernel, compiler_params=GRANT, grid_spec=pltpu.Pref...  4.2 us
  transfers between devices with their start and end apart: 13, of which 7 were waited for; matrix products, arithmetic and copies ran while one was open for 0% of the time, Pallas kernels for 5%

profile of v3, /device:TPU:34, one launch (start us, length us, event | category | flops | bytes accessed | tf_op | source)
XLA Modules:
  0.0 117.0 jit_solution(7006692946060018820)
XLA Ops:
  0.6 0.0 copy-start.1
  0.6 1.2 %copy-done.1 = bf16[32,1024,16]{1,2,0:T(8,128)(2,1)S(1)} copy-done((bf16[32,1024,16]{1,2,0:T(8,128)(2,1)S(1)}, bf16[32,1024,16]{1,2,0:T(8,128)(2,1)}, u32[]{:S(2)}) %copy-start.1) | copy-done | bytes 1048600
  1.9 0.0 copy-start.3
  1.9 0.9 copy-done.3
  2.8 0.0 copy-start.4
  2.8 0.9 copy-done.4
  3.7 0.0 copy-start.5
  3.7 0.8 copy-done.5
  4.5 0.0 copy-start.7
  4.5 0.7 copy-done.7
  5.1 0.0 copy-start.8
  5.1 0.7 copy-done.8
  5.8 0.0 copy-start.9
  5.8 0.7 copy-done.9
  6.4 1.4 %shard_map.106 = (f32[32,32,128]{2,1,0:T(8,128)}, f32[8,128]{1,0:T(8,128)S(1)}, bf16[136,384]{1,0:T(8,128)(2,1)S(1)}, bf16[136,384]{1,0:T(8,128)(2,1)S(1)}, bf16...) custom-call(bf16[128,1024]{1,0:T(8,128)(2,1)S(1)} %copy-done.3, bf16[128,128]{1,0:T(8,128)(2,1)S(1)} %copy-done.5, ...), custom_call_target="tpu_custom_call" | custom-call | flops 1000000000 | tf_op jit(solution)/shard_map/pallas_call | solution.py:157
  7.9 7.6 %all-to-all-start = ((f32[32,32,128]{2,1,0:T(8,128)}), f32[32,32,128]{2,1,0:T(8,128)S(1)}, u32[]{:S(2)}, u32[]{:S(2)}) async-start(f32[32,32,128]{2,1,0:T(8,128)} %get-tuple-element.21), calls=%async_computation | async-start | bytes 1048576 | tf_op jit(solution)/shard_map/all_to_all | solution.py:118
  15.5 3.4 %collective-permute-start.4 = (bf16[136,384]{1,0:T(8,128)(2,1)S(1)}, bf16[136,384]{1,0:T(8,128)(2,1)S(1)}, u32[]{:S(2)}, u32[]{:S(2)}) collective-permute-start(bf16[136,384]{1,0:T(8,128)(2,1)S(1)} %get-tuple-element.23), channel_id=1, source_target_pairs={{0,8},{8,0},{16,24},{24,16},{1,9},{9,1},{17,25},{25,17},{2,10},{10... | collective-permute-start | bytes 313352 | tf_op jit(solution)/shard_map/ppermute | solution.py:122
  18.9 4.6 %collective-permute-start.5 = (bf16[136,384]{1,0:T(8,128)(2,1)S(1)}, bf16[136,384]{1,0:T(8,128)(2,1)S(1)}, u32[]{:S(2)}, u32[]{:S(2)}) collective-permute-start(bf16[136,384]{1,0:T(8,128)(2,1)S(1)} %get-tuple-element.24), channel_id=1, source_target_pairs={{0,16},{8,24},{16,0},{24,8},{1,17},{9,25},{17,1},{25,9},{2,18},{10... | collective-permute-start | bytes 313352 | tf_op jit(solution)/shard_map/ppermute | solution.py:122
  23.5 2.4 %collective-permute-start.6 = (bf16[136,384]{1,0:T(8,128)(2,1)S(1)}, bf16[136,384]{1,0:T(8,128)(2,1)S(1)}, u32[]{:S(2)}, u32[]{:S(2)}) collective-permute-start(bf16[136,384]{1,0:T(8,128)(2,1)S(1)} %get-tuple-element.25), channel_id=1, source_target_pairs={{0,24},{8,16},{16,8},{24,0},{1,25},{9,17},{17,9},{25,1},{2,26},{10... | collective-permute-start | bytes 313352 | tf_op jit(solution)/shard_map/ppermute | solution.py:122
  25.9 0.0 collective-permute-done.4.p1
  25.9 3.7 %collective-permute-done.5.p2 = bf16[136,384]{1,0:T(8,128)(2,1)S(1)} collective-permute-done((bf16[136,384]{1,0:T(8,128)(2,1)S(1)}, bf16[136,384]{1,0:T(8,128)(2,1)S(1)}, u32[]{:S(2)}, u32[]{:S(2)}) %collective-permute-start.5) | collective-permute-done | bytes 104480 | tf_op jit(solution)/shard_map/ppermute | solution.py:122
  29.6 2.2 %collective-permute-done.6.p3 = bf16[136,384]{1,0:T(8,128)(2,1)S(1)} collective-permute-done((bf16[136,384]{1,0:T(8,128)(2,1)S(1)}, bf16[136,384]{1,0:T(8,128)(2,1)S(1)}, u32[]{:S(2)}, u32[]{:S(2)}) %collective-permute-start.6) | collective-permute-done | bytes 104480 | tf_op jit(solution)/shard_map/ppermute | solution.py:122
  31.9 0.0 all-to-all-done.parts
  31.9 0.0 copy-start
  31.9 0.0 copy-start.6
  31.9 1.1 shard_map.107
  32.9 15.2 %all-to-all-start.1 = ((bf16[16,72,128]{2,1,0:T(8,128)(2,1)}), bf16[16,72,128]{2,1,0:T(8,128)(2,1)S(1)}, u32[]{:S(2)}, u32[]{:S(2)}) async-start(bf16[16,72,128]{2,1,0:T(8,128)(2,1)} %get-tuple-element.28), calls=%async_computation.1 | async-start | bytes 589824 | tf_op jit(solution)/shard_map/all_to_all | solution.py:118
  48.1 0.1 pad_add_fusion.1.where
  48.2 0.0 copy-done
  48.2 0.0 copy-done.6
  48.2 2.7 %shard_map.104 = bf16[4,128,1024]{2,1,0:T(8,128)(2,1)} custom-call(s32[2]{0:T(128)S(1)} %pad_add_fusion.1.where, bf16[128,128]{1,0:T(8,128)(2,1)S(1)} %copy-done.6, bf16[8192,128]{1,0:T(8,128)(2,1)S(1)} %copy-done), custom_call_target="tpu_custom_call" | custom-call | flops 1000000000 | tf_op jit(solution)/shard_map/pallas_call | solution.py:132
  50.9 1.9 %collective-permute-start = (bf16[4,128,1024]{2,1,0:T(8,128)(2,1)}, bf16[4,128,1024]{2,1,0:T(8,128)(2,1)S(1)}, u32[]{:S(2)}, u32[]{:S(2)}) collective-permute-start(bf16[4,128,1024]{2,1,0:T(8,128)(2,1)} %shard_map.104), channel_id=1, source_target_pairs={{0,1},{1,0},{2,3},{3,2},{4,5},{5,4},{6,7},{7,6},{8,9},{9,8},{10,11... | collective-permute-start | bytes 3145736 | tf_op jit(solution)/shard_map/ppermute | solution.py:122
  52.8 14.0 %all-to-all-done.1.parts = bf16[16,72,128]{2,1,0:T(8,128)(2,1)S(1)} async-done(((bf16[16,72,128]{2,1,0:T(8,128)(2,1)}), bf16[16,72,128]{2,1,0:T(8,128)(2,1)S(1)}, u32[]{:S(2)}, u32[]{:S(2)}) %all-to-all-start.1) | async-done | bytes 294944 | tf_op jit(solution)/shard_map/all_to_all | solution.py:118
  66.8 0.8 shard_map.109
  67.6 6.6 %all-to-all-start.2 = ((bf16[16,72,128]{2,1,0:T(8,128)(2,1)}), bf16[16,72,128]{2,1,0:T(8,128)(2,1)S(1)}, u32[]{:S(2)}, u32[]{:S(2)}) async-start(bf16[16,72,128]{2,1,0:T(8,128)(2,1)} %shard_map.109), calls=%async_computation.2 | async-start | bytes 589824 | tf_op jit(solution)/shard_map/all_to_all | solution.py:118
  74.2 0.1 pad_add_fusion.where
  74.3 1.5 %shard_map.103.kept = bf16[4,128,1024]{2,1,0:T(8,128)(2,1)S(1)} custom-call(s32[2]{0:T(128)S(1)} %pad_add_fusion.where, bf16[128,128]{1,0:T(8,128)(2,1)S(1)} %copy-done.6, bf16[8192,128]{1,0:T(8,128)(2,1)S(1)} %copy-done), custom_call_target="tpu_custom_call" | custom-call | flops 1000000000 | tf_op jit(solution)/shard_map/pallas_call | solution.py:132
  75.8 0.0 copy-start.2
  75.8 0.0 collective-permute-done.came
  75.8 0.2 shard_map.105
  76.1 3.1 %collective-permute-start.1 = (bf16[128,1024]{1,0:T(8,128)(2,1)S(1)}, bf16[128,1024]{1,0:T(8,128)(2,1)S(1)}, u32[]{:S(2)}, u32[]{:S(2)}) collective-permute-start(bf16[128,1024]{1,0:T(8,128)(2,1)S(1)} %get-tuple-element.18), channel_id=1, source_target_pairs={{0,2},{1,3},{2,0},{3,1},{4,6},{5,7},{6,4},{7,5},{8,10},{9,11},{10,... | collective-permute-start | bytes 786440 | tf_op jit(solution)/shard_map/ppermute | solution.py:122
  79.1 3.8 %collective-permute-start.2 = (bf16[128,1024]{1,0:T(8,128)(2,1)S(1)}, bf16[128,1024]{1,0:T(8,128)(2,1)S(1)}, u32[]{:S(2)}, u32[]{:S(2)}) collective-permute-start(bf16[128,1024]{1,0:T(8,128)(2,1)S(1)} %get-tuple-element.19), channel_id=1, source_target_pairs={{0,4},{1,5},{2,6},{3,7},{4,0},{5,1},{6,2},{7,3},{8,12},{9,13},{10,... | collective-permute-start | bytes 786440 | tf_op jit(solution)/shard_map/ppermute | solution.py:122
  82.9 2.5 %collective-permute-start.3 = (bf16[128,1024]{1,0:T(8,128)(2,1)S(1)}, bf16[128,1024]{1,0:T(8,128)(2,1)S(1)}, u32[]{:S(2)}, u32[]{:S(2)}) collective-permute-start(bf16[128,1024]{1,0:T(8,128)(2,1)S(1)} %get-tuple-element.20), channel_id=1, source_target_pairs={{0,6},{1,7},{2,4},{3,5},{4,2},{5,3},{6,0},{7,1},{8,14},{9,15},{10,... | collective-permute-start | bytes 786440 | tf_op jit(solution)/shard_map/ppermute | solution.py:122
  85.4 7.4 %all-to-all-done.2.g0 = bf16[16,72,128]{2,1,0:T(8,128)(2,1)S(1)} async-done(((bf16[16,72,128]{2,1,0:T(8,128)(2,1)}), bf16[16,72,128]{2,1,0:T(8,128)(2,1)S(1)}, u32[]{:S(2)}, u32[]{:S(2)}) %all-to-all-start.2) | async-done | bytes 294944 | tf_op jit(solution)/shard_map/all_to_all | solution.py:118
  92.8 2.4 %collective-permute-start.7 = (bf16[16,72,128]{2,1,0:T(8,128)(2,1)S(1)}, bf16[16,72,128]{2,1,0:T(8,128)(2,1)S(1)}, u32[]{:S(2)}, u32[]{:S(2)}) collective-permute-start(bf16[16,72,128]{2,1,0:T(8,128)(2,1)S(1)} %all-to-all-done.2.g0), channel_id=1, source_target_pairs={{0,8},{8,0},{16,24},{24,16},{1,9},{9,1},{17,25},{25,17},{2,10},{10... | collective-permute-start | bytes 884744 | tf_op jit(solution)/shard_map/ppermute | solution.py:122
  95.3 4.5 %collective-permute-start.8 = (bf16[16,72,128]{2,1,0:T(8,128)(2,1)S(1)}, bf16[16,72,128]{2,1,0:T(8,128)(2,1)S(1)}, u32[]{:S(2)}, u32[]{:S(2)}) collective-permute-start(bf16[16,72,128]{2,1,0:T(8,128)(2,1)S(1)} %all-to-all-done.2.g0), channel_id=1, source_target_pairs={{0,16},{8,24},{16,0},{24,8},{1,17},{9,25},{17,1},{25,9},{2,18},{10... | collective-permute-start | bytes 884744 | tf_op jit(solution)/shard_map/ppermute | solution.py:122
  99.7 0.0 collective-permute-done.1.f1
  99.7 3.5 %collective-permute-start.9 = (bf16[16,72,128]{2,1,0:T(8,128)(2,1)S(1)}, bf16[16,72,128]{2,1,0:T(8,128)(2,1)S(1)}, u32[]{:S(2)}, u32[]{:S(2)}) collective-permute-start(bf16[16,72,128]{2,1,0:T(8,128)(2,1)S(1)} %all-to-all-done.2.g0), channel_id=1, source_target_pairs={{0,24},{8,16},{16,8},{24,0},{1,25},{9,17},{17,9},{25,1},{2,26},{10... | collective-permute-start | bytes 884744 | tf_op jit(solution)/shard_map/ppermute | solution.py:122
  103.3 0.0 collective-permute-done.2.f2
  103.3 0.0 collective-permute-done.3.f3
  103.3 0.0 copy-done.2
  103.3 1.1 shard_map.108
  104.4 0.2 collective-permute-done.7.g1
  104.6 5.7 %collective-permute-done.8.g2 = bf16[16,72,128]{2,1,0:T(8,128)(2,1)S(1)} collective-permute-done((bf16[16,72,128]{2,1,0:T(8,128)(2,1)S(1)}, bf16[16,72,128]{2,1,0:T(8,128)(2,1)S(1)}, u32[]{:S(2)}, u32[]{:S(2)}) %collective-permute-start.8) | collective-permute-done | bytes 294944 | tf_op jit(solution)/shard_map/ppermute | solution.py:122
  110.2 5.4 %collective-permute-done.9.g3 = bf16[16,72,128]{2,1,0:T(8,128)(2,1)S(1)} collective-permute-done((bf16[16,72,128]{2,1,0:T(8,128)(2,1)S(1)}, bf16[16,72,128]{2,1,0:T(8,128)(2,1)S(1)}, u32[]{:S(2)}, u32[]{:S(2)}) %collective-permute-start.9) | collective-permute-done | bytes 294944 | tf_op jit(solution)/shard_map/ppermute | solution.py:122
  115.7 1.3 %shard_map.110 = (bf16[512,1024]{1,0:T(8,128)(2,1)}, bf16[512,128]{1,0:T(8,128)(2,1)}) custom-call(s32[1]{0:T(128)} %bitcast.3.me, bf16[16,72,128]{2,1,0:T(8,128)(2,1)S(1)} %all-to-all-done.2.g0, bf16[16,72,128]{2,1,0:T(8,128)(2,1)S(1)} %collective-permute-done.7.g1, bf16[16,72,128]{2,1,0:T(8,128)(2,1)S(1)} %collective-permute-done.8.g2, ...), custom_call_target="tpu_custom_call" | custom-call | tf_op jit(solution)/shard_map/pallas_call | solution.py:186
Async XLA Ops:
  0.6 1.2 %copy-start.1 = (bf16[32,1024,16]{1,2,0:T(8,128)(2,1)S(1)}, bf16[32,1024,16]{1,2,0:T(8,128)(2,1)}, u32[]{:S(2)}) copy-start(bf16[32,1024,16]{1,2,0:T(8,128)(2,1)} %param.11) | copy-start | bytes 3145732
  1.9 0.9 copy-start.3
  2.8 0.9 copy-start.4
  3.7 0.8 copy-start.5
  4.5 0.7 copy-start.7
  5.1 0.7 copy-start.8
  5.8 0.7 copy-start.9
  7.9 24.0 %all-to-all-start = ((f32[32,32,128]{2,1,0:T(8,128)}), f32[32,32,128]{2,1,0:T(8,128)S(1)}, u32[]{:S(2)}, u32[]{:S(2)}) async-start(f32[32,32,128]{2,1,0:T(8,128)} %get-tuple-element.21), calls=%async_computation | async-start | bytes 1048576 | tf_op jit(solution)/shard_map/all_to_all | solution.py:118
  15.5 10.4 %collective-permute-start.4 = (bf16[136,384]{1,0:T(8,128)(2,1)S(1)}, bf16[136,384]{1,0:T(8,128)(2,1)S(1)}, u32[]{:S(2)}, u32[]{:S(2)}) collective-permute-start(bf16[136,384]{1,0:T(8,128)(2,1)S(1)} %get-tuple-element.23), channel_id=1, source_target_pairs={{0,8},{8,0},{16,24},{24,16},{1,9},{9,1},{17,25},{25,17},{2,10},{10... | collective-permute-start | bytes 313352 | tf_op jit(solution)/shard_map/ppermute | solution.py:122
  18.9 10.8 %collective-permute-start.5 = (bf16[136,384]{1,0:T(8,128)(2,1)S(1)}, bf16[136,384]{1,0:T(8,128)(2,1)S(1)}, u32[]{:S(2)}, u32[]{:S(2)}) collective-permute-start(bf16[136,384]{1,0:T(8,128)(2,1)S(1)} %get-tuple-element.24), channel_id=1, source_target_pairs={{0,16},{8,24},{16,0},{24,8},{1,17},{9,25},{17,1},{25,9},{2,18},{10... | collective-permute-start | bytes 313352 | tf_op jit(solution)/shard_map/ppermute | solution.py:122
  23.5 8.3 %collective-permute-start.6 = (bf16[136,384]{1,0:T(8,128)(2,1)S(1)}, bf16[136,384]{1,0:T(8,128)(2,1)S(1)}, u32[]{:S(2)}, u32[]{:S(2)}) collective-permute-start(bf16[136,384]{1,0:T(8,128)(2,1)S(1)} %get-tuple-element.25), channel_id=1, source_target_pairs={{0,24},{8,16},{16,8},{24,0},{1,25},{9,17},{17,9},{25,1},{2,26},{10... | collective-permute-start | bytes 313352 | tf_op jit(solution)/shard_map/ppermute | solution.py:122
  31.9 16.4 %copy-start = (bf16[8192,128]{1,0:T(8,128)(2,1)S(1)}, bf16[8192,128]{1,0:T(8,128)(2,1)}, u32[]{:S(2)}) copy-start(bf16[8192,128]{1,0:T(8,128)(2,1)} %w.3) | copy-start | bytes 6291460
  31.9 16.4 %copy-start.6 = (bf16[128,128]{1,0:T(8,128)(2,1)S(1)}, bf16[128,128]{1,0:T(8,128)(2,1)}, u32[]{:S(2)}) copy-start(bf16[128,128]{1,0:T(8,128)(2,1)} %c.5) | copy-start | bytes 98308
  32.9 33.9 %all-to-all-start.1 = ((bf16[16,72,128]{2,1,0:T(8,128)(2,1)}), bf16[16,72,128]{2,1,0:T(8,128)(2,1)S(1)}, u32[]{:S(2)}, u32[]{:S(2)}) async-start(bf16[16,72,128]{2,1,0:T(8,128)(2,1)} %get-tuple-element.28), calls=%async_computation.1 | async-start | bytes 589824 | tf_op jit(solution)/shard_map/all_to_all | solution.py:118
  50.9 24.9 %collective-permute-start = (bf16[4,128,1024]{2,1,0:T(8,128)(2,1)}, bf16[4,128,1024]{2,1,0:T(8,128)(2,1)S(1)}, u32[]{:S(2)}, u32[]{:S(2)}) collective-permute-start(bf16[4,128,1024]{2,1,0:T(8,128)(2,1)} %shard_map.104), channel_id=1, source_target_pairs={{0,1},{1,0},{2,3},{3,2},{4,5},{5,4},{6,7},{7,6},{8,9},{9,8},{10,11... | collective-permute-start | bytes 3145736 | tf_op jit(solution)/shard_map/ppermute | solution.py:122
  67.6 25.3 %all-to-all-start.2 = ((bf16[16,72,128]{2,1,0:T(8,128)(2,1)}), bf16[16,72,128]{2,1,0:T(8,128)(2,1)S(1)}, u32[]{:S(2)}, u32[]{:S(2)}) async-start(bf16[16,72,128]{2,1,0:T(8,128)(2,1)} %shard_map.109), calls=%async_computation.2 | async-start | bytes 589824 | tf_op jit(solution)/shard_map/all_to_all | solution.py:118
  75.8 27.5 %copy-start.2 = (bf16[32,1024,16]{1,2,0:T(8,128)(2,1)S(1)}, bf16[32,1024,16]{1,2,0:T(8,128)(2,1)}, u32[]{:S(2)}) copy-start(bf16[32,1024,16]{1,2,0:T(8,128)(2,1)} %param.11) | copy-start | bytes 3145732
  76.1 23.7 %collective-permute-start.1 = (bf16[128,1024]{1,0:T(8,128)(2,1)S(1)}, bf16[128,1024]{1,0:T(8,128)(2,1)S(1)}, u32[]{:S(2)}, u32[]{:S(2)}) collective-permute-start(bf16[128,1024]{1,0:T(8,128)(2,1)S(1)} %get-tuple-element.18), channel_id=1, source_target_pairs={{0,2},{1,3},{2,0},{3,1},{4,6},{5,7},{6,4},{7,5},{8,10},{9,11},{10,... | collective-permute-start | bytes 786440 | tf_op jit(solution)/shard_map/ppermute | solution.py:122
  79.1 24.1 %collective-permute-start.2 = (bf16[128,1024]{1,0:T(8,128)(2,1)S(1)}, bf16[128,1024]{1,0:T(8,128)(2,1)S(1)}, u32[]{:S(2)}, u32[]{:S(2)}) collective-permute-start(bf16[128,1024]{1,0:T(8,128)(2,1)S(1)} %get-tuple-element.19), channel_id=1, source_target_pairs={{0,4},{1,5},{2,6},{3,7},{4,0},{5,1},{6,2},{7,3},{8,12},{9,13},{10,... | collective-permute-start | bytes 786440 | tf_op jit(solution)/shard_map/ppermute | solution.py:122
  82.9 20.4 %collective-permute-start.3 = (bf16[128,1024]{1,0:T(8,128)(2,1)S(1)}, bf16[128,1024]{1,0:T(8,128)(2,1)S(1)}, u32[]{:S(2)}, u32[]{:S(2)}) collective-permute-start(bf16[128,1024]{1,0:T(8,128)(2,1)S(1)} %get-tuple-element.20), channel_id=1, source_target_pairs={{0,6},{1,7},{2,4},{3,5},{4,2},{5,3},{6,0},{7,1},{8,14},{9,15},{10,... | collective-permute-start | bytes 786440 | tf_op jit(solution)/shard_map/ppermute | solution.py:122
  92.8 11.8 %collective-permute-start.7 = (bf16[16,72,128]{2,1,0:T(8,128)(2,1)S(1)}, bf16[16,72,128]{2,1,0:T(8,128)(2,1)S(1)}, u32[]{:S(2)}, u32[]{:S(2)}) collective-permute-start(bf16[16,72,128]{2,1,0:T(8,128)(2,1)S(1)} %all-to-all-done.2.g0), channel_id=1, source_target_pairs={{0,8},{8,0},{16,24},{24,16},{1,9},{9,1},{17,25},{25,17},{2,10},{10... | collective-permute-start | bytes 884744 | tf_op jit(solution)/shard_map/ppermute | solution.py:122
  95.3 15.0 %collective-permute-start.8 = (bf16[16,72,128]{2,1,0:T(8,128)(2,1)S(1)}, bf16[16,72,128]{2,1,0:T(8,128)(2,1)S(1)}, u32[]{:S(2)}, u32[]{:S(2)}) collective-permute-start(bf16[16,72,128]{2,1,0:T(8,128)(2,1)S(1)} %all-to-all-done.2.g0), channel_id=1, source_target_pairs={{0,16},{8,24},{16,0},{24,8},{1,17},{9,25},{17,1},{25,9},{2,18},{10... | collective-permute-start | bytes 884744 | tf_op jit(solution)/shard_map/ppermute | solution.py:122
  99.7 15.9 %collective-permute-start.9 = (bf16[16,72,128]{2,1,0:T(8,128)(2,1)S(1)}, bf16[16,72,128]{2,1,0:T(8,128)(2,1)S(1)}, u32[]{:S(2)}, u32[]{:S(2)}) collective-permute-start(bf16[16,72,128]{2,1,0:T(8,128)(2,1)S(1)} %all-to-all-done.2.g0), channel_id=1, source_target_pairs={{0,24},{8,16},{16,8},{24,0},{1,25},{9,17},{17,9},{25,1},{2,26},{10... | collective-permute-start | bytes 884744 | tf_op jit(solution)/shard_map/ppermute | solution.py:122

commit v4 on v3

--- a/solution.py
+++ b/solution.py
@@ -17,11 +17,11 @@
 GRANT = pltpu.CompilerParams(vmem_limit_bytes=12 << 20)
 
 
-def call(body, outs, flops=0, **kw):
+def call(body, outs, flops=0, grant=GRANT, **kw):
     return pl.pallas_call(
         body,
-        compiler_params=GRANT,
-        out_shape=[jax.ShapeDtypeStruct(s, d) for s, d in outs],
+        compiler_params=grant,
+        out_shape=[pltpu.VMEM(s, d) for s, d in outs],
         cost_estimate=pl.CostEstimate(flops=flops, bytes_accessed=0, transcendentals=0),
         **kw,
     )
@@ -158,6 +158,7 @@
         partial_kernel,
         [((Y * T, 2 * RANK, n), f32), ((8, n), f32)] + [((n + 8, fx // Y + fc), bf16)] * Y,
         flops=10**9,
+        grant=pltpu.CompilerParams(),
         in_specs=[pl.BlockSpec(memory_space=pltpu.VMEM)] * 7 + [pl.BlockSpec(memory_space=pltpu.SMEM)],
     )(x, c, down_rows, up_rows, doc[None], tenant[None], index[None], me)
     parts = swap(part, ("y", "tensor"))

time: 118 us -> 114 us (0.966)
  the two profiles are of different devices: /device:TPU:34 before, /device:TPU:38 now
where the time goes in v4:
time: 114 us; the launch traced here: 113 us
  starting transfers between devices  62.7 us (55%)
  waiting for transfers between devices  37.5 us (33%)
  Pallas kernels  9.85 us (9%)
  local copies, waits for them, and re-layouts  2.35 us (2%)
    ppermute x10, starting transfers between devices, trade(): lax.ppermute(value, axis, [(i, i ^ k) for i in range(lax.axis_size(axis))])  33.3 us
    all_to_all x3, starting transfers between devices, swap(): return lax.all_to_all(value, axis, 0, 0, tiled=True)  29.4 us
    all_to_all x3, waiting for transfers between devices, swap(): return lax.all_to_all(value, axis, 0, 0, tiled=True)  20.1 us
    ppermute x10, waiting for transfers between devices, trade(): lax.ppermute(value, axis, [(i, i ^ k) for i in range(lax.axis_size(axis))])  17.3 us
    pallas_call x2, Pallas kernels, frozen_blocks(): pl.pallas_call(frozen_kernel, compiler_params=GRANT, grid_spec=pltpu.Pref...  4.21 us
    pallas_call x1, Pallas kernels, per_device(): call(partial_kernel, [((Y * T, 2 * RANK, n), f32), ((8, n), f32)] + [((n...  2.86 us
    unnamed x9, local copies, waits for them, and re-layouts  2.35 us
  transfers between devices with their start and end apart: 13, of which 8 were waited for; matrix products, arithmetic and copies ran while one was open for 1% of the time, Pallas kernels for 5%

profile of v4, /device:TPU:38, one launch (start us, length us, event | category | flops | bytes accessed | tf_op | source)
XLA Modules:
  0.0 113.3 jit_solution(4692250708824612595)
XLA Ops:
  0.6 2.9 %shard_map.106 = (f32[32,32,128]{2,1,0:T(8,128)}, f32[8,128]{1,0:T(8,128)S(1)}, bf16[136,384]{1,0:T(8,128)(2,1)S(1)}, bf16[136,384]{1,0:T(8,128)(2,1)S(1)}, bf16...) custom-call(bf16[128,1024]{1,0:T(8,128)(2,1)} %x.1, bf16[128,128]{1,0:T(8,128)(2,1)} %c.5, ...), custom_call_target="tpu_custom_call" | custom-call | flops 1000000000 | tf_op jit(solution)/shard_map/pallas_call | solution.py:157
  3.5 7.6 %all-to-all-start = ((f32[32,32,128]{2,1,0:T(8,128)}), f32[32,32,128]{2,1,0:T(8,128)S(1)}, u32[]{:S(2)}, u32[]{:S(2)}) async-start(f32[32,32,128]{2,1,0:T(8,128)} %get-tuple-element.21), calls=%async_computation | async-start | bytes 1048576 | tf_op jit(solution)/shard_map/all_to_all | solution.py:118
  11.1 3.4 %collective-permute-start.4 = (bf16[136,384]{1,0:T(8,128)(2,1)S(1)}, bf16[136,384]{1,0:T(8,128)(2,1)S(1)}, u32[]{:S(2)}, u32[]{:S(2)}) collective-permute-start(bf16[136,384]{1,0:T(8,128)(2,1)S(1)} %get-tuple-element.23), channel_id=1, source_target_pairs={{0,8},{8,0},{16,24},{24,16},{1,9},{9,1},{17,25},{25,17},{2,10},{10... | collective-permute-start | bytes 313352 | tf_op jit(solution)/shard_map/ppermute | solution.py:122
  14.5 4.7 %collective-permute-start.5 = (bf16[136,384]{1,0:T(8,128)(2,1)S(1)}, bf16[136,384]{1,0:T(8,128)(2,1)S(1)}, u32[]{:S(2)}, u32[]{:S(2)}) collective-permute-start(bf16[136,384]{1,0:T(8,128)(2,1)S(1)} %get-tuple-element.24), channel_id=1, source_target_pairs={{0,16},{8,24},{16,0},{24,8},{1,17},{9,25},{17,1},{25,9},{2,18},{10... | collective-permute-start | bytes 313352 | tf_op jit(solution)/shard_map/ppermute | solution.py:122
  19.1 2.4 %collective-permute-start.6 = (bf16[136,384]{1,0:T(8,128)(2,1)S(1)}, bf16[136,384]{1,0:T(8,128)(2,1)S(1)}, u32[]{:S(2)}, u32[]{:S(2)}) collective-permute-start(bf16[136,384]{1,0:T(8,128)(2,1)S(1)} %get-tuple-element.25), channel_id=1, source_target_pairs={{0,24},{8,16},{16,8},{24,0},{1,25},{9,17},{17,9},{25,1},{2,26},{10... | collective-permute-start | bytes 313352 | tf_op jit(solution)/shard_map/ppermute | solution.py:122
  21.5 0.3 collective-permute-done.4.p1
  21.8 3.4 %collective-permute-done.5.p2 = bf16[136,384]{1,0:T(8,128)(2,1)S(1)} collective-permute-done((bf16[136,384]{1,0:T(8,128)(2,1)S(1)}, bf16[136,384]{1,0:T(8,128)(2,1)S(1)}, u32[]{:S(2)}, u32[]{:S(2)}) %collective-permute-start.5) | collective-permute-done | bytes 104480 | tf_op jit(solution)/shard_map/ppermute | solution.py:122
  25.2 2.2 %collective-permute-done.6.p3 = bf16[136,384]{1,0:T(8,128)(2,1)S(1)} collective-permute-done((bf16[136,384]{1,0:T(8,128)(2,1)S(1)}, bf16[136,384]{1,0:T(8,128)(2,1)S(1)}, u32[]{:S(2)}, u32[]{:S(2)}) %collective-permute-start.6) | collective-permute-done | bytes 104480 | tf_op jit(solution)/shard_map/ppermute | solution.py:122
  27.5 0.0 all-to-all-done.parts
  27.5 0.0 copy-start
  27.5 0.0 copy-start.2
  27.5 1.1 shard_map.107
  28.6 15.2 %all-to-all-start.1 = ((bf16[16,72,128]{2,1,0:T(8,128)(2,1)}), bf16[16,72,128]{2,1,0:T(8,128)(2,1)S(1)}, u32[]{:S(2)}, u32[]{:S(2)}) async-start(bf16[16,72,128]{2,1,0:T(8,128)(2,1)} %get-tuple-element.28), calls=%async_computation.1 | async-start | bytes 589824 | tf_op jit(solution)/shard_map/all_to_all | solution.py:118
  43.8 0.1 pad_add_fusion.1.where
  43.9 0.0 copy-done
  43.9 0.0 copy-done.2
  43.9 2.7 %shard_map.104 = bf16[4,128,1024]{2,1,0:T(8,128)(2,1)} custom-call(s32[2]{0:T(128)S(1)} %pad_add_fusion.1.where, bf16[128,128]{1,0:T(8,128)(2,1)S(1)} %copy-done.2, bf16[8192,128]{1,0:T(8,128)(2,1)S(1)} %copy-done), custom_call_target="tpu_custom_call" | custom-call | flops 1000000000 | tf_op jit(solution)/shard_map/pallas_call | solution.py:132
  46.5 1.9 %collective-permute-start = (bf16[4,128,1024]{2,1,0:T(8,128)(2,1)}, bf16[4,128,1024]{2,1,0:T(8,128)(2,1)S(1)}, u32[]{:S(2)}, u32[]{:S(2)}) collective-permute-start(bf16[4,128,1024]{2,1,0:T(8,128)(2,1)} %shard_map.104), channel_id=1, source_target_pairs={{0,1},{1,0},{2,3},{3,2},{4,5},{5,4},{6,7},{7,6},{8,9},{9,8},{10,11... | collective-permute-start | bytes 3145736 | tf_op jit(solution)/shard_map/ppermute | solution.py:122
  48.5 14.0 %all-to-all-done.1.parts = bf16[16,72,128]{2,1,0:T(8,128)(2,1)S(1)} async-done(((bf16[16,72,128]{2,1,0:T(8,128)(2,1)}), bf16[16,72,128]{2,1,0:T(8,128)(2,1)S(1)}, u32[]{:S(2)}, u32[]{:S(2)}) %all-to-all-start.1) | async-done | bytes 294944 | tf_op jit(solution)/shard_map/all_to_all | solution.py:118
  62.4 0.8 shard_map.109
  63.2 6.6 %all-to-all-start.2 = ((bf16[16,72,128]{2,1,0:T(8,128)(2,1)}), bf16[16,72,128]{2,1,0:T(8,128)(2,1)S(1)}, u32[]{:S(2)}, u32[]{:S(2)}) async-start(bf16[16,72,128]{2,1,0:T(8,128)(2,1)} %shard_map.109), calls=%async_computation.2 | async-start | bytes 589824 | tf_op jit(solution)/shard_map/all_to_all | solution.py:118
  69.8 0.1 pad_add_fusion.where
  69.9 1.5 %shard_map.103.kept = bf16[4,128,1024]{2,1,0:T(8,128)(2,1)S(1)} custom-call(s32[2]{0:T(128)S(1)} %pad_add_fusion.where, bf16[128,128]{1,0:T(8,128)(2,1)S(1)} %copy-done.2, bf16[8192,128]{1,0:T(8,128)(2,1)S(1)} %copy-done), custom_call_target="tpu_custom_call" | custom-call | flops 1000000000 | tf_op jit(solution)/shard_map/pallas_call | solution.py:132
  71.4 0.0 copy-start.1
  71.5 0.0 collective-permute-done.came
  71.5 0.2 shard_map.105
  71.7 2.8 %collective-permute-start.1 = (bf16[128,1024]{1,0:T(8,128)(2,1)S(1)}, bf16[128,1024]{1,0:T(8,128)(2,1)S(1)}, u32[]{:S(2)}, u32[]{:S(2)}) collective-permute-start(bf16[128,1024]{1,0:T(8,128)(2,1)S(1)} %get-tuple-element.18), channel_id=1, source_target_pairs={{0,2},{1,3},{2,0},{3,1},{4,6},{5,7},{6,4},{7,5},{8,10},{9,11},{10,... | collective-permute-start | bytes 786440 | tf_op jit(solution)/shard_map/ppermute | solution.py:122
  74.6 3.6 %collective-permute-start.2 = (bf16[128,1024]{1,0:T(8,128)(2,1)S(1)}, bf16[128,1024]{1,0:T(8,128)(2,1)S(1)}, u32[]{:S(2)}, u32[]{:S(2)}) collective-permute-start(bf16[128,1024]{1,0:T(8,128)(2,1)S(1)} %get-tuple-element.19), channel_id=1, source_target_pairs={{0,4},{1,5},{2,6},{3,7},{4,0},{5,1},{6,2},{7,3},{8,12},{9,13},{10,... | collective-permute-start | bytes 786440 | tf_op jit(solution)/shard_map/ppermute | solution.py:122
  78.1 4.2 %collective-permute-start.3 = (bf16[128,1024]{1,0:T(8,128)(2,1)S(1)}, bf16[128,1024]{1,0:T(8,128)(2,1)S(1)}, u32[]{:S(2)}, u32[]{:S(2)}) collective-permute-start(bf16[128,1024]{1,0:T(8,128)(2,1)S(1)} %get-tuple-element.20), channel_id=1, source_target_pairs={{0,6},{1,7},{2,4},{3,5},{4,2},{5,3},{6,0},{7,1},{8,14},{9,15},{10,... | collective-permute-start | bytes 786440 | tf_op jit(solution)/shard_map/ppermute | solution.py:122
  82.3 6.2 %all-to-all-done.2.g0 = bf16[16,72,128]{2,1,0:T(8,128)(2,1)S(1)} async-done(((bf16[16,72,128]{2,1,0:T(8,128)(2,1)}), bf16[16,72,128]{2,1,0:T(8,128)(2,1)S(1)}, u32[]{:S(2)}, u32[]{:S(2)}) %all-to-all-start.2) | async-done | bytes 294944 | tf_op jit(solution)/shard_map/all_to_all | solution.py:118
  88.5 2.3 %collective-permute-start.7 = (bf16[16,72,128]{2,1,0:T(8,128)(2,1)S(1)}, bf16[16,72,128]{2,1,0:T(8,128)(2,1)S(1)}, u32[]{:S(2)}, u32[]{:S(2)}) collective-permute-start(bf16[16,72,128]{2,1,0:T(8,128)(2,1)S(1)} %all-to-all-done.2.g0), channel_id=1, source_target_pairs={{0,8},{8,0},{16,24},{24,16},{1,9},{9,1},{17,25},{25,17},{2,10},{10... | collective-permute-start | bytes 884744 | tf_op jit(solution)/shard_map/ppermute | solution.py:122
  90.8 4.6 %collective-permute-start.8 = (bf16[16,72,128]{2,1,0:T(8,128)(2,1)S(1)}, bf16[16,72,128]{2,1,0:T(8,128)(2,1)S(1)}, u32[]{:S(2)}, u32[]{:S(2)}) collective-permute-start(bf16[16,72,128]{2,1,0:T(8,128)(2,1)S(1)} %all-to-all-done.2.g0), channel_id=1, source_target_pairs={{0,16},{8,24},{16,0},{24,8},{1,17},{9,25},{17,1},{25,9},{2,18},{10... | collective-permute-start | bytes 884744 | tf_op jit(solution)/shard_map/ppermute | solution.py:122
  95.4 0.0 collective-permute-done.1.f1
  95.4 3.5 %collective-permute-start.9 = (bf16[16,72,128]{2,1,0:T(8,128)(2,1)S(1)}, bf16[16,72,128]{2,1,0:T(8,128)(2,1)S(1)}, u32[]{:S(2)}, u32[]{:S(2)}) collective-permute-start(bf16[16,72,128]{2,1,0:T(8,128)(2,1)S(1)} %all-to-all-done.2.g0), channel_id=1, source_target_pairs={{0,24},{8,16},{16,8},{24,0},{1,25},{9,17},{17,9},{25,1},{2,26},{10... | collective-permute-start | bytes 884744 | tf_op jit(solution)/shard_map/ppermute | solution.py:122
  98.9 0.0 collective-permute-done.2.f2
  98.9 0.0 collective-permute-done.3.f3
  98.9 0.0 copy-done.1
  98.9 0.4 shard_map.108
  99.3 0.7 copy.11
  100.0 0.2 collective-permute-done.7.g1
  100.2 5.7 %collective-permute-done.8.g2 = bf16[16,72,128]{2,1,0:T(8,128)(2,1)S(1)} collective-permute-done((bf16[16,72,128]{2,1,0:T(8,128)(2,1)S(1)}, bf16[16,72,128]{2,1,0:T(8,128)(2,1)S(1)}, u32[]{:S(2)}, u32[]{:S(2)}) %collective-permute-start.8) | collective-permute-done | bytes 294944 | tf_op jit(solution)/shard_map/ppermute | solution.py:122
  106.0 5.4 %collective-permute-done.9.g3 = bf16[16,72,128]{2,1,0:T(8,128)(2,1)S(1)} collective-permute-done((bf16[16,72,128]{2,1,0:T(8,128)(2,1)S(1)}, bf16[16,72,128]{2,1,0:T(8,128)(2,1)S(1)}, u32[]{:S(2)}, u32[]{:S(2)}) %collective-permute-start.9) | collective-permute-done | bytes 294944 | tf_op jit(solution)/shard_map/ppermute | solution.py:122
  111.4 0.3 shard_map.110
  111.7 1.0 copy.12
  112.7 0.7 copy.13
Async XLA Ops:
  3.5 24.0 %all-to-all-start = ((f32[32,32,128]{2,1,0:T(8,128)}), f32[32,32,128]{2,1,0:T(8,128)S(1)}, u32[]{:S(2)}, u32[]{:S(2)}) async-start(f32[32,32,128]{2,1,0:T(8,128)} %get-tuple-element.21), calls=%async_computation | async-start | bytes 1048576 | tf_op jit(solution)/shard_map/all_to_all | solution.py:118
  11.1 10.7 %collective-permute-start.4 = (bf16[136,384]{1,0:T(8,128)(2,1)S(1)}, bf16[136,384]{1,0:T(8,128)(2,1)S(1)}, u32[]{:S(2)}, u32[]{:S(2)}) collective-permute-start(bf16[136,384]{1,0:T(8,128)(2,1)S(1)} %get-tuple-element.23), channel_id=1, source_target_pairs={{0,8},{8,0},{16,24},{24,16},{1,9},{9,1},{17,25},{25,17},{2,10},{10... | collective-permute-start | bytes 313352 | tf_op jit(solution)/shard_map/ppermute | solution.py:122
  14.5 10.8 %collective-permute-start.5 = (bf16[136,384]{1,0:T(8,128)(2,1)S(1)}, bf16[136,384]{1,0:T(8,128)(2,1)S(1)}, u32[]{:S(2)}, u32[]{:S(2)}) collective-permute-start(bf16[136,384]{1,0:T(8,128)(2,1)S(1)} %get-tuple-element.24), channel_id=1, source_target_pairs={{0,16},{8,24},{16,0},{24,8},{1,17},{9,25},{17,1},{25,9},{2,18},{10... | collective-permute-start | bytes 313352 | tf_op jit(solution)/shard_map/ppermute | solution.py:122
  19.1 8.3 %collective-permute-start.6 = (bf16[136,384]{1,0:T(8,128)(2,1)S(1)}, bf16[136,384]{1,0:T(8,128)(2,1)S(1)}, u32[]{:S(2)}, u32[]{:S(2)}) collective-permute-start(bf16[136,384]{1,0:T(8,128)(2,1)S(1)} %get-tuple-element.25), channel_id=1, source_target_pairs={{0,24},{8,16},{16,8},{24,0},{1,25},{9,17},{17,9},{25,1},{2,26},{10... | collective-permute-start | bytes 313352 | tf_op jit(solution)/shard_map/ppermute | solution.py:122
  27.5 16.4 %copy-start = (bf16[8192,128]{1,0:T(8,128)(2,1)S(1)}, bf16[8192,128]{1,0:T(8,128)(2,1)}, u32[]{:S(2)}) copy-start(bf16[8192,128]{1,0:T(8,128)(2,1)} %w.3) | copy-start | bytes 6291460
  27.5 16.4 %copy-start.2 = (bf16[128,128]{1,0:T(8,128)(2,1)S(1)}, bf16[128,128]{1,0:T(8,128)(2,1)}, u32[]{:S(2)}) copy-start(bf16[128,128]{1,0:T(8,128)(2,1)} %c.5) | copy-start | bytes 98308
  28.6 33.9 %all-to-all-start.1 = ((bf16[16,72,128]{2,1,0:T(8,128)(2,1)}), bf16[16,72,128]{2,1,0:T(8,128)(2,1)S(1)}, u32[]{:S(2)}, u32[]{:S(2)}) async-start(bf16[16,72,128]{2,1,0:T(8,128)(2,1)} %get-tuple-element.28), calls=%async_computation.1 | async-start | bytes 589824 | tf_op jit(solution)/shard_map/all_to_all | solution.py:118
  46.5 24.9 %collective-permute-start = (bf16[4,128,1024]{2,1,0:T(8,128)(2,1)}, bf16[4,128,1024]{2,1,0:T(8,128)(2,1)S(1)}, u32[]{:S(2)}, u32[]{:S(2)}) collective-permute-start(bf16[4,128,1024]{2,1,0:T(8,128)(2,1)} %shard_map.104), channel_id=1, source_target_pairs={{0,1},{1,0},{2,3},{3,2},{4,5},{5,4},{6,7},{7,6},{8,9},{9,8},{10,11... | collective-permute-start | bytes 3145736 | tf_op jit(solution)/shard_map/ppermute | solution.py:122
  63.2 25.2 %all-to-all-start.2 = ((bf16[16,72,128]{2,1,0:T(8,128)(2,1)}), bf16[16,72,128]{2,1,0:T(8,128)(2,1)S(1)}, u32[]{:S(2)}, u32[]{:S(2)}) async-start(bf16[16,72,128]{2,1,0:T(8,128)(2,1)} %shard_map.109), calls=%async_computation.2 | async-start | bytes 589824 | tf_op jit(solution)/shard_map/all_to_all | solution.py:118
  71.4 27.5 %copy-start.1 = (bf16[32,1024,16]{1,2,0:T(8,128)(2,1)S(1)}, bf16[32,1024,16]{1,2,0:T(8,128)(2,1)}, u32[]{:S(2)}) copy-start(bf16[32,1024,16]{1,2,0:T(8,128)(2,1)} %param.11) | copy-start | bytes 3145732
  71.7 23.7 %collective-permute-start.1 = (bf16[128,1024]{1,0:T(8,128)(2,1)S(1)}, bf16[128,1024]{1,0:T(8,128)(2,1)S(1)}, u32[]{:S(2)}, u32[]{:S(2)}) collective-permute-start(bf16[128,1024]{1,0:T(8,128)(2,1)S(1)} %get-tuple-element.18), channel_id=1, source_target_pairs={{0,2},{1,3},{2,0},{3,1},{4,6},{5,7},{6,4},{7,5},{8,10},{9,11},{10,... | collective-permute-start | bytes 786440 | tf_op jit(solution)/shard_map/ppermute | solution.py:122
  74.6 24.3 %collective-permute-start.2 = (bf16[128,1024]{1,0:T(8,128)(2,1)S(1)}, bf16[128,1024]{1,0:T(8,128)(2,1)S(1)}, u32[]{:S(2)}, u32[]{:S(2)}) collective-permute-start(bf16[128,1024]{1,0:T(8,128)(2,1)S(1)} %get-tuple-element.19), channel_id=1, source_target_pairs={{0,4},{1,5},{2,6},{3,7},{4,0},{5,1},{6,2},{7,3},{8,12},{9,13},{10,... | collective-permute-start | bytes 786440 | tf_op jit(solution)/shard_map/ppermute | solution.py:122
  78.1 20.8 %collective-permute-start.3 = (bf16[128,1024]{1,0:T(8,128)(2,1)S(1)}, bf16[128,1024]{1,0:T(8,128)(2,1)S(1)}, u32[]{:S(2)}, u32[]{:S(2)}) collective-permute-start(bf16[128,1024]{1,0:T(8,128)(2,1)S(1)} %get-tuple-element.20), channel_id=1, source_target_pairs={{0,6},{1,7},{2,4},{3,5},{4,2},{5,3},{6,0},{7,1},{8,14},{9,15},{10,... | collective-permute-start | bytes 786440 | tf_op jit(solution)/shard_map/ppermute | solution.py:122
  88.5 11.8 %collective-permute-start.7 = (bf16[16,72,128]{2,1,0:T(8,128)(2,1)S(1)}, bf16[16,72,128]{2,1,0:T(8,128)(2,1)S(1)}, u32[]{:S(2)}, u32[]{:S(2)}) collective-permute-start(bf16[16,72,128]{2,1,0:T(8,128)(2,1)S(1)} %all-to-all-done.2.g0), channel_id=1, source_target_pairs={{0,8},{8,0},{16,24},{24,16},{1,9},{9,1},{17,25},{25,17},{2,10},{10... | collective-permute-start | bytes 884744 | tf_op jit(solution)/shard_map/ppermute | solution.py:122
  90.8 15.2 %collective-permute-start.8 = (bf16[16,72,128]{2,1,0:T(8,128)(2,1)S(1)}, bf16[16,72,128]{2,1,0:T(8,128)(2,1)S(1)}, u32[]{:S(2)}, u32[]{:S(2)}) collective-permute-start(bf16[16,72,128]{2,1,0:T(8,128)(2,1)S(1)} %all-to-all-done.2.g0), channel_id=1, source_target_pairs={{0,16},{8,24},{16,0},{24,8},{1,17},{9,25},{17,1},{25,9},{2,18},{10... | collective-permute-start | bytes 884744 | tf_op jit(solution)/shard_map/ppermute | solution.py:122
  95.4 16.0 %collective-permute-start.9 = (bf16[16,72,128]{2,1,0:T(8,128)(2,1)S(1)}, bf16[16,72,128]{2,1,0:T(8,128)(2,1)S(1)}, u32[]{:S(2)}, u32[]{:S(2)}) collective-permute-start(bf16[16,72,128]{2,1,0:T(8,128)(2,1)S(1)} %all-to-all-done.2.g0), channel_id=1, source_target_pairs={{0,24},{8,16},{16,8},{24,0},{1,25},{9,17},{17,9},{25,1},{2,26},{10... | collective-permute-start | bytes 884744 | tf_op jit(solution)/shard_map/ppermute | solution.py:122

commit v5 on v4

--- a/solution.py
+++ b/solution.py
@@ -17,11 +17,11 @@
 GRANT = pltpu.CompilerParams(vmem_limit_bytes=12 << 20)
 
 
-def call(body, outs, flops=0, grant=GRANT, **kw):
+def call(body, outs, flops=0, grant=GRANT, out=pltpu.VMEM, **kw):
     return pl.pallas_call(
         body,
         compiler_params=grant,
-        out_shape=[pltpu.VMEM(s, d) for s, d in outs],
+        out_shape=[out(s, d) for s, d in outs],
         cost_estimate=pl.CostEstimate(flops=flops, bytes_accessed=0, transcendentals=0),
         **kw,
     )
@@ -45,7 +45,7 @@
     g_all = lax.dot_general(up[...], c[...], NT, preferred_element_type=f32)
     g = jnp.sum(jnp.where(member, g_all, 0.0).reshape(SLOTS, RANK, n), axis=0)
     h = jnp.sum(jnp.where(member, h_all, 0.0).reshape(SLOTS, RANK, n), axis=0)
-    both = jnp.concatenate([g, h], axis=0)
+    both = jnp.concatenate([g, h], axis=0).astype(bf16)
     for i in range(Y * T):
         part[i] = both
     fx = x.shape[1] // Y
@@ -61,9 +61,9 @@
     gs, hs = [], []
     for k, pack in enumerate((p0, p1, p2, p3)):
         at = me[0] ^ k
-        both = parts[at * T]
+        both = parts[at * T].astype(f32)
         for j in range(1, T):
-            both = both + parts[at * T + j]
+            both = both + parts[at * T + j].astype(f32)
         both = both.astype(bf16)
         if k == 0:
             low_out[...] = both
@@ -156,7 +156,7 @@
     block = (ROWS // Z * 2 + ROWS // Y // Z, 128)
     part, slot, *packs = call(
         partial_kernel,
-        [((Y * T, 2 * RANK, n), f32), ((8, n), f32)] + [((n + 8, fx // Y + fc), bf16)] * Y,
+        [((Y * T, 2 * RANK, n), bf16), ((8, n), f32)] + [((n + 8, fx // Y + fc), bf16)] * Y,
         flops=10**9,
         grant=pltpu.CompilerParams(),
         in_specs=[pl.BlockSpec(memory_space=pltpu.VMEM)] * 7 + [pl.BlockSpec(memory_space=pltpu.SMEM)],
@@ -180,11 +180,13 @@
         frozens.append(trade(pairs[k], "tensor", 2 * k))
     (done,) = call(finish_kernel, [((Z, *block), bf16)], flops=10**8)(sums)
     rows = swap(done, "z")
-    (input_gradient,) = call(input_kernel, [((n, fx), bf16)], flops=10**9)(*frozens, low, slot, down_rows)
+    (input_gradient,) = call(input_kernel, [((n, fx), bf16)], flops=10**9, out=jax.ShapeDtypeStruct)(*frozens, low, slot, down_rows)
     outs = [rows]
     for k in (1, 2, 3):
         outs.append(trade(rows, "y", k))
-    whole, up_whole = call(layout_kernel, [((ROWS, fx), bf16), ((ROWS, fc), bf16)], in_specs=specs(4))(me, *outs)
+    whole, up_whole = call(
+        layout_kernel, [((ROWS, fx), bf16), ((ROWS, fc), bf16)], out=jax.ShapeDtypeStruct, in_specs=specs(4)
+    )(me, *outs)
     down_gradient = jnp.transpose(whole.reshape(SLOTS, RANK, fx), (0, 2, 1))
     up_gradient = up_whole.reshape(SLOTS, RANK, fc)
     return input_gradient, down_gradient, up_gradient

time: 114 us -> 111 us (0.974)
  local copies, waits for them, and re-layouts: 2.35 us -> 0.01 us
  waiting for transfers between devices: 37.5 us -> 35.9 us
  Pallas kernels: 9.85 us -> 11.4 us
    unnamed x9 -> x6, local copies, waits for them, and re-layouts: 2.35 us -> 0.01 us
    pallas_call x3, Pallas kernels: 3.55 us -> 5.14 us  [the longest x1 2.74 us: per_device(): call(partial_kernel, [((Y * T, 2 * RANK, n), bf16), ((8, n), f32)] + [((n...]
  transfers between devices with their start and end apart: 13 -> 13, of which waited for: 8 -> 7; matrix products, arithmetic and copies ran while one was open for 1% -> 0% of each run, Pallas kernels for 5% -> 6%
where the time goes in v5:
time: 111 us; the launch traced here: 110 us
  starting transfers between devices  62.2 us (56%)
  waiting for transfers between devices  35.9 us (32%)
  Pallas kernels  11.4 us (10%)
    ppermute x10, starting transfers between devices, trade(): lax.ppermute(value, axis, [(i, i ^ k) for i in range(lax.axis_size(axis))])  33.3 us
    all_to_all x3, starting transfers between devices, swap(): return lax.all_to_all(value, axis, 0, 0, tiled=True)  28.9 us
    all_to_all x3, waiting for transfers between devices, swap(): return lax.all_to_all(value, axis, 0, 0, tiled=True)  19.2 us
    ppermute x10, waiting for transfers between devices, trade(): lax.ppermute(value, axis, [(i, i ^ k) for i in range(lax.axis_size(axis))])  16.7 us
    pallas_call x2, Pallas kernels, frozen_blocks(): pl.pallas_call(frozen_kernel, compiler_params=GRANT, grid_spec=pltpu.Pref...  4.21 us
    pallas_call x1, Pallas kernels, per_device(): call(partial_kernel, [((Y * T, 2 * RANK, n), bf16), ((8, n), f32)] + [((n...  2.74 us
  transfers between devices with their start and end apart: 13, of which 7 were waited for; matrix products, arithmetic and copies ran while one was open for 0% of the time, Pallas kernels for 6%

profile of v5, /device:TPU:38, one launch (start us, length us, event | category | flops | bytes accessed | tf_op | source)
XLA Modules:
  0.0 110.5 jit_solution(18190470546686625214)
XLA Ops:
  0.6 2.7 %shard_map.106 = (bf16[32,32,128]{2,1,0:T(8,128)(2,1)}, f32[8,128]{1,0:T(8,128)S(1)}, bf16[136,384]{1,0:T(8,128)(2,1)S(1)}, bf16[136,384]{1,0:T(8,128)(2,1)S(1)}...) custom-call(bf16[128,1024]{1,0:T(8,128)(2,1)} %x.1, bf16[128,128]{1,0:T(8,128)(2,1)} %c.5, ...), custom_call_target="tpu_custom_call" | custom-call | flops 1000000000 | tf_op jit(solution)/shard_map/pallas_call | solution.py:157
  3.4 7.6 %all-to-all-start = ((bf16[32,32,128]{2,1,0:T(8,128)(2,1)}), bf16[32,32,128]{2,1,0:T(8,128)(2,1)S(1)}, u32[]{:S(2)}, u32[]{:S(2)}) async-start(bf16[32,32,128]{2,1,0:T(8,128)(2,1)} %get-tuple-element.21), calls=%async_computation | async-start | bytes 524288 | tf_op jit(solution)/shard_map/all_to_all | solution.py:118
  11.0 3.4 %collective-permute-start.4 = (bf16[136,384]{1,0:T(8,128)(2,1)S(1)}, bf16[136,384]{1,0:T(8,128)(2,1)S(1)}, u32[]{:S(2)}, u32[]{:S(2)}) collective-permute-start(bf16[136,384]{1,0:T(8,128)(2,1)S(1)} %get-tuple-element.23), channel_id=1, source_target_pairs={{0,8},{8,0},{16,24},{24,16},{1,9},{9,1},{17,25},{25,17},{2,10},{10... | collective-permute-start | bytes 313352 | tf_op jit(solution)/shard_map/ppermute | solution.py:122
  14.3 4.7 %collective-permute-start.5 = (bf16[136,384]{1,0:T(8,128)(2,1)S(1)}, bf16[136,384]{1,0:T(8,128)(2,1)S(1)}, u32[]{:S(2)}, u32[]{:S(2)}) collective-permute-start(bf16[136,384]{1,0:T(8,128)(2,1)S(1)} %get-tuple-element.24), channel_id=1, source_target_pairs={{0,16},{8,24},{16,0},{24,8},{1,17},{9,25},{17,1},{25,9},{2,18},{10... | collective-permute-start | bytes 313352 | tf_op jit(solution)/shard_map/ppermute | solution.py:122
  19.0 2.4 %collective-permute-start.6 = (bf16[136,384]{1,0:T(8,128)(2,1)S(1)}, bf16[136,384]{1,0:T(8,128)(2,1)S(1)}, u32[]{:S(2)}, u32[]{:S(2)}) collective-permute-start(bf16[136,384]{1,0:T(8,128)(2,1)S(1)} %get-tuple-element.25), channel_id=1, source_target_pairs={{0,24},{8,16},{16,8},{24,0},{1,25},{9,17},{17,9},{25,1},{2,26},{10... | collective-permute-start | bytes 313352 | tf_op jit(solution)/shard_map/ppermute | solution.py:122
  21.4 0.0 collective-permute-done.4.p1
  21.4 1.1 collective-permute-done.5.p2
  22.5 4.3 %collective-permute-done.6.p3 = bf16[136,384]{1,0:T(8,128)(2,1)S(1)} collective-permute-done((bf16[136,384]{1,0:T(8,128)(2,1)S(1)}, bf16[136,384]{1,0:T(8,128)(2,1)S(1)}, u32[]{:S(2)}, u32[]{:S(2)}) %collective-permute-start.6) | collective-permute-done | bytes 104480 | tf_op jit(solution)/shard_map/ppermute | solution.py:122
  26.8 0.0 all-to-all-done.parts
  26.8 0.0 copy-start
  26.8 0.0 copy-start.2
  26.8 1.1 shard_map.107
  27.9 15.2 %all-to-all-start.1 = ((bf16[16,72,128]{2,1,0:T(8,128)(2,1)}), bf16[16,72,128]{2,1,0:T(8,128)(2,1)S(1)}, u32[]{:S(2)}, u32[]{:S(2)}) async-start(bf16[16,72,128]{2,1,0:T(8,128)(2,1)} %get-tuple-element.28), calls=%async_computation.1 | async-start | bytes 589824 | tf_op jit(solution)/shard_map/all_to_all | solution.py:118
  43.1 0.1 pad_add_fusion.1.where
  43.2 0.0 copy-done
  43.2 0.0 copy-done.2
  43.2 2.7 %shard_map.104 = bf16[4,128,1024]{2,1,0:T(8,128)(2,1)} custom-call(s32[2]{0:T(128)S(1)} %pad_add_fusion.1.where, bf16[128,128]{1,0:T(8,128)(2,1)S(1)} %copy-done.2, bf16[8192,128]{1,0:T(8,128)(2,1)S(1)} %copy-done), custom_call_target="tpu_custom_call" | custom-call | flops 1000000000 | tf_op jit(solution)/shard_map/pallas_call | solution.py:132
  45.9 1.9 %collective-permute-start = (bf16[4,128,1024]{2,1,0:T(8,128)(2,1)}, bf16[4,128,1024]{2,1,0:T(8,128)(2,1)S(1)}, u32[]{:S(2)}, u32[]{:S(2)}) collective-permute-start(bf16[4,128,1024]{2,1,0:T(8,128)(2,1)} %shard_map.104), channel_id=1, source_target_pairs={{0,1},{1,0},{2,3},{3,2},{4,5},{5,4},{6,7},{7,6},{8,9},{9,8},{10,11... | collective-permute-start | bytes 3145736 | tf_op jit(solution)/shard_map/ppermute | solution.py:122
  47.8 13.3 %all-to-all-done.1.parts = bf16[16,72,128]{2,1,0:T(8,128)(2,1)S(1)} async-done(((bf16[16,72,128]{2,1,0:T(8,128)(2,1)}), bf16[16,72,128]{2,1,0:T(8,128)(2,1)S(1)}, u32[]{:S(2)}, u32[]{:S(2)}) %all-to-all-start.1) | async-done | bytes 294944 | tf_op jit(solution)/shard_map/all_to_all | solution.py:118
  61.1 0.8 shard_map.109
  61.9 6.1 %all-to-all-start.2 = ((bf16[16,72,128]{2,1,0:T(8,128)(2,1)}), bf16[16,72,128]{2,1,0:T(8,128)(2,1)S(1)}, u32[]{:S(2)}, u32[]{:S(2)}) async-start(bf16[16,72,128]{2,1,0:T(8,128)(2,1)} %shard_map.109), calls=%async_computation.2 | async-start | bytes 589824 | tf_op jit(solution)/shard_map/all_to_all | solution.py:118
  68.0 0.1 pad_add_fusion.where
  68.1 1.5 %shard_map.103.kept = bf16[4,128,1024]{2,1,0:T(8,128)(2,1)S(1)} custom-call(s32[2]{0:T(128)S(1)} %pad_add_fusion.where, bf16[128,128]{1,0:T(8,128)(2,1)S(1)} %copy-done.2, bf16[8192,128]{1,0:T(8,128)(2,1)S(1)} %copy-done), custom_call_target="tpu_custom_call" | custom-call | flops 1000000000 | tf_op jit(solution)/shard_map/pallas_call | solution.py:132
  69.6 0.0 copy-start.1
  69.6 0.0 collective-permute-done.came
  69.6 0.2 shard_map.105
  69.9 2.9 %collective-permute-start.1 = (bf16[128,1024]{1,0:T(8,128)(2,1)S(1)}, bf16[128,1024]{1,0:T(8,128)(2,1)S(1)}, u32[]{:S(2)}, u32[]{:S(2)}) collective-permute-start(bf16[128,1024]{1,0:T(8,128)(2,1)S(1)} %get-tuple-element.18), channel_id=1, source_target_pairs={{0,2},{1,3},{2,0},{3,1},{4,6},{5,7},{6,4},{7,5},{8,10},{9,11},{10,... | collective-permute-start | bytes 786440 | tf_op jit(solution)/shard_map/ppermute | solution.py:122
  72.8 3.0 %collective-permute-start.2 = (bf16[128,1024]{1,0:T(8,128)(2,1)S(1)}, bf16[128,1024]{1,0:T(8,128)(2,1)S(1)}, u32[]{:S(2)}, u32[]{:S(2)}) collective-permute-start(bf16[128,1024]{1,0:T(8,128)(2,1)S(1)} %get-tuple-element.19), channel_id=1, source_target_pairs={{0,4},{1,5},{2,6},{3,7},{4,0},{5,1},{6,2},{7,3},{8,12},{9,13},{10,... | collective-permute-start | bytes 786440 | tf_op jit(solution)/shard_map/ppermute | solution.py:122
  75.8 4.6 %collective-permute-start.3 = (bf16[128,1024]{1,0:T(8,128)(2,1)S(1)}, bf16[128,1024]{1,0:T(8,128)(2,1)S(1)}, u32[]{:S(2)}, u32[]{:S(2)}) collective-permute-start(bf16[128,1024]{1,0:T(8,128)(2,1)S(1)} %get-tuple-element.20), channel_id=1, source_target_pairs={{0,6},{1,7},{2,4},{3,5},{4,2},{5,3},{6,0},{7,1},{8,14},{9,15},{10,... | collective-permute-start | bytes 786440 | tf_op jit(solution)/shard_map/ppermute | solution.py:122
  80.5 5.8 %all-to-all-done.2.g0 = bf16[16,72,128]{2,1,0:T(8,128)(2,1)S(1)} async-done(((bf16[16,72,128]{2,1,0:T(8,128)(2,1)}), bf16[16,72,128]{2,1,0:T(8,128)(2,1)S(1)}, u32[]{:S(2)}, u32[]{:S(2)}) %all-to-all-start.2) | async-done | bytes 294944 | tf_op jit(solution)/shard_map/all_to_all | solution.py:118
  86.3 1.9 %collective-permute-start.7 = (bf16[16,72,128]{2,1,0:T(8,128)(2,1)S(1)}, bf16[16,72,128]{2,1,0:T(8,128)(2,1)S(1)}, u32[]{:S(2)}, u32[]{:S(2)}) collective-permute-start(bf16[16,72,128]{2,1,0:T(8,128)(2,1)S(1)} %all-to-all-done.2.g0), channel_id=1, source_target_pairs={{0,8},{8,0},{16,24},{24,16},{1,9},{9,1},{17,25},{25,17},{2,10},{10... | collective-permute-start | bytes 884744 | tf_op jit(solution)/shard_map/ppermute | solution.py:122
  88.2 4.5 %collective-permute-start.8 = (bf16[16,72,128]{2,1,0:T(8,128)(2,1)S(1)}, bf16[16,72,128]{2,1,0:T(8,128)(2,1)S(1)}, u32[]{:S(2)}, u32[]{:S(2)}) collective-permute-start(bf16[16,72,128]{2,1,0:T(8,128)(2,1)S(1)} %all-to-all-done.2.g0), channel_id=1, source_target_pairs={{0,16},{8,24},{16,0},{24,8},{1,17},{9,25},{17,1},{25,9},{2,18},{10... | collective-permute-start | bytes 884744 | tf_op jit(solution)/shard_map/ppermute | solution.py:122
  92.7 0.0 collective-permute-done.1.f1
  92.8 4.0 %collective-permute-start.9 = (bf16[16,72,128]{2,1,0:T(8,128)(2,1)S(1)}, bf16[16,72,128]{2,1,0:T(8,128)(2,1)S(1)}, u32[]{:S(2)}, u32[]{:S(2)}) collective-permute-start(bf16[16,72,128]{2,1,0:T(8,128)(2,1)S(1)} %all-to-all-done.2.g0), channel_id=1, source_target_pairs={{0,24},{8,16},{16,8},{24,0},{1,25},{9,17},{17,9},{25,1},{2,26},{10... | collective-permute-start | bytes 884744 | tf_op jit(solution)/shard_map/ppermute | solution.py:122
  96.7 0.0 collective-permute-done.2.f2
  96.7 0.0 collective-permute-done.3.f3
  96.7 0.0 copy-done.1
  96.7 1.1 shard_map.108
  97.8 0.2 collective-permute-done.7.g1
  98.0 5.5 %collective-permute-done.8.g2 = bf16[16,72,128]{2,1,0:T(8,128)(2,1)S(1)} collective-permute-done((bf16[16,72,128]{2,1,0:T(8,128)(2,1)S(1)}, bf16[16,72,128]{2,1,0:T(8,128)(2,1)S(1)}, u32[]{:S(2)}, u32[]{:S(2)}) %collective-permute-start.8) | collective-permute-done | bytes 294944 | tf_op jit(solution)/shard_map/ppermute | solution.py:122
  103.6 5.6 %collective-permute-done.9.g3 = bf16[16,72,128]{2,1,0:T(8,128)(2,1)S(1)} collective-permute-done((bf16[16,72,128]{2,1,0:T(8,128)(2,1)S(1)}, bf16[16,72,128]{2,1,0:T(8,128)(2,1)S(1)}, u32[]{:S(2)}, u32[]{:S(2)}) %collective-permute-start.9) | collective-permute-done | bytes 294944 | tf_op jit(solution)/shard_map/ppermute | solution.py:122
  109.1 1.3 %shard_map.110 = (bf16[512,1024]{1,0:T(8,128)(2,1)}, bf16[512,128]{1,0:T(8,128)(2,1)}) custom-call(s32[1]{0:T(128)} %bitcast.3.me, bf16[16,72,128]{2,1,0:T(8,128)(2,1)S(1)} %all-to-all-done.2.g0, bf16[16,72,128]{2,1,0:T(8,128)(2,1)S(1)} %collective-permute-done.7.g1, bf16[16,72,128]{2,1,0:T(8,128)(2,1)S(1)} %collective-permute-done.8.g2, ...), custom_call_target="tpu_custom_call" | custom-call | tf_op jit(solution)/shard_map/pallas_call | solution.py:187
Async XLA Ops:
  3.4 23.4 %all-to-all-start = ((bf16[32,32,128]{2,1,0:T(8,128)(2,1)}), bf16[32,32,128]{2,1,0:T(8,128)(2,1)S(1)}, u32[]{:S(2)}, u32[]{:S(2)}) async-start(bf16[32,32,128]{2,1,0:T(8,128)(2,1)} %get-tuple-element.21), calls=%async_computation | async-start | bytes 524288 | tf_op jit(solution)/shard_map/all_to_all | solution.py:118
  11.0 10.4 %collective-permute-start.4 = (bf16[136,384]{1,0:T(8,128)(2,1)S(1)}, bf16[136,384]{1,0:T(8,128)(2,1)S(1)}, u32[]{:S(2)}, u32[]{:S(2)}) collective-permute-start(bf16[136,384]{1,0:T(8,128)(2,1)S(1)} %get-tuple-element.23), channel_id=1, source_target_pairs={{0,8},{8,0},{16,24},{24,16},{1,9},{9,1},{17,25},{25,17},{2,10},{10... | collective-permute-start | bytes 313352 | tf_op jit(solution)/shard_map/ppermute | solution.py:122
  14.3 8.2 %collective-permute-start.5 = (bf16[136,384]{1,0:T(8,128)(2,1)S(1)}, bf16[136,384]{1,0:T(8,128)(2,1)S(1)}, u32[]{:S(2)}, u32[]{:S(2)}) collective-permute-start(bf16[136,384]{1,0:T(8,128)(2,1)S(1)} %get-tuple-element.24), channel_id=1, source_target_pairs={{0,16},{8,24},{16,0},{24,8},{1,17},{9,25},{17,1},{25,9},{2,18},{10... | collective-permute-start | bytes 313352 | tf_op jit(solution)/shard_map/ppermute | solution.py:122
  19.0 7.8 %collective-permute-start.6 = (bf16[136,384]{1,0:T(8,128)(2,1)S(1)}, bf16[136,384]{1,0:T(8,128)(2,1)S(1)}, u32[]{:S(2)}, u32[]{:S(2)}) collective-permute-start(bf16[136,384]{1,0:T(8,128)(2,1)S(1)} %get-tuple-element.25), channel_id=1, source_target_pairs={{0,24},{8,16},{16,8},{24,0},{1,25},{9,17},{17,9},{25,1},{2,26},{10... | collective-permute-start | bytes 313352 | tf_op jit(solution)/shard_map/ppermute | solution.py:122
  26.8 16.4 %copy-start = (bf16[8192,128]{1,0:T(8,128)(2,1)S(1)}, bf16[8192,128]{1,0:T(8,128)(2,1)}, u32[]{:S(2)}) copy-start(bf16[8192,128]{1,0:T(8,128)(2,1)} %w.3) | copy-start | bytes 6291460
  26.8 16.4 %copy-start.2 = (bf16[128,128]{1,0:T(8,128)(2,1)S(1)}, bf16[128,128]{1,0:T(8,128)(2,1)}, u32[]{:S(2)}) copy-start(bf16[128,128]{1,0:T(8,128)(2,1)} %c.5) | copy-start | bytes 98308
  27.9 33.2 %all-to-all-start.1 = ((bf16[16,72,128]{2,1,0:T(8,128)(2,1)}), bf16[16,72,128]{2,1,0:T(8,128)(2,1)S(1)}, u32[]{:S(2)}, u32[]{:S(2)}) async-start(bf16[16,72,128]{2,1,0:T(8,128)(2,1)} %get-tuple-element.28), calls=%async_computation.1 | async-start | bytes 589824 | tf_op jit(solution)/shard_map/all_to_all | solution.py:118
  45.9 23.8 %collective-permute-start = (bf16[4,128,1024]{2,1,0:T(8,128)(2,1)}, bf16[4,128,1024]{2,1,0:T(8,128)(2,1)S(1)}, u32[]{:S(2)}, u32[]{:S(2)}) collective-permute-start(bf16[4,128,1024]{2,1,0:T(8,128)(2,1)} %shard_map.104), channel_id=1, source_target_pairs={{0,1},{1,0},{2,3},{3,2},{4,5},{5,4},{6,7},{7,6},{8,9},{9,8},{10,11... | collective-permute-start | bytes 3145736 | tf_op jit(solution)/shard_map/ppermute | solution.py:122
  61.9 24.4 %all-to-all-start.2 = ((bf16[16,72,128]{2,1,0:T(8,128)(2,1)}), bf16[16,72,128]{2,1,0:T(8,128)(2,1)S(1)}, u32[]{:S(2)}, u32[]{:S(2)}) async-start(bf16[16,72,128]{2,1,0:T(8,128)(2,1)} %shard_map.109), calls=%async_computation.2 | async-start | bytes 589824 | tf_op jit(solution)/shard_map/all_to_all | solution.py:118
  69.6 27.1 %copy-start.1 = (bf16[32,1024,16]{1,2,0:T(8,128)(2,1)S(1)}, bf16[32,1024,16]{1,2,0:T(8,128)(2,1)}, u32[]{:S(2)}) copy-start(bf16[32,1024,16]{1,2,0:T(8,128)(2,1)} %param.11) | copy-start | bytes 3145732
  69.9 22.9 %collective-permute-start.1 = (bf16[128,1024]{1,0:T(8,128)(2,1)S(1)}, bf16[128,1024]{1,0:T(8,128)(2,1)S(1)}, u32[]{:S(2)}, u32[]{:S(2)}) collective-permute-start(bf16[128,1024]{1,0:T(8,128)(2,1)S(1)} %get-tuple-element.18), channel_id=1, source_target_pairs={{0,2},{1,3},{2,0},{3,1},{4,6},{5,7},{6,4},{7,5},{8,10},{9,11},{10,... | collective-permute-start | bytes 786440 | tf_op jit(solution)/shard_map/ppermute | solution.py:122
  72.8 23.9 %collective-permute-start.2 = (bf16[128,1024]{1,0:T(8,128)(2,1)S(1)}, bf16[128,1024]{1,0:T(8,128)(2,1)S(1)}, u32[]{:S(2)}, u32[]{:S(2)}) collective-permute-start(bf16[128,1024]{1,0:T(8,128)(2,1)S(1)} %get-tuple-element.19), channel_id=1, source_target_pairs={{0,4},{1,5},{2,6},{3,7},{4,0},{5,1},{6,2},{7,3},{8,12},{9,13},{10,... | collective-permute-start | bytes 786440 | tf_op jit(solution)/shard_map/ppermute | solution.py:122
  75.8 20.9 %collective-permute-start.3 = (bf16[128,1024]{1,0:T(8,128)(2,1)S(1)}, bf16[128,1024]{1,0:T(8,128)(2,1)S(1)}, u32[]{:S(2)}, u32[]{:S(2)}) collective-permute-start(bf16[128,1024]{1,0:T(8,128)(2,1)S(1)} %get-tuple-element.20), channel_id=1, source_target_pairs={{0,6},{1,7},{2,4},{3,5},{4,2},{5,3},{6,0},{7,1},{8,14},{9,15},{10,... | collective-permute-start | bytes 786440 | tf_op jit(solution)/shard_map/ppermute | solution.py:122
  86.3 11.8 %collective-permute-start.7 = (bf16[16,72,128]{2,1,0:T(8,128)(2,1)S(1)}, bf16[16,72,128]{2,1,0:T(8,128)(2,1)S(1)}, u32[]{:S(2)}, u32[]{:S(2)}) collective-permute-start(bf16[16,72,128]{2,1,0:T(8,128)(2,1)S(1)} %all-to-all-done.2.g0), channel_id=1, source_target_pairs={{0,8},{8,0},{16,24},{24,16},{1,9},{9,1},{17,25},{25,17},{2,10},{10... | collective-permute-start | bytes 884744 | tf_op jit(solution)/shard_map/ppermute | solution.py:122
  88.2 15.4 %collective-permute-start.8 = (bf16[16,72,128]{2,1,0:T(8,128)(2,1)S(1)}, bf16[16,72,128]{2,1,0:T(8,128)(2,1)S(1)}, u32[]{:S(2)}, u32[]{:S(2)}) collective-permute-start(bf16[16,72,128]{2,1,0:T(8,128)(2,1)S(1)} %all-to-all-done.2.g0), channel_id=1, source_target_pairs={{0,16},{8,24},{16,0},{24,8},{1,17},{9,25},{17,1},{25,9},{2,18},{10... | collective-permute-start | bytes 884744 | tf_op jit(solution)/shard_map/ppermute | solution.py:122
  92.8 16.4 %collective-permute-start.9 = (bf16[16,72,128]{2,1,0:T(8,128)(2,1)S(1)}, bf16[16,72,128]{2,1,0:T(8,128)(2,1)S(1)}, u32[]{:S(2)}, u32[]{:S(2)}) collective-permute-start(bf16[16,72,128]{2,1,0:T(8,128)(2,1)S(1)} %all-to-all-done.2.g0), channel_id=1, source_target_pairs={{0,24},{8,16},{16,8},{24,0},{1,25},{9,17},{17,9},{25,1},{2,26},{10... | collective-permute-start | bytes 884744 | tf_op jit(solution)/shard_map/ppermute | solution.py:122

commit v6 on v4

--- a/solution.py
+++ b/solution.py
@@ -17,11 +17,11 @@
 GRANT = pltpu.CompilerParams(vmem_limit_bytes=12 << 20)
 
 
-def call(body, outs, flops=0, grant=GRANT, **kw):
+def call(body, outs, flops=0, grant=GRANT, out=pltpu.VMEM, **kw):
     return pl.pallas_call(
         body,
         compiler_params=grant,
-        out_shape=[pltpu.VMEM(s, d) for s, d in outs],
+        out_shape=[out(s, d) for s, d in outs],
         cost_estimate=pl.CostEstimate(flops=flops, bytes_accessed=0, transcendentals=0),
         **kw,
     )
@@ -83,18 +83,19 @@
 
 def finish_kernel(parts, out):
     total = (adapter_scale * jnp.sum(parts[...].astype(f32), axis=0)).astype(bf16)
-    for z in range(Z):
+    for z in range(Z // 2):
         out[z] = total
 
 
-def layout_kernel(me, g0, g1, g2, g3, down, up):
+def layout_kernel(parts, down, up):
     rd = ROWS // Z
-    for k, g in enumerate((g0, g1, g2, g3)):
-        at = me[0] ^ k
-        v = g[...].astype(f32)
-        down[:, pl.ds(pl.multiple_of(at * 256, 256), 128)] = v[:, :rd].reshape(ROWS, 128).astype(bf16)
-        down[:, pl.ds(pl.multiple_of(at * 256 + 128, 128), 128)] = v[:, rd : 2 * rd].reshape(ROWS, 128).astype(bf16)
-        up[pl.ds(pl.multiple_of(at * 128, 128), 128)] = v[:, 2 * rd :].reshape(128, 128).astype(bf16)
+    for q in range(2 * Y):
+        b, y = q // Y, q % Y
+        v = parts[q].astype(f32)
+        for k in (0, 1):
+            at = y * 256 + k * 128
+            down[:, b, :, at : at + 128] = v[:, k * rd : (k + 1) * rd].astype(bf16)
+        up[y, :, b] = v[:, 2 * rd :].astype(bf16)
 
 
 def frozen_kernel(where, c, w, out):
@@ -120,6 +121,11 @@
 
 def trade(value, axis, k):
     return lax.ppermute(value, axis, [(i, i ^ k) for i in range(lax.axis_size(axis))])
+
+
+def to_all(value, axes):
+    count = lax.axis_size(axes)
+    return swap(jnp.broadcast_to(value[None], (count, *value.shape)), axes)
 
 
 def specs(count):
@@ -170,7 +176,7 @@
         flops=10**9,
         in_specs=specs(5),
     )(me, parts, *packs)
-    sums = swap(piece, "z")
+    sums = swap(piece, ("zh", "zl"))
     send = frozen_blocks(c, w, jnp.stack([at >> 1, (at & 1) ^ 1]))
     came = trade(send, "tensor", 1)
     kept = frozen_blocks(c, w, jnp.stack([at >> 1, at & 1]))
@@ -178,21 +184,23 @@
     frozens = [pairs[0]]
     for k in (1, 2, 3):
         frozens.append(trade(pairs[k], "tensor", 2 * k))
-    (done,) = call(finish_kernel, [((Z, *block), bf16)], flops=10**8)(sums)
-    rows = swap(done, "z")
-    (input_gradient,) = call(input_kernel, [((n, fx), bf16)], flops=10**9)(*frozens, low, slot, down_rows)
-    outs = [rows]
-    for k in (1, 2, 3):
-        outs.append(trade(rows, "y", k))
-    whole, up_whole = call(layout_kernel, [((ROWS, fx), bf16), ((ROWS, fc), bf16)], in_specs=specs(4))(me, *outs)
+    (done,) = call(finish_kernel, [((Z // 2, *block), bf16)], flops=10**8)(sums)
+    rows = swap(done, "zh")
+    (input_gradient,) = call(input_kernel, [((n, fx), bf16)], flops=10**9, out=jax.ShapeDtypeStruct)(*frozens, low, slot, down_rows)
+    outs = to_all(rows, ("zl", "y"))
+    whole, up_whole = call(
+        layout_kernel,
+        [((Z // 2, 2, ROWS // Z, fx), bf16), ((Y, Z // 2, 2, ROWS // Y // Z, fc), bf16)],
+        out=jax.ShapeDtypeStruct,
+    )(outs)
     down_gradient = jnp.transpose(whole.reshape(SLOTS, RANK, fx), (0, 2, 1))
     up_gradient = up_whole.reshape(SLOTS, RANK, fc)
     return input_gradient, down_gradient, up_gradient
 
 
 def solution(mesh):
-    grid = Mesh(mesh.devices.reshape(Z, Y, T), ("z", "y", "tensor"))
-    dp = ("z", "y")
+    grid = Mesh(mesh.devices.reshape(Z // 2, 2, Y, T), ("zh", "zl", "y", "tensor"))
+    dp = ("zh", "zl", "y")
     in_specs = (
         P(dp, "tensor"),
         P(dp, "tensor"),

time: 114 us -> 123 us (1.079)
  the two profiles are of different devices: /device:TPU:38 before, /device:TPU:1 now
where the time goes in v6:
time: 123 us
  blocking collectives  50.7 us (41%)
  starting transfers between devices  39.9 us (32%)
  waiting for transfers between devices  20.9 us (17%)
  Pallas kernels  8.96 us (7%)
    all_to_all x2, blocking collectives, swap(): return lax.all_to_all(value, axis, 0, 0, tiled=True)  50.7 us
    ppermute x7, starting transfers between devices, trade(): lax.ppermute(value, axis, [(i, i ^ k) for i in range(lax.axis_size(axis))])  25.6 us
    ppermute x7, waiting for transfers between devices, trade(): lax.ppermute(value, axis, [(i, i ^ k) for i in range(lax.axis_size(axis))])  20.9 us
    all_to_all x2, starting transfers between devices, swap(): return lax.all_to_all(value, axis, 0, 0, tiled=True)  14.3 us
    pallas_call x2, Pallas kernels, frozen_blocks(): pl.pallas_call(frozen_kernel, compiler_params=GRANT, grid_spec=pltpu.Pref...  3.07 us
    pallas_call x1, Pallas kernels, per_device(): call(partial_kernel, [((Y * T, 2 * RANK, n), f32), ((8, n), f32)] + [((n...  2.86 us
  transfers between devices with their start and end apart: 9, of which 6 were waited for; matrix products, arithmetic and copies ran while one was open for 0% of the time, Pallas kernels for 4%

profile of v6, /device:TPU:1, one launch (start us, length us, event | category | flops | bytes accessed | tf_op | source)
XLA Modules:
  0.0 122.6 jit_solution(11498463540683458917)
XLA Ops:
  0.6 2.9 %shard_map.106 = (f32[32,32,128]{2,1,0:T(8,128)}, f32[8,128]{1,0:T(8,128)S(1)}, bf16[136,384]{1,0:T(8,128)(2,1)S(1)}, bf16[136,384]{1,0:T(8,128)(2,1)S(1)}, bf16...) custom-call(bf16[128,1024]{1,0:T(8,128)(2,1)} %x.1, bf16[128,128]{1,0:T(8,128)(2,1)} %c.5, ...), custom_call_target="tpu_custom_call" | custom-call | flops 1000000000 | tf_op jit(solution)/shard_map/pallas_call | solution.py:163
  3.5 10.4 %all-to-all-start = ((f32[32,32,128]{2,1,0:T(8,128)}), f32[32,32,128]{2,1,0:T(8,128)S(1)}, u32[]{:S(2)}, u32[]{:S(2)}) async-start(f32[32,32,128]{2,1,0:T(8,128)} %get-tuple-element.21), calls=%async_computation | async-start | bytes 1048576 | tf_op jit(solution)/shard_map/all_to_all | solution.py:119
  13.9 3.3 %collective-permute-start.4 = (bf16[136,384]{1,0:T(8,128)(2,1)S(1)}, bf16[136,384]{1,0:T(8,128)(2,1)S(1)}, u32[]{:S(2)}, u32[]{:S(2)}) collective-permute-start(bf16[136,384]{1,0:T(8,128)(2,1)S(1)} %get-tuple-element.23), channel_id=1, source_target_pairs={{0,8},{8,0},{16,24},{24,16},{1,9},{9,1},{17,25},{25,17},{2,10},{10... | collective-permute-start | bytes 313352 | tf_op jit(solution)/shard_map/ppermute | solution.py:123
  17.2 4.4 %collective-permute-start.5 = (bf16[136,384]{1,0:T(8,128)(2,1)S(1)}, bf16[136,384]{1,0:T(8,128)(2,1)S(1)}, u32[]{:S(2)}, u32[]{:S(2)}) collective-permute-start(bf16[136,384]{1,0:T(8,128)(2,1)S(1)} %get-tuple-element.24), channel_id=1, source_target_pairs={{0,16},{8,24},{16,0},{24,8},{1,17},{9,25},{17,1},{25,9},{2,18},{10... | collective-permute-start | bytes 313352 | tf_op jit(solution)/shard_map/ppermute | solution.py:123
  21.6 1.9 %collective-permute-start.6 = (bf16[136,384]{1,0:T(8,128)(2,1)S(1)}, bf16[136,384]{1,0:T(8,128)(2,1)S(1)}, u32[]{:S(2)}, u32[]{:S(2)}) collective-permute-start(bf16[136,384]{1,0:T(8,128)(2,1)S(1)} %get-tuple-element.25), channel_id=1, source_target_pairs={{0,24},{8,16},{16,8},{24,0},{1,25},{9,17},{17,9},{25,1},{2,26},{10... | collective-permute-start | bytes 313352 | tf_op jit(solution)/shard_map/ppermute | solution.py:123
  23.6 0.8 collective-permute-done.4.p1
  24.3 3.6 %collective-permute-done.5.p2 = bf16[136,384]{1,0:T(8,128)(2,1)S(1)} collective-permute-done((bf16[136,384]{1,0:T(8,128)(2,1)S(1)}, bf16[136,384]{1,0:T(8,128)(2,1)S(1)}, u32[]{:S(2)}, u32[]{:S(2)}) %collective-permute-start.5) | collective-permute-done | bytes 104480 | tf_op jit(solution)/shard_map/ppermute | solution.py:123
  28.0 2.5 %collective-permute-done.6.p3 = bf16[136,384]{1,0:T(8,128)(2,1)S(1)} collective-permute-done((bf16[136,384]{1,0:T(8,128)(2,1)S(1)}, bf16[136,384]{1,0:T(8,128)(2,1)S(1)}, u32[]{:S(2)}, u32[]{:S(2)}) %collective-permute-start.6) | collective-permute-done | bytes 104480 | tf_op jit(solution)/shard_map/ppermute | solution.py:123
  30.4 0.0 all-to-all-done.parts
  30.4 0.3 shard_map.107
  30.8 27.0 %all_to_all.20.parts = bf16[16,72,128]{2,1,0:T(8,128)(2,1)S(1)} all-to-all(bf16[16,72,128]{2,1,0:T(8,128)(2,1)S(1)} %get-tuple-element.28), channel_id=1, replica_groups=mesh['zh'=8,'zl'=2,'y'=4,'tensor'=8] {'zh','zl'}, dimensions={0} | all-to-all | bytes 589824 | tf_op jit(solution)/shard_map/all_to_all | solution.py:119
  57.7 0.1 shard_map.109
  57.8 23.8 %all_to_all.21 = bf16[8,72,128]{2,1,0:T(8,128)(2,1)S(1)} all-to-all(bf16[8,72,128]{2,1,0:T(8,128)(2,1)S(1)} %shard_map.109), channel_id=1, replica_groups=mesh['zh'=8,'zl'=2,'y'=4,'tensor'=8] {'zh'}, dimensions={0} | all-to-all | bytes 294912 | tf_op jit(solution)/shard_map/all_to_all | solution.py:119
  81.6 1.2 broadcast_in_dim.22
  82.7 0.0 copy-start
  82.8 0.0 copy-start.2
  82.8 3.9 %all-to-all-start.3 = ((bf16[8,8,72,128]{3,2,1,0:T(8,128)(2,1)}), bf16[8,8,72,128]{3,2,1,0:T(8,128)(2,1)S(1)}, u32[]{:S(2)}, u32[]{:S(2)}) async-start(bf16[8,8,72,128]{3,2,1,0:T(8,128)(2,1)} %broadcast_in_dim.22), calls=%async_computation.3 | async-start | bytes 2359296 | tf_op jit(solution)/shard_map/all_to_all | solution.py:119
  86.7 0.1 pad_add_fusion.1.where
  86.7 0.0 copy-done
  86.8 0.0 copy-done.2
  86.8 1.5 %shard_map.104 = bf16[4,128,1024]{2,1,0:T(8,128)(2,1)S(1)} custom-call(s32[2]{0:T(128)S(1)} %pad_add_fusion.1.where, bf16[128,128]{1,0:T(8,128)(2,1)S(1)} %copy-done.2, bf16[8192,128]{1,0:T(8,128)(2,1)S(1)} %copy-done), custom_call_target="tpu_custom_call" | custom-call | flops 1000000000 | tf_op jit(solution)/shard_map/pallas_call | solution.py:138
  88.3 6.3 %collective-permute-start = (bf16[4,128,1024]{2,1,0:T(8,128)(2,1)S(1)}, bf16[4,128,1024]{2,1,0:T(8,128)(2,1)S(1)}, u32[]{:S(2)}, u32[]{:S(2)}) collective-permute-start(bf16[4,128,1024]{2,1,0:T(8,128)(2,1)S(1)} %shard_map.104), channel_id=1, source_target_pairs={{0,1},{1,0},{2,3},{3,2},{4,5},{5,4},{6,7},{7,6},{8,9},{9,8},{10,11... | collective-permute-start | bytes 3145736 | tf_op jit(solution)/shard_map/ppermute | solution.py:123
  94.6 0.1 pad_add_fusion.where
  94.7 1.5 %shard_map.103.kept = bf16[4,128,1024]{2,1,0:T(8,128)(2,1)S(1)} custom-call(s32[2]{0:T(128)S(1)} %pad_add_fusion.where, bf16[128,128]{1,0:T(8,128)(2,1)S(1)} %copy-done.2, bf16[8192,128]{1,0:T(8,128)(2,1)S(1)} %copy-done), custom_call_target="tpu_custom_call" | custom-call | flops 1000000000 | tf_op jit(solution)/shard_map/pallas_call | solution.py:138
  96.3 0.0 copy-start.1
  96.3 0.6 collective-permute-done.came
  96.9 0.2 shard_map.105
  97.1 2.6 %collective-permute-start.1 = (bf16[128,1024]{1,0:T(8,128)(2,1)S(1)}, bf16[128,1024]{1,0:T(8,128)(2,1)S(1)}, u32[]{:S(2)}, u32[]{:S(2)}) collective-permute-start(bf16[128,1024]{1,0:T(8,128)(2,1)S(1)} %get-tuple-element.18), channel_id=1, source_target_pairs={{0,2},{1,3},{2,0},{3,1},{4,6},{5,7},{6,4},{7,5},{8,10},{9,11},{10,... | collective-permute-start | bytes 786440 | tf_op jit(solution)/shard_map/ppermute | solution.py:123
  99.8 4.3 %collective-permute-start.2 = (bf16[128,1024]{1,0:T(8,128)(2,1)S(1)}, bf16[128,1024]{1,0:T(8,128)(2,1)S(1)}, u32[]{:S(2)}, u32[]{:S(2)}) collective-permute-start(bf16[128,1024]{1,0:T(8,128)(2,1)S(1)} %get-tuple-element.19), channel_id=1, source_target_pairs={{0,4},{1,5},{2,6},{3,7},{4,0},{5,1},{6,2},{7,3},{8,12},{9,13},{10,... | collective-permute-start | bytes 786440 | tf_op jit(solution)/shard_map/ppermute | solution.py:123
  104.1 2.6 %collective-permute-start.3 = (bf16[128,1024]{1,0:T(8,128)(2,1)S(1)}, bf16[128,1024]{1,0:T(8,128)(2,1)S(1)}, u32[]{:S(2)}, u32[]{:S(2)}) collective-permute-start(bf16[128,1024]{1,0:T(8,128)(2,1)S(1)} %get-tuple-element.20), channel_id=1, source_target_pairs={{0,6},{1,7},{2,4},{3,5},{4,2},{5,3},{6,0},{7,1},{8,14},{9,15},{10,... | collective-permute-start | bytes 786440 | tf_op jit(solution)/shard_map/ppermute | solution.py:123
  106.8 0.0 collective-permute-done.1.f1
  106.8 7.1 %collective-permute-done.2.f2 = bf16[128,1024]{1,0:T(8,128)(2,1)S(1)} collective-permute-done((bf16[128,1024]{1,0:T(8,128)(2,1)S(1)}, bf16[128,1024]{1,0:T(8,128)(2,1)S(1)}, u32[]{:S(2)}, u32[]{:S(2)}) %collective-permute-start.2) | collective-permute-done | bytes 262176 | tf_op jit(solution)/shard_map/ppermute | solution.py:123
  113.9 6.3 %collective-permute-done.3.f3 = bf16[128,1024]{1,0:T(8,128)(2,1)S(1)} collective-permute-done((bf16[128,1024]{1,0:T(8,128)(2,1)S(1)}, bf16[128,1024]{1,0:T(8,128)(2,1)S(1)}, u32[]{:S(2)}, u32[]{:S(2)}) %collective-permute-start.3) | collective-permute-done | bytes 262176 | tf_op jit(solution)/shard_map/ppermute | solution.py:123
  120.2 0.0 copy-done.1
  120.2 1.1 shard_map.108
  121.3 0.0 all-to-all-done.3.parts
  121.3 1.3 %shard_map.110 = (bf16[8,2,32,1024]{3,2,1,0:T(8,128)(2,1)}, bf16[4,8,2,8,128]{4,3,2,1,0:T(8,128)(2,1)}) custom-call(bf16[8,8,72,128]{3,2,1,0:T(8,128)(2,1)S(1)} %all-to-all-done.3.parts), custom_call_target="tpu_custom_call" | custom-call | tf_op jit(solution)/shard_map/pallas_call | solution.py:191
Async XLA Ops:
  3.5 26.9 %all-to-all-start = ((f32[32,32,128]{2,1,0:T(8,128)}), f32[32,32,128]{2,1,0:T(8,128)S(1)}, u32[]{:S(2)}, u32[]{:S(2)}) async-start(f32[32,32,128]{2,1,0:T(8,128)} %get-tuple-element.21), calls=%async_computation | async-start | bytes 1048576 | tf_op jit(solution)/shard_map/all_to_all | solution.py:119
  13.9 10.4 %collective-permute-start.4 = (bf16[136,384]{1,0:T(8,128)(2,1)S(1)}, bf16[136,384]{1,0:T(8,128)(2,1)S(1)}, u32[]{:S(2)}, u32[]{:S(2)}) collective-permute-start(bf16[136,384]{1,0:T(8,128)(2,1)S(1)} %get-tuple-element.23), channel_id=1, source_target_pairs={{0,8},{8,0},{16,24},{24,16},{1,9},{9,1},{17,25},{25,17},{2,10},{10... | collective-permute-start | bytes 313352 | tf_op jit(solution)/shard_map/ppermute | solution.py:123
  17.2 10.8 %collective-permute-start.5 = (bf16[136,384]{1,0:T(8,128)(2,1)S(1)}, bf16[136,384]{1,0:T(8,128)(2,1)S(1)}, u32[]{:S(2)}, u32[]{:S(2)}) collective-permute-start(bf16[136,384]{1,0:T(8,128)(2,1)S(1)} %get-tuple-element.24), channel_id=1, source_target_pairs={{0,16},{8,24},{16,0},{24,8},{1,17},{9,25},{17,1},{25,9},{2,18},{10... | collective-permute-start | bytes 313352 | tf_op jit(solution)/shard_map/ppermute | solution.py:123
  21.6 8.8 %collective-permute-start.6 = (bf16[136,384]{1,0:T(8,128)(2,1)S(1)}, bf16[136,384]{1,0:T(8,128)(2,1)S(1)}, u32[]{:S(2)}, u32[]{:S(2)}) collective-permute-start(bf16[136,384]{1,0:T(8,128)(2,1)S(1)} %get-tuple-element.25), channel_id=1, source_target_pairs={{0,24},{8,16},{16,8},{24,0},{1,25},{9,17},{17,9},{25,1},{2,26},{10... | collective-permute-start | bytes 313352 | tf_op jit(solution)/shard_map/ppermute | solution.py:123
  82.7 4.0 %copy-start = (bf16[8192,128]{1,0:T(8,128)(2,1)S(1)}, bf16[8192,128]{1,0:T(8,128)(2,1)}, u32[]{:S(2)}) copy-start(bf16[8192,128]{1,0:T(8,128)(2,1)} %w.3) | copy-start | bytes 6291460
  82.8 4.0 %copy-start.2 = (bf16[128,128]{1,0:T(8,128)(2,1)S(1)}, bf16[128,128]{1,0:T(8,128)(2,1)}, u32[]{:S(2)}) copy-start(bf16[128,128]{1,0:T(8,128)(2,1)} %c.5) | copy-start | bytes 98308
  82.8 38.5 %all-to-all-start.3 = ((bf16[8,8,72,128]{3,2,1,0:T(8,128)(2,1)}), bf16[8,8,72,128]{3,2,1,0:T(8,128)(2,1)S(1)}, u32[]{:S(2)}, u32[]{:S(2)}) async-start(bf16[8,8,72,128]{3,2,1,0:T(8,128)(2,1)} %broadcast_in_dim.22), calls=%async_computation.3 | async-start | bytes 2359296 | tf_op jit(solution)/shard_map/all_to_all | solution.py:119
  88.3 8.6 %collective-permute-start = (bf16[4,128,1024]{2,1,0:T(8,128)(2,1)S(1)}, bf16[4,128,1024]{2,1,0:T(8,128)(2,1)S(1)}, u32[]{:S(2)}, u32[]{:S(2)}) collective-permute-start(bf16[4,128,1024]{2,1,0:T(8,128)(2,1)S(1)} %shard_map.104), channel_id=1, source_target_pairs={{0,1},{1,0},{2,3},{3,2},{4,5},{5,4},{6,7},{7,6},{8,9},{9,8},{10,11... | collective-permute-start | bytes 3145736 | tf_op jit(solution)/shard_map/ppermute | solution.py:123
  96.3 23.9 %copy-start.1 = (bf16[32,1024,16]{1,2,0:T(8,128)(2,1)S(1)}, bf16[32,1024,16]{1,2,0:T(8,128)(2,1)}, u32[]{:S(2)}) copy-start(bf16[32,1024,16]{1,2,0:T(8,128)(2,1)} %param.11) | copy-start | bytes 3145732
  97.1 9.6 %collective-permute-start.1 = (bf16[128,1024]{1,0:T(8,128)(2,1)S(1)}, bf16[128,1024]{1,0:T(8,128)(2,1)S(1)}, u32[]{:S(2)}, u32[]{:S(2)}) collective-permute-start(bf16[128,1024]{1,0:T(8,128)(2,1)S(1)} %get-tuple-element.18), channel_id=1, source_target_pairs={{0,2},{1,3},{2,0},{3,1},{4,6},{5,7},{6,4},{7,5},{8,10},{9,11},{10,... | collective-permute-start | bytes 786440 | tf_op jit(solution)/shard_map/ppermute | solution.py:123
  99.8 14.1 %collective-permute-start.2 = (bf16[128,1024]{1,0:T(8,128)(2,1)S(1)}, bf16[128,1024]{1,0:T(8,128)(2,1)S(1)}, u32[]{:S(2)}, u32[]{:S(2)}) collective-permute-start(bf16[128,1024]{1,0:T(8,128)(2,1)S(1)} %get-tuple-element.19), channel_id=1, source_target_pairs={{0,4},{1,5},{2,6},{3,7},{4,0},{5,1},{6,2},{7,3},{8,12},{9,13},{10,... | collective-permute-start | bytes 786440 | tf_op jit(solution)/shard_map/ppermute | solution.py:123
  104.1 16.1 %collective-permute-start.3 = (bf16[128,1024]{1,0:T(8,128)(2,1)S(1)}, bf16[128,1024]{1,0:T(8,128)(2,1)S(1)}, u32[]{:S(2)}, u32[]{:S(2)}) collective-permute-start(bf16[128,1024]{1,0:T(8,128)(2,1)S(1)} %get-tuple-element.20), channel_id=1, source_target_pairs={{0,6},{1,7},{2,4},{3,5},{4,2},{5,3},{6,0},{7,1},{8,14},{9,15},{10,... | collective-permute-start | bytes 786440 | tf_op jit(solution)/shard_map/ppermute | solution.py:123

commit v7 on v6

--- a/solution.py
+++ b/solution.py
@@ -32,7 +32,7 @@
     return jnp.where(at == slot, jnp.concatenate([low] * slots, axis=0), 0.0)
 
 
-def partial_kernel(x, c, down, up, doc, tenant, index, me, part, slot_out, *packs):
+def partial_kernel(x, c, down, up, doc, tenant, index, part, slot_out, pack):
     n = x.shape[0]
     tenant_of = (lax.broadcasted_iota(jnp.int32, (SLOTS, tenant.shape[1]), 0) == tenant[...]).astype(bf16)
     table = jnp.broadcast_to(index[...].astype(f32), (8, SLOTS)).astype(bf16)
@@ -50,29 +50,30 @@
         part[i] = both
     fx = x.shape[1] // Y
     slots = jnp.concatenate([slot, jnp.zeros((8, fx + c.shape[1] - n), f32)], axis=1)
-    for k, pack in enumerate(packs):
-        at = pl.multiple_of((me[0] ^ k) * fx, fx)
-        mine = jnp.concatenate([x[:, pl.ds(at, fx)], c[...]], axis=1)
-        pack[...] = jnp.concatenate([mine.astype(f32), slots], axis=0).astype(bf16)
-
-
-def gradient_kernel(me, parts, p0, p1, p2, p3, out, low_out):
-    fx = p0.shape[1] - 128
+    for y in range(Y):
+        mine = jnp.concatenate([x[:, y * fx : (y + 1) * fx], c[...]], axis=1)
+        pack[y] = jnp.concatenate([mine.astype(f32), slots], axis=0).astype(bf16)
+
+
+def gradient_kernel(me, parts, packs, out, low_out):
+    fx = packs.shape[2] - 128
     gs, hs = [], []
-    for k, pack in enumerate((p0, p1, p2, p3)):
-        at = me[0] ^ k
-        both = parts[at * T]
+    for y in range(Y):
+        both = parts[y * T]
         for j in range(1, T):
-            both = both + parts[at * T + j]
+            both = both + parts[y * T + j]
         both = both.astype(bf16)
-        if k == 0:
+
+        @pl.when(me[0] == y)
+        def _():
             low_out[...] = both
+
         both = both.astype(f32)
-        slot = pack[128:, :128].astype(f32)[:1].astype(jnp.int32)
+        slot = packs[y, 128:, :128].astype(f32)[:1].astype(jnp.int32)
         gs.append(spread(both[:RANK], slot).astype(bf16))
         hs.append(spread(both[RANK:], slot, me[0] * (SLOTS // Y), SLOTS // Y).astype(bf16))
-    xs = jnp.concatenate([p[:128, :fx] for p in (p0, p1, p2, p3)], axis=0)
-    cs = jnp.concatenate([p[:128, fx:] for p in (p0, p1, p2, p3)], axis=0)
+    xs = jnp.concatenate([packs[y, :128, :fx] for y in range(Y)], axis=0)
+    cs = jnp.concatenate([packs[y, :128, fx:] for y in range(Y)], axis=0)
     down = jnp.dot(jnp.concatenate(gs, axis=1), xs, preferred_element_type=f32)
     up = jnp.dot(jnp.concatenate(hs, axis=1), cs, preferred_element_type=f32)
     rd, ru = ROWS // Z, ROWS // Y // Z
@@ -83,19 +84,18 @@
 
 def finish_kernel(parts, out):
     total = (adapter_scale * jnp.sum(parts[...].astype(f32), axis=0)).astype(bf16)
-    for z in range(Z // 2):
+    for z in range(Z):
         out[z] = total
 
 
 def layout_kernel(parts, down, up):
     rd = ROWS // Z
-    for q in range(2 * Y):
-        b, y = q // Y, q % Y
-        v = parts[q].astype(f32)
+    for y in range(Y):
+        v = parts[y].astype(f32)
         for k in (0, 1):
             at = y * 256 + k * 128
-            down[:, b, :, at : at + 128] = v[:, k * rd : (k + 1) * rd].astype(bf16)
-        up[y, :, b] = v[:, 2 * rd :].astype(bf16)
+            down[:, at : at + 128] = v[:, k * rd : (k + 1) * rd].reshape(ROWS, 128).astype(bf16)
+        up[y * 128 : (y + 1) * 128] = v[:, 2 * rd :].reshape(128, 128).astype(bf16)
 
 
 def frozen_kernel(where, c, w, out):
@@ -157,40 +157,41 @@
     fc = c.shape[1]
     me = lax.axis_index("y")[None]
     at = lax.axis_index("tensor")
+    mine, other = at & 1, (at & 1) ^ 1
+    column = at >> 1
     down_rows = jnp.transpose(down, (0, 2, 1)).reshape(ROWS, fx)
     up_rows = up.reshape(ROWS, fc)
     block = (ROWS // Z * 2 + ROWS // Y // Z, 128)
-    part, slot, *packs = call(
+    part, slot, pack = call(
         partial_kernel,
-        [((Y * T, 2 * RANK, n), f32), ((8, n), f32)] + [((n + 8, fx // Y + fc), bf16)] * Y,
+        [((Y * T, 2 * RANK, n), f32), ((8, n), f32), ((Y, n + 8, fx // Y + fc), bf16)],
         flops=10**9,
         grant=pltpu.CompilerParams(),
-        in_specs=[pl.BlockSpec(memory_space=pltpu.VMEM)] * 7 + [pl.BlockSpec(memory_space=pltpu.SMEM)],
-    )(x, c, down_rows, up_rows, doc[None], tenant[None], index[None], me)
+    )(x, c, down_rows, up_rows, doc[None], tenant[None], index[None])
     parts = swap(part, ("y", "tensor"))
-    for k in (1, 2, 3):
-        packs[k] = trade(packs[k], "y", k)
+    packs = swap(pack, "y")
     piece, low = call(
         gradient_kernel,
         [((Z, *block), bf16), ((2 * RANK, n), bf16)],
         flops=10**9,
-        in_specs=specs(5),
-    )(me, parts, *packs)
-    sums = swap(piece, ("zh", "zl"))
-    send = frozen_blocks(c, w, jnp.stack([at >> 1, (at & 1) ^ 1]))
+        in_specs=specs(2),
+    )(me, parts, packs)
+    sums = swap(piece, "z")
+    to_send, to_keep = jnp.stack([column, other]), jnp.stack([column, mine])
+    send = frozen_blocks(c, w, to_send)
     came = trade(send, "tensor", 1)
-    kept = frozen_blocks(c, w, jnp.stack([at >> 1, at & 1]))
+    kept = frozen_blocks(c, w, to_keep)
     pairs = call(pair_kernel, [((n, fx), bf16)] * 4, flops=10**8)(kept, came)
     frozens = [pairs[0]]
     for k in (1, 2, 3):
         frozens.append(trade(pairs[k], "tensor", 2 * k))
-    (done,) = call(finish_kernel, [((Z // 2, *block), bf16)], flops=10**8)(sums)
-    rows = swap(done, "zh")
+    (done,) = call(finish_kernel, [((Z, *block), bf16)], flops=10**8)(sums)
+    rows = swap(done, "z")
     (input_gradient,) = call(input_kernel, [((n, fx), bf16)], flops=10**9, out=jax.ShapeDtypeStruct)(*frozens, low, slot, down_rows)
-    outs = to_all(rows, ("zl", "y"))
+    outs = to_all(rows, "y")
     whole, up_whole = call(
         layout_kernel,
-        [((Z // 2, 2, ROWS // Z, fx), bf16), ((Y, Z // 2, 2, ROWS // Y // Z, fc), bf16)],
+        [((ROWS, fx), bf16), ((ROWS, fc), bf16)],
         out=jax.ShapeDtypeStruct,
     )(outs)
     down_gradient = jnp.transpose(whole.reshape(SLOTS, RANK, fx), (0, 2, 1))
@@ -199,8 +200,8 @@
 
 
 def solution(mesh):
-    grid = Mesh(mesh.devices.reshape(Z // 2, 2, Y, T), ("zh", "zl", "y", "tensor"))
-    dp = ("zh", "zl", "y")
+    grid = Mesh(mesh.devices.reshape(Z, Y, T), ("z", "y", "tensor"))
+    dp = ("z", "y")
     in_specs = (
         P(dp, "tensor"),
         P(dp, "tensor"),

time: 123 us -> 127 us (1.033)
  the two profiles are of different devices: /device:TPU:1 before, /device:TPU:32 now
where the time goes in v7:
time: 127 us; the launch traced here: 126 us
  blocking collectives  46.9 us (37%)
  waiting for transfers between devices  36.8 us (29%)
  starting transfers between devices  28 us (22%)
  Pallas kernels  10.9 us (9%)
  local copies, waits for them, and re-layouts  2.8 us (2%)
    all_to_all x2, blocking collectives, swap(): return lax.all_to_all(value, axis, 0, 0, tiled=True)  46.9 us
    all_to_all x3, waiting for transfers between devices, swap(): return lax.all_to_all(value, axis, 0, 0, tiled=True)  25.8 us
    all_to_all x3, starting transfers between devices, swap(): return lax.all_to_all(value, axis, 0, 0, tiled=True)  15.5 us
    ppermute x4, starting transfers between devices, trade(): lax.ppermute(value, axis, [(i, i ^ k) for i in range(lax.axis_size(axis))])  12.5 us
    ppermute x4, waiting for transfers between devices, trade(): lax.ppermute(value, axis, [(i, i ^ k) for i in range(lax.axis_size(axis))])  11 us
    pallas_call x2, Pallas kernels, frozen_blocks(): pl.pallas_call(frozen_kernel, compiler_params=GRANT, grid_spec=pltpu.Pref...  4.21 us
    pallas_call x1, Pallas kernels, per_device(): call(partial_kernel, [((Y * T, 2 * RANK, n), f32), ((8, n), f32), ((Y, n...  2.85 us
  transfers between devices with their start and end apart: 7, of which 5 were waited for; matrix products, arithmetic and copies ran while one was open for 1% of the time, Pallas kernels for 4%

profile of v7, /device:TPU:32, one launch (start us, length us, event | category | flops | bytes accessed | tf_op | source)
XLA Modules:
  0.0 126.2 jit_solution(9267614396609073974)
XLA Ops:
  0.6 2.9 %shard_map.106 = (f32[32,32,128]{2,1,0:T(8,128)}, f32[8,128]{1,0:T(8,128)S(1)}, bf16[4,136,384]{2,1,0:T(8,128)(2,1)S(1)}) custom-call(bf16[128,1024]{1,0:T(8,128)(2,1)} %x.1, bf16[128,128]{1,0:T(8,128)(2,1)} %c.5, bf16[512,1024]{1,0:T(8,128)(2,1)} %bitcast.15, bf16[512,128]{1,0:T(8,128)(2,1)} %bitcast.18, s32[1,128]{1,0:T(1,128)} %bitcast.20, ...), custom_call_target="tpu_custom_call" | custom-call | flops 1000000000 | tf_op jit(solution)/shard_map/pallas_call | solution.py:165
  3.5 12.6 %all_to_all.25.packs = bf16[4,136,384]{2,1,0:T(8,128)(2,1)S(1)} all-to-all(bf16[4,136,384]{2,1,0:T(8,128)(2,1)S(1)} %get-tuple-element.19), channel_id=1, replica_groups=mesh['z'=16,'y'=4,'tensor'=8] {'y'}, dimensions={0} | all-to-all | bytes 835584 | tf_op jit(solution)/shard_map/all_to_all | solution.py:119
  16.1 5.3 %all-to-all-start = ((f32[32,32,128]{2,1,0:T(8,128)}), f32[32,32,128]{2,1,0:T(8,128)S(1)}, u32[]{:S(2)}, u32[]{:S(2)}) async-start(f32[32,32,128]{2,1,0:T(8,128)} %get-tuple-element.18), calls=%async_computation | async-start | bytes 1048576 | tf_op jit(solution)/shard_map/all_to_all | solution.py:119
  21.4 11.6 %all-to-all-done.parts = f32[32,32,128]{2,1,0:T(8,128)S(1)} async-done(((f32[32,32,128]{2,1,0:T(8,128)}), f32[32,32,128]{2,1,0:T(8,128)S(1)}, u32[]{:S(2)}, u32[]{:S(2)}) %all-to-all-start) | async-done | bytes 524320 | tf_op jit(solution)/shard_map/all_to_all | solution.py:119
  33.0 0.0 copy-start
  33.0 0.4 shard_map.107
  33.4 0.0 copy-start.3
  33.4 34.3 %all_to_all.26.parts = bf16[16,72,128]{2,1,0:T(8,128)(2,1)S(1)} all-to-all(bf16[16,72,128]{2,1,0:T(8,128)(2,1)S(1)} %get-tuple-element.22), channel_id=1, replica_groups=mesh['z'=16,'y'=4,'tensor'=8] {'z'}, dimensions={0} | all-to-all | bytes 589824 | tf_op jit(solution)/shard_map/all_to_all | solution.py:119
  67.7 0.8 shard_map.109
  68.5 6.7 %all-to-all-start.3 = ((bf16[16,72,128]{2,1,0:T(8,128)(2,1)}), bf16[16,72,128]{2,1,0:T(8,128)(2,1)S(1)}, u32[]{:S(2)}, u32[]{:S(2)}) async-start(bf16[16,72,128]{2,1,0:T(8,128)(2,1)} %shard_map.109), calls=%async_computation.3 | async-start | bytes 589824 | tf_op jit(solution)/shard_map/all_to_all | solution.py:119
  75.1 0.1 pad_add_fusion.1.where
  75.2 0.0 copy-done
  75.2 0.0 copy-done.3
  75.2 2.7 %shard_map.104 = bf16[4,128,1024]{2,1,0:T(8,128)(2,1)} custom-call(s32[2]{0:T(128)S(1)} %pad_add_fusion.1.where, bf16[128,128]{1,0:T(8,128)(2,1)S(1)} %copy-done.3, bf16[8192,128]{1,0:T(8,128)(2,1)S(1)} %copy-done), custom_call_target="tpu_custom_call" | custom-call | flops 1000000000 | tf_op jit(solution)/shard_map/pallas_call | solution.py:138
  77.9 1.9 %collective-permute-start = (bf16[4,128,1024]{2,1,0:T(8,128)(2,1)}, bf16[4,128,1024]{2,1,0:T(8,128)(2,1)S(1)}, u32[]{:S(2)}, u32[]{:S(2)}) collective-permute-start(bf16[4,128,1024]{2,1,0:T(8,128)(2,1)} %shard_map.104), channel_id=1, source_target_pairs={{0,1},{1,0},{2,3},{3,2},{4,5},{5,4},{6,7},{7,6},{8,9},{9,8},{10,11... | collective-permute-start | bytes 3145736 | tf_op jit(solution)/shard_map/ppermute | solution.py:123
  79.8 14.2 %all-to-all-done.3 = bf16[16,72,128]{2,1,0:T(8,128)(2,1)S(1)} async-done(((bf16[16,72,128]{2,1,0:T(8,128)(2,1)}), bf16[16,72,128]{2,1,0:T(8,128)(2,1)S(1)}, u32[]{:S(2)}, u32[]{:S(2)}) %all-to-all-start.3) | async-done | bytes 294944 | tf_op jit(solution)/shard_map/all_to_all | solution.py:119
  94.1 1.2 broadcast_in_dim.22
  95.2 3.5 %all-to-all-start.4 = ((bf16[4,16,72,128]{3,2,1,0:T(8,128)(2,1)}), bf16[4,16,72,128]{3,2,1,0:T(8,128)(2,1)S(1)}, u32[]{:S(2)}, u32[]{:S(2)}) async-start(bf16[4,16,72,128]{3,2,1,0:T(8,128)(2,1)} %broadcast_in_dim.22), calls=%async_computation.4 | async-start | bytes 2359296 | tf_op jit(solution)/shard_map/all_to_all | solution.py:119
  98.8 0.1 pad_add_fusion.where
  98.9 0.0 copy-start.1
  98.9 1.6 %copy-done.1 = bf16[8192,128]{1,0:T(8,128)(2,1)S(1)} copy-done((bf16[8192,128]{1,0:T(8,128)(2,1)S(1)}, bf16[8192,128]{1,0:T(8,128)(2,1)}, u32[]{:S(2)}) %copy-start.1) | copy-done | bytes 2097176
  100.5 1.5 %shard_map.103.kept = bf16[4,128,1024]{2,1,0:T(8,128)(2,1)S(1)} custom-call(s32[2]{0:T(128)S(1)} %pad_add_fusion.where, bf16[128,128]{1,0:T(8,128)(2,1)S(1)} %copy-done.3, bf16[8192,128]{1,0:T(8,128)(2,1)S(1)} %copy-done.1), custom_call_target="tpu_custom_call" | custom-call | flops 1000000000 | tf_op jit(solution)/shard_map/pallas_call | solution.py:138
  102.0 0.0 copy-start.2
  102.0 0.0 collective-permute-done.came
  102.0 0.2 shard_map.105
  102.3 3.1 %collective-permute-start.1 = (bf16[128,1024]{1,0:T(8,128)(2,1)S(1)}, bf16[128,1024]{1,0:T(8,128)(2,1)S(1)}, u32[]{:S(2)}, u32[]{:S(2)}) collective-permute-start(bf16[128,1024]{1,0:T(8,128)(2,1)S(1)} %get-tuple-element.15), channel_id=1, source_target_pairs={{0,2},{1,3},{2,0},{3,1},{4,6},{5,7},{6,4},{7,5},{8,10},{9,11},{10,... | collective-permute-start | bytes 786440 | tf_op jit(solution)/shard_map/ppermute | solution.py:123
  105.4 4.2 %collective-permute-start.2 = (bf16[128,1024]{1,0:T(8,128)(2,1)S(1)}, bf16[128,1024]{1,0:T(8,128)(2,1)S(1)}, u32[]{:S(2)}, u32[]{:S(2)}) collective-permute-start(bf16[128,1024]{1,0:T(8,128)(2,1)S(1)} %get-tuple-element.16), channel_id=1, source_target_pairs={{0,4},{1,5},{2,6},{3,7},{4,0},{5,1},{6,2},{7,3},{8,12},{9,13},{10,... | collective-permute-start | bytes 786440 | tf_op jit(solution)/shard_map/ppermute | solution.py:123
  109.6 3.2 %collective-permute-start.3 = (bf16[128,1024]{1,0:T(8,128)(2,1)S(1)}, bf16[128,1024]{1,0:T(8,128)(2,1)S(1)}, u32[]{:S(2)}, u32[]{:S(2)}) collective-permute-start(bf16[128,1024]{1,0:T(8,128)(2,1)S(1)} %get-tuple-element.17), channel_id=1, source_target_pairs={{0,6},{1,7},{2,4},{3,5},{4,2},{5,3},{6,0},{7,1},{8,14},{9,15},{10,... | collective-permute-start | bytes 786440 | tf_op jit(solution)/shard_map/ppermute | solution.py:123
  112.8 0.6 collective-permute-done.1.f1
  113.5 5.3 %collective-permute-done.2.f2 = bf16[128,1024]{1,0:T(8,128)(2,1)S(1)} collective-permute-done((bf16[128,1024]{1,0:T(8,128)(2,1)S(1)}, bf16[128,1024]{1,0:T(8,128)(2,1)S(1)}, u32[]{:S(2)}, u32[]{:S(2)}) %collective-permute-start.2) | collective-permute-done | bytes 262176 | tf_op jit(solution)/shard_map/ppermute | solution.py:123
  118.8 5.1 %collective-permute-done.3.f3 = bf16[128,1024]{1,0:T(8,128)(2,1)S(1)} collective-permute-done((bf16[128,1024]{1,0:T(8,128)(2,1)S(1)}, bf16[128,1024]{1,0:T(8,128)(2,1)S(1)}, u32[]{:S(2)}, u32[]{:S(2)}) %collective-permute-start.3) | collective-permute-done | bytes 262176 | tf_op jit(solution)/shard_map/ppermute | solution.py:123
  123.8 0.0 copy-done.2
  123.8 1.1 shard_map.108
  124.9 0.0 all-to-all-done.4.parts
  124.9 1.3 %shard_map.110 = (bf16[512,1024]{1,0:T(8,128)(2,1)}, bf16[512,128]{1,0:T(8,128)(2,1)}) custom-call(bf16[4,16,72,128]{3,2,1,0:T(8,128)(2,1)S(1)} %all-to-all-done.4.parts), custom_call_target="tpu_custom_call" | custom-call | tf_op jit(solution)/shard_map/pallas_call | solution.py:192
Async XLA Ops:
  16.1 16.9 %all-to-all-start = ((f32[32,32,128]{2,1,0:T(8,128)}), f32[32,32,128]{2,1,0:T(8,128)S(1)}, u32[]{:S(2)}, u32[]{:S(2)}) async-start(f32[32,32,128]{2,1,0:T(8,128)} %get-tuple-element.18), calls=%async_computation | async-start | bytes 1048576 | tf_op jit(solution)/shard_map/all_to_all | solution.py:119
  33.0 42.2 %copy-start = (bf16[8192,128]{1,0:T(8,128)(2,1)S(1)}, bf16[8192,128]{1,0:T(8,128)(2,1)}, u32[]{:S(2)}) copy-start(bf16[8192,128]{1,0:T(8,128)(2,1)} %w.3) | copy-start | bytes 6291460
  33.4 41.8 %copy-start.3 = (bf16[128,128]{1,0:T(8,128)(2,1)S(1)}, bf16[128,128]{1,0:T(8,128)(2,1)}, u32[]{:S(2)}) copy-start(bf16[128,128]{1,0:T(8,128)(2,1)} %c.5) | copy-start | bytes 98308
  68.5 25.6 %all-to-all-start.3 = ((bf16[16,72,128]{2,1,0:T(8,128)(2,1)}), bf16[16,72,128]{2,1,0:T(8,128)(2,1)S(1)}, u32[]{:S(2)}, u32[]{:S(2)}) async-start(bf16[16,72,128]{2,1,0:T(8,128)(2,1)} %shard_map.109), calls=%async_computation.3 | async-start | bytes 589824 | tf_op jit(solution)/shard_map/all_to_all | solution.py:119
  77.9 24.1 %collective-permute-start = (bf16[4,128,1024]{2,1,0:T(8,128)(2,1)}, bf16[4,128,1024]{2,1,0:T(8,128)(2,1)S(1)}, u32[]{:S(2)}, u32[]{:S(2)}) collective-permute-start(bf16[4,128,1024]{2,1,0:T(8,128)(2,1)} %shard_map.104), channel_id=1, source_target_pairs={{0,1},{1,0},{2,3},{3,2},{4,5},{5,4},{6,7},{7,6},{8,9},{9,8},{10,11... | collective-permute-start | bytes 3145736 | tf_op jit(solution)/shard_map/ppermute | solution.py:123
  95.2 29.7 %all-to-all-start.4 = ((bf16[4,16,72,128]{3,2,1,0:T(8,128)(2,1)}), bf16[4,16,72,128]{3,2,1,0:T(8,128)(2,1)S(1)}, u32[]{:S(2)}, u32[]{:S(2)}) async-start(bf16[4,16,72,128]{3,2,1,0:T(8,128)(2,1)} %broadcast_in_dim.22), calls=%async_computation.4 | async-start | bytes 2359296 | tf_op jit(solution)/shard_map/all_to_all | solution.py:119
  98.9 1.6 %copy-start.1 = (bf16[8192,128]{1,0:T(8,128)(2,1)S(1)}, bf16[8192,128]{1,0:T(8,128)(2,1)}, u32[]{:S(2)}) copy-start(bf16[8192,128]{1,0:T(8,128)(2,1)} %w.3) | copy-start | bytes 6291460
  102.0 21.8 %copy-start.2 = (bf16[32,1024,16]{1,2,0:T(8,128)(2,1)S(1)}, bf16[32,1024,16]{1,2,0:T(8,128)(2,1)}, u32[]{:S(2)}) copy-start(bf16[32,1024,16]{1,2,0:T(8,128)(2,1)} %param.11) | copy-start | bytes 3145732
  102.3 11.2 %collective-permute-start.1 = (bf16[128,1024]{1,0:T(8,128)(2,1)S(1)}, bf16[128,1024]{1,0:T(8,128)(2,1)S(1)}, u32[]{:S(2)}, u32[]{:S(2)}) collective-permute-start(bf16[128,1024]{1,0:T(8,128)(2,1)S(1)} %get-tuple-element.15), channel_id=1, source_target_pairs={{0,2},{1,3},{2,0},{3,1},{4,6},{5,7},{6,4},{7,5},{8,10},{9,11},{10,... | collective-permute-start | bytes 786440 | tf_op jit(solution)/shard_map/ppermute | solution.py:123
  105.4 13.4 %collective-permute-start.2 = (bf16[128,1024]{1,0:T(8,128)(2,1)S(1)}, bf16[128,1024]{1,0:T(8,128)(2,1)S(1)}, u32[]{:S(2)}, u32[]{:S(2)}) collective-permute-start(bf16[128,1024]{1,0:T(8,128)(2,1)S(1)} %get-tuple-element.16), channel_id=1, source_target_pairs={{0,4},{1,5},{2,6},{3,7},{4,0},{5,1},{6,2},{7,3},{8,12},{9,13},{10,... | collective-permute-start | bytes 786440 | tf_op jit(solution)/shard_map/ppermute | solution.py:123
  109.6 14.2 %collective-permute-start.3 = (bf16[128,1024]{1,0:T(8,128)(2,1)S(1)}, bf16[128,1024]{1,0:T(8,128)(2,1)S(1)}, u32[]{:S(2)}, u32[]{:S(2)}) collective-permute-start(bf16[128,1024]{1,0:T(8,128)(2,1)S(1)} %get-tuple-element.17), channel_id=1, source_target_pairs={{0,6},{1,7},{2,4},{3,5},{4,2},{5,3},{6,0},{7,1},{8,14},{9,15},{10,... | collective-permute-start | bytes 786440 | tf_op jit(solution)/shard_map/ppermute | solution.py:123

commit v8 on v6

--- a/solution.py
+++ b/solution.py
@@ -32,7 +32,7 @@
     return jnp.where(at == slot, jnp.concatenate([low] * slots, axis=0), 0.0)
 
 
-def partial_kernel(x, c, down, up, doc, tenant, index, me, part, slot_out, *packs):
+def token_kernel(x, c, doc, tenant, index, me, slot_out, *packs):
     n = x.shape[0]
     tenant_of = (lax.broadcasted_iota(jnp.int32, (SLOTS, tenant.shape[1]), 0) == tenant[...]).astype(bf16)
     table = jnp.broadcast_to(index[...].astype(f32), (8, SLOTS)).astype(bf16)
@@ -40,14 +40,6 @@
     doc_of = (lax.broadcasted_iota(jnp.int32, (tenant.shape[1], n), 0) == doc[...]).astype(bf16)
     slot = jnp.dot(slot_of_doc, doc_of, preferred_element_type=f32)
     slot_out[...] = slot
-    member = lax.broadcasted_iota(jnp.int32, (ROWS, n), 0) // RANK == slot[:1].astype(jnp.int32)
-    h_all = lax.dot_general(down[...], x[...], NT, preferred_element_type=f32)
-    g_all = lax.dot_general(up[...], c[...], NT, preferred_element_type=f32)
-    g = jnp.sum(jnp.where(member, g_all, 0.0).reshape(SLOTS, RANK, n), axis=0)
-    h = jnp.sum(jnp.where(member, h_all, 0.0).reshape(SLOTS, RANK, n), axis=0)
-    both = jnp.concatenate([g, h], axis=0)
-    for i in range(Y * T):
-        part[i] = both
     fx = x.shape[1] // Y
     slots = jnp.concatenate([slot, jnp.zeros((8, fx + c.shape[1] - n), f32)], axis=1)
     for k, pack in enumerate(packs):
@@ -56,14 +48,34 @@
         pack[...] = jnp.concatenate([mine.astype(f32), slots], axis=0).astype(bf16)
 
 
+def partial_kernel(x_in, c_in, down_in, up_in, slot, part, x, c, down, up, sems):
+    loads = [
+        pltpu.make_async_copy(source, target, sems.at[i])
+        for i, (source, target) in enumerate(((down_in, down), (x_in, x), (up_in, up), (c_in, c)))
+    ]
+    for load in loads:
+        load.start()
+    for load in loads:
+        load.wait()
+    n = x.shape[0]
+    member = lax.broadcasted_iota(jnp.int32, (ROWS, n), 0) // RANK == slot[:1].astype(jnp.int32)
+    h_all = lax.dot_general(down[...], x[...], NT, preferred_element_type=f32)
+    g_all = lax.dot_general(up[...], c[...], NT, preferred_element_type=f32)
+    g = jnp.sum(jnp.where(member, g_all, 0.0).reshape(SLOTS, RANK, n), axis=0)
+    h = jnp.sum(jnp.where(member, h_all, 0.0).reshape(SLOTS, RANK, n), axis=0)
+    both = jnp.concatenate([g, h], axis=0).astype(bf16)
+    for i in range(Y * T):
+        part[i] = both
+
+
 def gradient_kernel(me, parts, p0, p1, p2, p3, out, low_out):
     fx = p0.shape[1] - 128
     gs, hs = [], []
     for k, pack in enumerate((p0, p1, p2, p3)):
         at = me[0] ^ k
-        both = parts[at * T]
+        both = parts[at * T].astype(f32)
         for j in range(1, T):
-            both = both + parts[at * T + j]
+            both = both + parts[at * T + j].astype(f32)
         both = both.astype(bf16)
         if k == 0:
             low_out[...] = both
@@ -160,13 +172,27 @@
     down_rows = jnp.transpose(down, (0, 2, 1)).reshape(ROWS, fx)
     up_rows = up.reshape(ROWS, fc)
     block = (ROWS // Z * 2 + ROWS // Y // Z, 128)
-    part, slot, *packs = call(
+    slot, *packs = call(
+        token_kernel,
+        [((8, n), f32)] + [((n + 8, fx // Y + fc), bf16)] * Y,
+        flops=10**8,
+        grant=pltpu.CompilerParams(),
+        out=jax.ShapeDtypeStruct,
+        in_specs=[pl.BlockSpec(memory_space=pltpu.VMEM)] * 5 + [pl.BlockSpec(memory_space=pltpu.SMEM)],
+    )(x, c, doc[None], tenant[None], index[None], me)
+    (part,) = call(
         partial_kernel,
-        [((Y * T, 2 * RANK, n), f32), ((8, n), f32)] + [((n + 8, fx // Y + fc), bf16)] * Y,
+        [((Y * T, 2 * RANK, n), bf16)],
         flops=10**9,
-        grant=pltpu.CompilerParams(),
-        in_specs=[pl.BlockSpec(memory_space=pltpu.VMEM)] * 7 + [pl.BlockSpec(memory_space=pltpu.SMEM)],
-    )(x, c, down_rows, up_rows, doc[None], tenant[None], index[None], me)
+        in_specs=[pl.BlockSpec(memory_space=pltpu.HBM)] * 4 + [pl.BlockSpec(memory_space=pltpu.VMEM)],
+        scratch_shapes=[
+            pltpu.VMEM((n, fx), bf16),
+            pltpu.VMEM((n, fc), bf16),
+            pltpu.VMEM((ROWS, fx), bf16),
+            pltpu.VMEM((ROWS, fc), bf16),
+            pltpu.SemaphoreType.DMA((4,)),
+        ],
+    )(*(pltpu.with_memory_space_constraint(v, pltpu.HBM) for v in (x, c, down_rows, up_rows)), slot)
     parts = swap(part, ("y", "tensor"))
     for k in (1, 2, 3):
         packs[k] = trade(packs[k], "y", k)

time: 123 us -> 124 us (level)
  Pallas kernels: 8.96 us -> 10.7 us
  waiting for transfers between devices: 20.9 us -> 19.2 us
    pallas_call x1 -> x2, Pallas kernels: 2.86 us -> 4.56 us  [the longest x1 2.57 us: per_device(): call(partial_kernel, [((Y * T, 2 * RANK, n), bf16)], flops=10 ** 9, in_sp...]
    ppermute x7, waiting for transfers between devices: 20.9 us -> 19.2 us  [trade(): lax.ppermute(value, axis, [(i, i ^ k) for i in range(lax.axis_size(axis))])]
  transfers between devices with their start and end apart: 9 -> 9, of which waited for: 6 -> 5; matrix products, arithmetic and copies ran while one was open for 0% -> 0% of each run, Pallas kernels for 4% -> 4%
where the time goes in v8:
time: 124 us; the launch traced here: 123 us
  blocking collectives  50.7 us (41%)
  starting transfers between devices  39.8 us (32%)
  waiting for transfers between devices  19.2 us (15%)
  Pallas kernels  10.7 us (9%)
  local copies, waits for them, and re-layouts  1.89 us (2%)
    all_to_all x2, blocking collectives, swap(): return lax.all_to_all(value, axis, 0, 0, tiled=True)  50.7 us
    ppermute x7, starting transfers between devices, trade(): lax.ppermute(value, axis, [(i, i ^ k) for i in range(lax.axis_size(axis))])  24.8 us
    ppermute x7, waiting for transfers between devices, trade(): lax.ppermute(value, axis, [(i, i ^ k) for i in range(lax.axis_size(axis))])  19.2 us
    all_to_all x2, starting transfers between devices, swap(): return lax.all_to_all(value, axis, 0, 0, tiled=True)  15.1 us
    pallas_call x2, Pallas kernels, frozen_blocks(): pl.pallas_call(frozen_kernel, compiler_params=GRANT, grid_spec=pltpu.Pref...  3.07 us
    pallas_call x1, Pallas kernels, per_device(): call(partial_kernel, [((Y * T, 2 * RANK, n), bf16)], flops=10 ** 9, in_sp...  2.57 us
  transfers between devices with their start and end apart: 9, of which 5 were waited for; matrix products, arithmetic and copies ran while one was open for 0% of the time, Pallas kernels for 4%

profile of v8, /device:TPU:1, one launch (start us, length us, event | category | flops | bytes accessed | tf_op | source)
XLA Modules:
  0.0 123.3 jit_solution(1194385755863361952)
XLA Ops:
  0.6 2.0 %shard_map.106 = (f32[8,128]{1,0:T(8,128)}, bf16[136,384]{1,0:T(8,128)(2,1)}, bf16[136,384]{1,0:T(8,128)(2,1)}, bf16[136,384]{1,0:T(8,128)(2,1)}, bf16[136,384]{1,0:T(8,128)(2,1)}) custom-call(bf16[128,1024]{1,0:T(8,128)(2,1)} %x_in.1, bf16[128,128]{1,0:T(8,128)(2,1)} %c_in.1, s32[1,128]{1,0:T(1,128)} %bitcast.20, s32[1,128]{1,0:T(1,128)} %bitcast.21, ...), custom_call_target="tpu_custom_call" | custom-call | flops 100000000 | tf_op jit(solution)/shard_map/pallas_call | solution.py:175
  2.6 0.0 copy-start.4
  2.6 0.7 copy-done.4
  3.3 0.0 copy-start.8
  3.3 0.0 copy-start.7
  3.3 0.0 copy-start.6
  3.3 0.0 copy-start.3
  3.3 2.6 %shard_map.107 = bf16[32,32,128]{2,1,0:T(8,128)(2,1)} custom-call(bf16[128,1024]{1,0:T(8,128)(2,1)} %x_in.1, bf16[128,128]{1,0:T(8,128)(2,1)} %c_in.1, bf16[512,1024]{1,0:T(8,128)(2,1)} %bitcast.15, bf16[512,128]{1,0:T(8,128)(2,1)} %bitcast.18, f32[8,128]{1,0:T(8,128)S(1)} %copy-done.4), custom_call_target="tpu_custom_call" | custom-call | flops 1000000000 | tf_op jit(solution)/shard_map/pallas_call | solution.py:183
  5.9 10.4 %all-to-all-start = ((bf16[32,32,128]{2,1,0:T(8,128)(2,1)}), bf16[32,32,128]{2,1,0:T(8,128)(2,1)S(1)}, u32[]{:S(2)}, u32[]{:S(2)}) async-start(bf16[32,32,128]{2,1,0:T(8,128)(2,1)} %shard_map.107), calls=%async_computation | async-start | bytes 524288 | tf_op jit(solution)/shard_map/all_to_all | solution.py:131
  16.3 0.0 copy-done.8
  16.3 3.3 %collective-permute-start.4 = (bf16[136,384]{1,0:T(8,128)(2,1)S(1)}, bf16[136,384]{1,0:T(8,128)(2,1)S(1)}, u32[]{:S(2)}, u32[]{:S(2)}) collective-permute-start(bf16[136,384]{1,0:T(8,128)(2,1)S(1)} %copy-done.8), channel_id=1, source_target_pairs={{0,8},{8,0},{16,24},{24,16},{1,9},{9,1},{17,25},{25,17},{2,10},{10... | collective-permute-start | bytes 313352 | tf_op jit(solution)/shard_map/ppermute | solution.py:135
  19.6 0.0 copy-done.7
  19.6 4.4 %collective-permute-start.5 = (bf16[136,384]{1,0:T(8,128)(2,1)S(1)}, bf16[136,384]{1,0:T(8,128)(2,1)S(1)}, u32[]{:S(2)}, u32[]{:S(2)}) collective-permute-start(bf16[136,384]{1,0:T(8,128)(2,1)S(1)} %copy-done.7), channel_id=1, source_target_pairs={{0,16},{8,24},{16,0},{24,8},{1,17},{9,25},{17,1},{25,9},{2,18},{10... | collective-permute-start | bytes 313352 | tf_op jit(solution)/shard_map/ppermute | solution.py:135
  24.0 0.0 copy-done.6
  24.0 1.9 %collective-permute-start.6 = (bf16[136,384]{1,0:T(8,128)(2,1)S(1)}, bf16[136,384]{1,0:T(8,128)(2,1)S(1)}, u32[]{:S(2)}, u32[]{:S(2)}) collective-permute-start(bf16[136,384]{1,0:T(8,128)(2,1)S(1)} %copy-done.6), channel_id=1, source_target_pairs={{0,24},{8,16},{16,8},{24,0},{1,25},{9,17},{17,9},{25,1},{2,26},{10... | collective-permute-start | bytes 313352 | tf_op jit(solution)/shard_map/ppermute | solution.py:135
  26.0 0.0 collective-permute-done.4.p1
  26.0 2.9 %collective-permute-done.5.p2 = bf16[136,384]{1,0:T(8,128)(2,1)S(1)} collective-permute-done((bf16[136,384]{1,0:T(8,128)(2,1)S(1)}, bf16[136,384]{1,0:T(8,128)(2,1)S(1)}, u32[]{:S(2)}, u32[]{:S(2)}) %collective-permute-start.5) | collective-permute-done | bytes 104480 | tf_op jit(solution)/shard_map/ppermute | solution.py:135
  28.8 1.8 %collective-permute-done.6.p3 = bf16[136,384]{1,0:T(8,128)(2,1)S(1)} collective-permute-done((bf16[136,384]{1,0:T(8,128)(2,1)S(1)}, bf16[136,384]{1,0:T(8,128)(2,1)S(1)}, u32[]{:S(2)}, u32[]{:S(2)}) %collective-permute-start.6) | collective-permute-done | bytes 104480 | tf_op jit(solution)/shard_map/ppermute | solution.py:135
  30.7 0.0 all-to-all-done.parts
  30.7 0.0 copy-done.3
  30.7 0.4 shard_map.108
  31.0 25.9 %all_to_all.20.parts = bf16[16,72,128]{2,1,0:T(8,128)(2,1)S(1)} all-to-all(bf16[16,72,128]{2,1,0:T(8,128)(2,1)S(1)} %get-tuple-element.26), channel_id=1, replica_groups=mesh['zh'=8,'zl'=2,'y'=4,'tensor'=8] {'zh','zl'}, dimensions={0} | all-to-all | bytes 589824 | tf_op jit(solution)/shard_map/all_to_all | solution.py:131
  56.9 0.1 shard_map.110
  57.0 24.8 %all_to_all.21 = bf16[8,72,128]{2,1,0:T(8,128)(2,1)S(1)} all-to-all(bf16[8,72,128]{2,1,0:T(8,128)(2,1)S(1)} %shard_map.110), channel_id=1, replica_groups=mesh['zh'=8,'zl'=2,'y'=4,'tensor'=8] {'zh'}, dimensions={0} | all-to-all | bytes 294912 | tf_op jit(solution)/shard_map/all_to_all | solution.py:131
  81.8 1.2 broadcast_in_dim.22
  83.0 0.0 copy-start
  83.0 0.0 copy-start.2
  83.0 4.7 %all-to-all-start.3 = ((bf16[8,8,72,128]{3,2,1,0:T(8,128)(2,1)}), bf16[8,8,72,128]{3,2,1,0:T(8,128)(2,1)S(1)}, u32[]{:S(2)}, u32[]{:S(2)}) async-start(bf16[8,8,72,128]{3,2,1,0:T(8,128)(2,1)} %broadcast_in_dim.22), calls=%async_computation.3 | async-start | bytes 2359296 | tf_op jit(solution)/shard_map/all_to_all | solution.py:131
  87.7 0.1 pad_add_fusion.1.where
  87.7 0.0 copy-done
  87.7 0.0 copy-done.2
  87.7 1.5 %shard_map.104 = bf16[4,128,1024]{2,1,0:T(8,128)(2,1)S(1)} custom-call(s32[2]{0:T(128)S(1)} %pad_add_fusion.1.where, bf16[128,128]{1,0:T(8,128)(2,1)S(1)} %copy-done.2, bf16[8192,128]{1,0:T(8,128)(2,1)S(1)} %copy-done), custom_call_target="tpu_custom_call" | custom-call | flops 1000000000 | tf_op jit(solution)/shard_map/pallas_call | solution.py:150
  89.3 5.5 %collective-permute-start = (bf16[4,128,1024]{2,1,0:T(8,128)(2,1)S(1)}, bf16[4,128,1024]{2,1,0:T(8,128)(2,1)S(1)}, u32[]{:S(2)}, u32[]{:S(2)}) collective-permute-start(bf16[4,128,1024]{2,1,0:T(8,128)(2,1)S(1)} %shard_map.104), channel_id=1, source_target_pairs={{0,1},{1,0},{2,3},{3,2},{4,5},{5,4},{6,7},{7,6},{8,9},{9,8},{10,11... | collective-permute-start | bytes 3145736 | tf_op jit(solution)/shard_map/ppermute | solution.py:135
  94.8 0.1 pad_add_fusion.where
  94.9 1.5 %shard_map.103.kept = bf16[4,128,1024]{2,1,0:T(8,128)(2,1)S(1)} custom-call(s32[2]{0:T(128)S(1)} %pad_add_fusion.where, bf16[128,128]{1,0:T(8,128)(2,1)S(1)} %copy-done.2, bf16[8192,128]{1,0:T(8,128)(2,1)S(1)} %copy-done), custom_call_target="tpu_custom_call" | custom-call | flops 1000000000 | tf_op jit(solution)/shard_map/pallas_call | solution.py:150
  96.4 0.0 copy-start.1
  96.5 0.0 copy-start.5
  96.5 0.6 collective-permute-done.came
  97.1 0.2 shard_map.105
  97.3 3.1 %collective-permute-start.1 = (bf16[128,1024]{1,0:T(8,128)(2,1)S(1)}, bf16[128,1024]{1,0:T(8,128)(2,1)S(1)}, u32[]{:S(2)}, u32[]{:S(2)}) collective-permute-start(bf16[128,1024]{1,0:T(8,128)(2,1)S(1)} %get-tuple-element.17), channel_id=1, source_target_pairs={{0,2},{1,3},{2,0},{3,1},{4,6},{5,7},{6,4},{7,5},{8,10},{9,11},{10,... | collective-permute-start | bytes 786440 | tf_op jit(solution)/shard_map/ppermute | solution.py:135
  100.5 4.3 %collective-permute-start.2 = (bf16[128,1024]{1,0:T(8,128)(2,1)S(1)}, bf16[128,1024]{1,0:T(8,128)(2,1)S(1)}, u32[]{:S(2)}, u32[]{:S(2)}) collective-permute-start(bf16[128,1024]{1,0:T(8,128)(2,1)S(1)} %get-tuple-element.18), channel_id=1, source_target_pairs={{0,4},{1,5},{2,6},{3,7},{4,0},{5,1},{6,2},{7,3},{8,12},{9,13},{10,... | collective-permute-start | bytes 786440 | tf_op jit(solution)/shard_map/ppermute | solution.py:135
  104.8 2.1 %collective-permute-start.3 = (bf16[128,1024]{1,0:T(8,128)(2,1)S(1)}, bf16[128,1024]{1,0:T(8,128)(2,1)S(1)}, u32[]{:S(2)}, u32[]{:S(2)}) collective-permute-start(bf16[128,1024]{1,0:T(8,128)(2,1)S(1)} %get-tuple-element.19), channel_id=1, source_target_pairs={{0,6},{1,7},{2,4},{3,5},{4,2},{5,3},{6,0},{7,1},{8,14},{9,15},{10,... | collective-permute-start | bytes 786440 | tf_op jit(solution)/shard_map/ppermute | solution.py:135
  106.9 0.0 collective-permute-done.1.f1
  107.0 7.6 %collective-permute-done.2.f2 = bf16[128,1024]{1,0:T(8,128)(2,1)S(1)} collective-permute-done((bf16[128,1024]{1,0:T(8,128)(2,1)S(1)}, bf16[128,1024]{1,0:T(8,128)(2,1)S(1)}, u32[]{:S(2)}, u32[]{:S(2)}) %collective-permute-start.2) | collective-permute-done | bytes 262176 | tf_op jit(solution)/shard_map/ppermute | solution.py:135
  114.6 6.3 %collective-permute-done.3.f3 = bf16[128,1024]{1,0:T(8,128)(2,1)S(1)} collective-permute-done((bf16[128,1024]{1,0:T(8,128)(2,1)S(1)}, bf16[128,1024]{1,0:T(8,128)(2,1)S(1)}, u32[]{:S(2)}, u32[]{:S(2)}) %collective-permute-start.3) | collective-permute-done | bytes 262176 | tf_op jit(solution)/shard_map/ppermute | solution.py:135
  120.9 0.0 copy-done.1
  120.9 0.0 copy-done.5
  120.9 1.1 shard_map.109
  122.0 0.0 all-to-all-done.3.parts
  122.0 1.3 %shard_map.111 = (bf16[8,2,32,1024]{3,2,1,0:T(8,128)(2,1)}, bf16[4,8,2,8,128]{4,3,2,1,0:T(8,128)(2,1)}) custom-call(bf16[8,8,72,128]{3,2,1,0:T(8,128)(2,1)S(1)} %all-to-all-done.3.parts), custom_call_target="tpu_custom_call" | custom-call | tf_op jit(solution)/shard_map/pallas_call | solution.py:217
Async XLA Ops:
  2.6 0.7 copy-start.4
  3.3 13.0 %copy-start.8 = (bf16[136,384]{1,0:T(8,128)(2,1)S(1)}, bf16[136,384]{1,0:T(8,128)(2,1)}, u32[]{:S(2)}) copy-start(bf16[136,384]{1,0:T(8,128)(2,1)} %get-tuple-element.22) | copy-start | bytes 313348
  3.3 16.3 %copy-start.7 = (bf16[136,384]{1,0:T(8,128)(2,1)S(1)}, bf16[136,384]{1,0:T(8,128)(2,1)}, u32[]{:S(2)}) copy-start(bf16[136,384]{1,0:T(8,128)(2,1)} %get-tuple-element.23) | copy-start | bytes 313348
  3.3 20.7 %copy-start.6 = (bf16[136,384]{1,0:T(8,128)(2,1)S(1)}, bf16[136,384]{1,0:T(8,128)(2,1)}, u32[]{:S(2)}) copy-start(bf16[136,384]{1,0:T(8,128)(2,1)} %get-tuple-element.24) | copy-start | bytes 313348
  3.3 27.4 %copy-start.3 = (bf16[136,384]{1,0:T(8,128)(2,1)S(1)}, bf16[136,384]{1,0:T(8,128)(2,1)}, u32[]{:S(2)}) copy-start(bf16[136,384]{1,0:T(8,128)(2,1)} %get-tuple-element.21.p0) | copy-start | bytes 313348
  5.9 24.8 %all-to-all-start = ((bf16[32,32,128]{2,1,0:T(8,128)(2,1)}), bf16[32,32,128]{2,1,0:T(8,128)(2,1)S(1)}, u32[]{:S(2)}, u32[]{:S(2)}) async-start(bf16[32,32,128]{2,1,0:T(8,128)(2,1)} %shard_map.107), calls=%async_computation | async-start | bytes 524288 | tf_op jit(solution)/shard_map/all_to_all | solution.py:131
  16.3 9.7 %collective-permute-start.4 = (bf16[136,384]{1,0:T(8,128)(2,1)S(1)}, bf16[136,384]{1,0:T(8,128)(2,1)S(1)}, u32[]{:S(2)}, u32[]{:S(2)}) collective-permute-start(bf16[136,384]{1,0:T(8,128)(2,1)S(1)} %copy-done.8), channel_id=1, source_target_pairs={{0,8},{8,0},{16,24},{24,16},{1,9},{9,1},{17,25},{25,17},{2,10},{10... | collective-permute-start | bytes 313352 | tf_op jit(solution)/shard_map/ppermute | solution.py:135
  19.6 9.2 %collective-permute-start.5 = (bf16[136,384]{1,0:T(8,128)(2,1)S(1)}, bf16[136,384]{1,0:T(8,128)(2,1)S(1)}, u32[]{:S(2)}, u32[]{:S(2)}) collective-permute-start(bf16[136,384]{1,0:T(8,128)(2,1)S(1)} %copy-done.7), channel_id=1, source_target_pairs={{0,16},{8,24},{16,0},{24,8},{1,17},{9,25},{17,1},{25,9},{2,18},{10... | collective-permute-start | bytes 313352 | tf_op jit(solution)/shard_map/ppermute | solution.py:135
  24.0 6.6 %collective-permute-start.6 = (bf16[136,384]{1,0:T(8,128)(2,1)S(1)}, bf16[136,384]{1,0:T(8,128)(2,1)S(1)}, u32[]{:S(2)}, u32[]{:S(2)}) collective-permute-start(bf16[136,384]{1,0:T(8,128)(2,1)S(1)} %copy-done.6), channel_id=1, source_target_pairs={{0,24},{8,16},{16,8},{24,0},{1,25},{9,17},{17,9},{25,1},{2,26},{10... | collective-permute-start | bytes 313352 | tf_op jit(solution)/shard_map/ppermute | solution.py:135
  83.0 4.8 %copy-start = (bf16[8192,128]{1,0:T(8,128)(2,1)S(1)}, bf16[8192,128]{1,0:T(8,128)(2,1)}, u32[]{:S(2)}) copy-start(bf16[8192,128]{1,0:T(8,128)(2,1)} %w.3) | copy-start | bytes 6291460
  83.0 4.8 %copy-start.2 = (bf16[128,128]{1,0:T(8,128)(2,1)S(1)}, bf16[128,128]{1,0:T(8,128)(2,1)}, u32[]{:S(2)}) copy-start(bf16[128,128]{1,0:T(8,128)(2,1)} %c_in.1) | copy-start | bytes 98308
  83.0 39.0 %all-to-all-start.3 = ((bf16[8,8,72,128]{3,2,1,0:T(8,128)(2,1)}), bf16[8,8,72,128]{3,2,1,0:T(8,128)(2,1)S(1)}, u32[]{:S(2)}, u32[]{:S(2)}) async-start(bf16[8,8,72,128]{3,2,1,0:T(8,128)(2,1)} %broadcast_in_dim.22), calls=%async_computation.3 | async-start | bytes 2359296 | tf_op jit(solution)/shard_map/all_to_all | solution.py:131
  89.3 7.8 %collective-permute-start = (bf16[4,128,1024]{2,1,0:T(8,128)(2,1)S(1)}, bf16[4,128,1024]{2,1,0:T(8,128)(2,1)S(1)}, u32[]{:S(2)}, u32[]{:S(2)}) collective-permute-start(bf16[4,128,1024]{2,1,0:T(8,128)(2,1)S(1)} %shard_map.104), channel_id=1, source_target_pairs={{0,1},{1,0},{2,3},{3,2},{4,5},{5,4},{6,7},{7,6},{8,9},{9,8},{10,11... | collective-permute-start | bytes 3145736 | tf_op jit(solution)/shard_map/ppermute | solution.py:135
  96.4 24.4 %copy-start.1 = (bf16[32,1024,16]{1,2,0:T(8,128)(2,1)S(1)}, bf16[32,1024,16]{1,2,0:T(8,128)(2,1)}, u32[]{:S(2)}) copy-start(bf16[32,1024,16]{1,2,0:T(8,128)(2,1)} %param.11) | copy-start | bytes 3145732
  96.5 24.4 %copy-start.5 = (f32[8,128]{1,0:T(8,128)S(1)}, f32[8,128]{1,0:T(8,128)}, u32[]{:S(2)}) copy-start(f32[8,128]{1,0:T(8,128)} %get-tuple-element.20.slot) | copy-start | bytes 12292
  97.3 9.6 %collective-permute-start.1 = (bf16[128,1024]{1,0:T(8,128)(2,1)S(1)}, bf16[128,1024]{1,0:T(8,128)(2,1)S(1)}, u32[]{:S(2)}, u32[]{:S(2)}) collective-permute-start(bf16[128,1024]{1,0:T(8,128)(2,1)S(1)} %get-tuple-element.17), channel_id=1, source_target_pairs={{0,2},{1,3},{2,0},{3,1},{4,6},{5,7},{6,4},{7,5},{8,10},{9,11},{10,... | collective-permute-start | bytes 786440 | tf_op jit(solution)/shard_map/ppermute | solution.py:135
  100.5 14.1 %collective-permute-start.2 = (bf16[128,1024]{1,0:T(8,128)(2,1)S(1)}, bf16[128,1024]{1,0:T(8,128)(2,1)S(1)}, u32[]{:S(2)}, u32[]{:S(2)}) collective-permute-start(bf16[128,1024]{1,0:T(8,128)(2,1)S(1)} %get-tuple-element.18), channel_id=1, source_target_pairs={{0,4},{1,5},{2,6},{3,7},{4,0},{5,1},{6,2},{7,3},{8,12},{9,13},{10,... | collective-permute-start | bytes 786440 | tf_op jit(solution)/shard_map/ppermute | solution.py:135
  104.8 16.1 %collective-permute-start.3 = (bf16[128,1024]{1,0:T(8,128)(2,1)S(1)}, bf16[128,1024]{1,0:T(8,128)(2,1)S(1)}, u32[]{:S(2)}, u32[]{:S(2)}) collective-permute-start(bf16[128,1024]{1,0:T(8,128)(2,1)S(1)} %get-tuple-element.19), channel_id=1, source_target_pairs={{0,6},{1,7},{2,4},{3,5},{4,2},{5,3},{6,0},{7,1},{8,14},{9,15},{10,... | collective-permute-start | bytes 786440 | tf_op jit(solution)/shard_map/ppermute | solution.py:135
